TPU v7x, 128 devices: a whole 4x4x4 slice. The times are simulated.
128 devices in a mesh: grp: 2 (over core), ta: 4 (over y), ha: 2 (over z_lo), wa: 8 (over x, z_hi).
Axes of the slice: x: 4, y: 4, z: 4 (z_hi: 2, z_lo: 2; z = z_hi * 2 + z_lo), core: 2. Of those that a mesh axis runs over, the one named last changes fastest.
Arguments:
- query_tiles: bfloat16 [4, 2, 8, 256, 3072], P('ta', 'ha', 'wa', None, 'grp'), may hold values from -11 to 11
- key_tiles: bfloat16 [4, 2, 8, 256, 3072], P('ta', 'ha', 'wa', None, 'grp'), may hold values from -11 to 11
- value_tiles: bfloat16 [4, 2, 8, 256, 3072], P('ta', 'ha', 'wa', None, 'grp'), may hold values from -6 to 6
- out_weight: bfloat16 [3072, 3072], P('grp'), may hold values from -0.15625 to 0.15625
- gate: bfloat16 [3072], P('grp'), may hold values from 8 to 64
Outputs:
- branch: bfloat16 [4, 2, 8, 256, 3072], P('ta', 'ha', 'wa', None, 'grp')
All inputs are finite; a program needn't handle non-finite values.
Results may differ from a plain program's by a relative error of at most 0.0057.
Values may be sent and summed in bfloat16 or wider, within the bound.
No kernel may reach another device: no remote copies, remote signals or barrier semaphores. Data moves between devices by JAX's collectives and lax.ppermute only.
A program may use at most 256 MiB of HBM per device.

v0:
```python
import jax
import jax.numpy as jnp
from jax import lax
from jax.sharding import PartitionSpec as P

HD = 128


def extended(cells, sides, width):
    for axis, dim in sides:
        count = lax.axis_size(axis)
        ends = count - 1
        head = lax.slice_in_dim(cells, 0, width, axis=dim)
        tail = lax.slice_in_dim(cells, cells.shape[dim] - width, cells.shape[dim], axis=dim)
        cells = jnp.concatenate(
            [
                lax.ppermute(tail, axis, [(i, (i + 1) % count) for i in range(ends)]),
                cells,
                lax.ppermute(head, axis, [((i + 1) % count, i) for i in range(ends)]),
            ],
            axis=dim,
        )
    return cells


def in_blocks(x, dim, peers):
    shape = x.shape
    tiles = x.reshape(*shape[:dim], peers, shape[dim] // peers, *shape[dim + 1 :])
    return jnp.moveaxis(tiles, dim, 0)


def summed_on_arrival(x, axis, dim):
    tiles = in_blocks(x, dim, lax.axis_size(axis))
    arrived = lax.all_to_all(tiles, axis, split_axis=0, concat_axis=0, tiled=True)
    return arrived.sum(axis=0)


def fetch_window(packed):
    return extended(packed, (("ta", 0), ("ha", 1), ("wa", 2)), 1)


def inside(position_now, count):
    offsets = jnp.arange(3, dtype=jnp.int32) - 1
    position = position_now + offsets
    return (position >= 0) & (position < count)


def shards(query_tiles, key_tiles, value_tiles, out_weight, gate):
    tile_rows = query_tiles.shape[3]
    features = query_tiles.shape[4]
    head_count = features // HD
    packed = jnp.concatenate([key_tiles, value_tiles], axis=4)
    window = fetch_window(packed)
    live_time = inside(lax.axis_index("ta"), lax.axis_size("ta"))
    live_height = inside(lax.axis_index("ha"), lax.axis_size("ha"))
    live_width = inside(lax.axis_index("wa"), lax.axis_size("wa"))
    live = live_time[:, None, None] & live_height[None, :, None] & live_width[None, None, :]
    live_keys = jnp.repeat(live.reshape(27), tile_rows)
    query_heads = jnp.moveaxis(query_tiles.reshape(tile_rows, head_count, HD), 1, 0)
    key_heads = jnp.moveaxis(window[..., :features].reshape(27 * tile_rows, head_count, HD), 1, 0)
    value_heads = jnp.moveaxis(window[..., features:].reshape(27 * tile_rows, head_count, HD), 1, 0)

    def attend_head(operands):
        queries, keys_here, values_here = operands
        scores = jnp.einsum(
            "qd,kd->qk", queries, keys_here, preferred_element_type=jnp.float32
        ) * HD ** (-0.5)
        scores = jnp.where(live_keys[None, :], scores, -1e30)
        peak = jnp.max(scores, axis=-1, keepdims=True)
        expo = jnp.exp(scores - peak)
        totals = jnp.sum(expo, axis=-1)
        probs = expo.astype(jnp.bfloat16)
        mixed = jnp.einsum("qk,kd->qd", probs, values_here, preferred_element_type=jnp.float32)
        return (mixed / totals[:, None]).astype(jnp.bfloat16)

    attended = lax.map(attend_head, (query_heads, key_heads, value_heads))
    attended = jnp.moveaxis(attended, 0, 1).reshape(tile_rows, features)
    partial_terms = jnp.dot(attended, out_weight, preferred_element_type=jnp.float32)
    summed = summed_on_arrival(partial_terms, "grp", 1)
    branch = (gate.astype(jnp.float32)[None, :] * summed).astype(jnp.bfloat16)
    return branch.reshape(1, 1, 1, tile_rows, branch.shape[1])


def solution(mesh):
    return jax.shard_map(
        shards,
        mesh=mesh,
        in_specs=(
            P("ta", "ha", "wa", None, "grp"),
            P("ta", "ha", "wa", None, "grp"),
            P("ta", "ha", "wa", None, "grp"),
            P("grp", None),
            P("grp"),
        ),
        out_specs=P("ta", "ha", "wa", None, "grp"),
        check_vma=False,
    )
```

profile of v0, /device:TPU:5, one launch (start us, length us, event | category | flops | bytes accessed | tf_op | source)
XLA Modules:
  0.0 1047.1 jit_solution(11661046474719894944)
XLA Ops:
  0.0 1.2 constant_dynamic-update-slice_fusion.2
  1.2 1.2 constant_dynamic-update-slice_fusion.1
  2.5 3.3 collective-permute-start
  5.8 1.3 collective-permute-start.1
  7.1 31.7 %collective-permute-done = bf16[1,1,1,256,3072]{4,3,2,1,0:T(8,128)(2,1)S(1)} collective-permute-done((bf16[1,1,1,256,3072]{4,3,2,1,0:T(8,128)(2,1)S(1)}, bf16[1,1,1,256,3072]{4,3,2,1,0:T(8,128)(2,1)S(1)}, u32[]{:S(2)}, u32[]{:S(2)}) %collective-permute-start) | collective-permute-done | bytes 1572896 | tf_op jit(solution)/shard_map/ppermute | solution.py:17
  38.7 3.9 collective-permute-done.1
  43.2 3.8 collective-permute-start.2
  47.1 1.3 collective-permute-start.3
  48.4 97.7 %collective-permute-done.2 = bf16[3,1,1,256,3072]{4,3,2,1,0:T(8,128)(2,1)S(1)} collective-permute-done((bf16[3,1,1,256,3072]{4,3,2,1,0:T(8,128)(2,1)S(1)}, bf16[3,1,1,256,3072]{4,3,2,1,0:T(8,128)(2,1)S(1)}, u32[]{:S(2)}, u32[]{:S(2)}) %collective-permute-start.2) | collective-permute-done | bytes 4718624 | tf_op jit(solution)/shard_map/ppermute | solution.py:17
  146.1 4.1 collective-permute-done.3
  150.2 6.5 pad_maximum_fusion.1
  156.7 5.2 collective-permute-start.4
  161.9 2.7 collective-permute-start.5
  164.9 2.3 copy.7
  167.2 12.7 %copy.16 = bf16[3072,1536]{1,0:T(8,128)(2,1)} copy(bf16[3072,1536]{0,1:T(8,128)(2,1)} %bitcast.56) | data formatting | bytes 18874368 | tf_op jit(solution)/shard_map/dot_general | solution.py:78
  179.8 586.4 %collective-permute-done.4 = bf16[3,3,1,256,3072]{4,3,2,1,0:T(8,128)(2,1)} collective-permute-done((bf16[3,3,1,256,3072]{4,3,2,1,0:T(8,128)(2,1)}, bf16[3,3,1,256,3072]{4,3,2,1,0:T(8,128)(2,1)}, u32[]{:S(2)}, u32[]{:S(2)}) %collective-permute-start.4) | collective-permute-done | bytes 14155808 | tf_op jit(solution)/shard_map/ppermute | solution.py:17
  766.2 4.4 collective-permute-done.5
  770.6 26.9 %pad_maximum_fusion = bf16[3,3,3,256,3072]{4,3,2,1,0:T(8,128)(2,1)} fusion(bf16[3,3,1,256,3072]{4,3,2,1,0:T(8,128)(2,1)} %collective-permute-done.5, bf16[3,1,1,256,3072]{4,3,2,1,0:T(8,128)(2,1)} %copy-done.1, bf16[1,1,1,256,3072]{4,3,2,1,0:T(8,128)(2,1)} %copy-done.2, bf16[1,1,1,256,3072]{4,3,2,1,0:T(8,128)(2,1)S(1)} %constant_dynamic-update-slice_fusion.1, ...), kind=kLoop, calls=%fused_computation.20 | loop fusion | flops 127401984 | bytes 84934656 | tf_op jit(solution)/shard_map/concatenate | solution.py:15
  797.5 28.3 %fusion.33 = (bf16[3,3,3,256,1536]{4,3,2,1,0:T(8,128)(2,1)}, bf16[3,3,3,256,1536]{4,3,2,1,0:T(8,128)(2,1)}) fusion(bf16[3,3,3,256,3072]{4,3,2,1,0:T(8,128)(2,1)} %pad_maximum_fusion), kind=kLoop, calls=%fused_computation.35 | loop fusion | bytes 84934656 | tf_op jit(solution)/shard_map/slice | solution.py:61
  825.8 38.3 %reshape.112 = bf16[6912,12,128]{2,1,0:T(8,128)(2,1)} reshape(bf16[3,3,3,256,1536]{4,3,2,1,0:T(8,128)(2,1)} %get-tuple-element.73) | data formatting | bytes 42467328 | tf_op jit(solution)/shard_map/reshape | solution.py:61
  864.1 22.0 %copy.10 = bf16[12,6912,128]{2,1,0:T(8,128)(2,1)} copy(bf16[12,6912,128]{2,0,1:T(8,128)(2,1)} %bitcast.54) | data formatting | bytes 42467328
  886.1 38.3 %reshape.111 = bf16[6912,12,128]{2,1,0:T(8,128)(2,1)} reshape(bf16[3,3,3,256,1536]{4,3,2,1,0:T(8,128)(2,1)} %get-tuple-element.74) | data formatting | bytes 42467328 | tf_op jit(solution)/shard_map/reshape | solution.py:60
  924.4 22.0 %copy.9 = bf16[12,6912,128]{2,1,0:T(8,128)(2,1)} copy(bf16[12,6912,128]{2,0,1:T(8,128)(2,1)} %bitcast.55) | data formatting | bytes 42467328
  946.4 85.1 %while.11 = (s32[]{:T(128)}, bf16[12,256,128]{1,2,0:T(8,128)(2,1)S(1)}, bf16[12,256,128]{1,2,0:T(8,128)(2,1)}, bf16[12,6912,128]{2,1,0:T(8,128)(2,1)}, bf16[12,6...) while((s32[]{:T(128)}, bf16[12,256,128]{1,2,0:T(8,128)(2,1)S(1)}, ...), condition=%wide.region_3.4_spmd.clone, body=%wide.region_0.3_spmd.clone.sunk | while | flops 918420992 | bytes 25200236 | solution.py:76
  946.5 2.9 fusion.43
  949.4 1.1 fusion.44
  950.6 2.8 fusion.45
  953.6 2.9 fusion.43
  956.5 1.1 fusion.44
  957.6 2.8 fusion.45
  960.7 2.9 fusion.43
  963.6 1.1 fusion.44
  964.7 2.8 fusion.45
  967.8 2.9 fusion.43
  970.7 1.1 fusion.44
  971.8 2.8 fusion.45
  974.9 2.9 fusion.43
  977.8 1.1 fusion.44
  978.9 2.8 fusion.45
  982.0 2.9 fusion.43
  984.9 1.1 fusion.44
  986.0 2.8 fusion.45
  989.1 2.9 fusion.43
  992.0 1.1 fusion.44
  993.1 2.8 fusion.45
  996.2 2.9 fusion.43
  999.1 1.1 fusion.44
  1000.2 2.8 fusion.45
  1003.3 2.9 fusion.43
  1006.2 1.1 fusion.44
  1007.3 2.8 fusion.45
  1010.4 2.9 fusion.43
  1013.3 1.1 fusion.44
  1014.4 2.8 fusion.45
  1017.5 2.9 fusion.43
  1020.4 1.1 fusion.44
  1021.5 2.8 fusion.45
  1024.6 2.9 fusion.43
  1027.5 1.1 fusion.44
  1028.6 2.8 fusion.45
  1031.6 5.3 convolution_bitcast_fusion
  1036.8 6.4 all_to_all.5
  1043.2 1.5 reduce_sum.20
  1044.7 2.4 fusion.31
  (66 shorter events, 3.4 us)
Async XLA Ops:
  2.5 36.3 %collective-permute-start = (bf16[1,1,1,256,3072]{4,3,2,1,0:T(8,128)(2,1)S(1)}, bf16[1,1,1,256,3072]{4,3,2,1,0:T(8,128)(2,1)S(1)}, u32[]{:S(2)}, u32[]{:S(2)}) collective-permute-start(bf16[1,1,1,256,3072]{4,3,2,1,0:T(8,128)(2,1)S(1)} %constant_dynamic-update-slice_fusion.1), channel_id=1, source_target_pairs={{0,16},{16,32},{32,48},{1,17},{17,33},{33,49},{2,18},{18,34},{34,5... | collective-permute-start | bytes 4718600 | tf_op jit(solution)/shard_map/ppermute | solution.py:17
  5.8 36.9 %collective-permute-start.1 = (bf16[1,1,1,256,3072]{4,3,2,1,0:T(8,128)(2,1)S(1)}, bf16[1,1,1,256,3072]{4,3,2,1,0:T(8,128)(2,1)S(1)}, u32[]{:S(2)}, u32[]{:S(2)}) collective-permute-start(bf16[1,1,1,256,3072]{4,3,2,1,0:T(8,128)(2,1)S(1)} %constant_dynamic-update-slice_fusion.1), channel_id=1, source_target_pairs={{16,0},{32,16},{48,32},{17,1},{33,17},{49,33},{18,2},{34,18},{50,3... | collective-permute-start | bytes 4718600 | tf_op jit(solution)/shard_map/ppermute | solution.py:19
  42.7 114.0 %copy-start.2 = (bf16[1,1,1,256,3072]{4,3,2,1,0:T(8,128)(2,1)}, bf16[1,1,1,256,3072]{4,3,2,1,0:T(8,128)(2,1)S(1)}, u32[]{:S(2)}) copy-start(bf16[1,1,1,256,3072]{4,3,2,1,0:T(8,128)(2,1)S(1)} %collective-permute-done.1) | copy-start | bytes 4718596
  43.2 102.9 %collective-permute-start.2 = (bf16[3,1,1,256,3072]{4,3,2,1,0:T(8,128)(2,1)S(1)}, bf16[3,1,1,256,3072]{4,3,2,1,0:T(8,128)(2,1)S(1)}, u32[]{:S(2)}, u32[]{:S(2)}) collective-permute-start(bf16[3,1,1,256,3072]{4,3,2,1,0:T(8,128)(2,1)S(1)} %pad_maximum_fusion.2), channel_id=1, source_target_pairs={{0,8},{1,9},{2,10},{3,11},{4,12},{5,13},{6,14},{7,15},{16,24},{17,... | collective-permute-start | bytes 14155784 | tf_op jit(solution)/shard_map/ppermute | solution.py:17
  47.1 103.2 %collective-permute-start.3 = (bf16[3,1,1,256,3072]{4,3,2,1,0:T(8,128)(2,1)S(1)}, bf16[3,1,1,256,3072]{4,3,2,1,0:T(8,128)(2,1)S(1)}, u32[]{:S(2)}, u32[]{:S(2)}) collective-permute-start(bf16[3,1,1,256,3072]{4,3,2,1,0:T(8,128)(2,1)S(1)} %pad_maximum_fusion.2), channel_id=1, source_target_pairs={{8,0},{9,1},{10,2},{11,3},{12,4},{13,5},{14,6},{15,7},{24,16},{25,... | collective-permute-start | bytes 14155784 | tf_op jit(solution)/shard_map/ppermute | solution.py:19
  146.1 10.6 %copy-start = (bf16[3,1,1,256,3072]{4,3,2,1,0:T(8,128)(2,1)}, bf16[3,1,1,256,3072]{4,3,2,1,0:T(8,128)(2,1)S(1)}, u32[]{:S(2)}) copy-start(bf16[3,1,1,256,3072]{4,3,2,1,0:T(8,128)(2,1)S(1)} %collective-permute-done.2) | copy-start | bytes 14155780
  150.2 6.5 copy-start.1
  156.7 609.5 %collective-permute-start.4 = (bf16[3,3,1,256,3072]{4,3,2,1,0:T(8,128)(2,1)}, bf16[3,3,1,256,3072]{4,3,2,1,0:T(8,128)(2,1)}, u32[]{:S(2)}, u32[]{:S(2)}) collective-permute-start(bf16[3,3,1,256,3072]{4,3,2,1,0:T(8,128)(2,1)} %pad_maximum_fusion.1), channel_id=1, source_target_pairs={{0,1},{1,2},{2,3},{3,4},{4,5},{5,6},{6,7},{8,9},{9,10},{10,11},{11... | collective-permute-start | bytes 42467336 | tf_op jit(solution)/shard_map/ppermute | solution.py:17
  161.9 608.7 %collective-permute-start.5 = (bf16[3,3,1,256,3072]{4,3,2,1,0:T(8,128)(2,1)}, bf16[3,3,1,256,3072]{4,3,2,1,0:T(8,128)(2,1)}, u32[]{:S(2)}, u32[]{:S(2)}) collective-permute-start(bf16[3,3,1,256,3072]{4,3,2,1,0:T(8,128)(2,1)} %pad_maximum_fusion.1), channel_id=1, source_target_pairs={{1,0},{2,1},{3,2},{4,3},{5,4},{6,5},{7,6},{9,8},{10,9},{11,10},{12... | collective-permute-start | bytes 42467336 | tf_op jit(solution)/shard_map/ppermute | solution.py:19
  167.2 12.7 %copy-start.3 = (bf16[1536]{0:T(1024)(128)(2,1)S(1)}, bf16[1536]{0:T(1024)(128)(2,1)}, u32[]{:S(2)}) copy-start(bf16[1536]{0:T(1024)(128)(2,1)} %param.11) | copy-start | bytes 9220
  924.4 22.0 %copy-start.4 = (bf16[12,256,128]{1,2,0:T(8,128)(2,1)S(1)}, bf16[12,256,128]{1,2,0:T(8,128)(2,1)}, u32[]{:S(2)}) copy-start(bf16[12,256,128]{1,2,0:T(8,128)(2,1)} %custom-call.1) | copy-start | bytes 2359300
where the time goes:
time: 1050 us
  waiting for transfers between devices  728 us (69%)
  local copies, waits for them, and re-layouts  169 us (16%)
  matrix products  73.7 us (7%)
  other arithmetic  51.7 us (5%)
  starting transfers between devices  17.6 us (2%)
    ppermute x3, waiting for transfers between devices, extended(): lax.ppermute(tail, axis, [(i, (i + 1) % count) for i in range(ends)])  716 us
    unnamed x14, local copies, waits for them, and re-layouts  47.5 us
    reshape x1, local copies, waits for them, and re-layouts, shards(): window[..., features:].reshape(27 * tile_rows, head_count, HD)  38.3 us
    reshape x1, local copies, waits for them, and re-layouts, shards(): window[..., :features].reshape(27 * tile_rows, head_count, HD)  38.3 us
    dot_general x12, matrix products, attend_head(): jnp.einsum('qd,kd->qk', queries, keys_here, preferred_element_type=jnp.fl...  34.7 us
    concatenate x3, other arithmetic, extended(): jnp.concatenate([lax.ppermute(tail, axis, [(i, (i + 1) % count) for i in...  33.9 us
    dot_general x12, matrix products, attend_head(): jnp.einsum('qk,kd->qd', probs, values_here, preferred_element_type=jnp.fl...  33.7 us
    slice x1, local copies, waits for them, and re-layouts, shards(): window[..., features:].reshape(27 * tile_rows, head_count, HD)  28.3 us
  transfers between devices with their start and end apart: 6, of which 6 were waited for; matrix products, arithmetic and copies ran while one was open for 1% of the time, Pallas kernels for 0%

commit v1 on v0

v1 whole, which is shorter than its diff:
```python
import functools
import math

import jax
import jax.numpy as jnp
from jax import lax
from jax.experimental import pallas as pl
from jax.experimental.pallas import tpu as pltpu
from jax.sharding import PartitionSpec as P

HD = 128
TILE = 256
AXES = ("grp", "ta", "ha", "wa")
FLIP = (0, 1, 1, 0)
SPLITS = ((0, 1, 2),)
SCALE = HD**-0.5 * math.log2(math.e)
F32 = jnp.float32
BF16 = jnp.bfloat16


def flat(core, y, z, x):
    return ((core * 4 + y) * 2 + z % 2) * 8 + x * 2 + z // 2


def pairs(move):
    found = []
    for core in range(2):
        for y in range(4):
            for z in range(4):
                for x in range(4):
                    there = move(core, y, z, x)
                    if there is not None:
                        found.append((flat(core, y, z, x), flat(*there)))
    return sorted(found)


def out_to_heads(step):
    def move(core, y, z, x):
        half = y // 2
        return FLIP[y], (core if half == 0 else 3 - core), (z + step) % 4, x

    return pairs(move)


def back_to_tiles(step):
    return sorted((b, a) for a, b in out_to_heads(step))


def to_partner(core, y, z, x):
    return 1 - core, y, z, x


def to_outer(core, y, z, x):
    return (core, 3 - y, z, x) if core == 1 else None


def to_edge(step):
    def move(core, y, z, x):
        x_there = x + 1 if ((z - step) % 4) >= 2 else x - 1
        return (core, y, z, x_there) if 0 <= x_there < 4 else None

    return pairs(move)


def send(x, perm):
    return lax.ppermute(x, AXES, perm)


def pack_body(place, *refs):
    ins, outs = refs[:12], refs[12:]
    at = 0
    for group in SPLITS:
        for step in range(4):
            q_in, k_in, v_in = ins[3 * step : 3 * step + 3]
            kv_out, q_out = outs[at : at + 2]
            at += 2
            for n, head in enumerate(group):
                cols = slice(head * HD, (head + 1) * HD)
                kv_out[n, 0] = k_in[:, cols]
                kv_out[n, 1] = v_in[:, cols]
                q_out[n] = q_in[:, cols]


def pack(place, q, k, v):
    specs = []
    for step in range(4):
        spec = pl.BlockSpec((TILE, 3 * HD), lambda i, place, step=step: (0, (place[0] + step) % 4))
        specs += [spec] * 3
    shapes, out_specs = [], []
    for group in SPLITS:
        for step in range(4):
            for dims in ((len(group), 2, TILE, HD), (len(group), TILE, HD)):
                shapes.append(jax.ShapeDtypeStruct(dims, BF16))
                out_specs.append(pl.BlockSpec(dims, lambda i, place, r=len(dims): (0,) * r))
    flat_out = pl.pallas_call(
        pack_body,
        grid_spec=pltpu.PrefetchScalarGridSpec(
            num_scalar_prefetch=1, grid=(1,), in_specs=specs, out_specs=out_specs
        ),
        out_shape=shapes,
        name="pack",
    )(place, *([q, k, v] * 4))
    return [
        [(flat_out[2 * (4 * g + step)], flat_out[2 * (4 * g + step) + 1]) for step in range(4)]
        for g in range(len(SPLITS))
    ]


def attend_body(count, place, *refs):
    kv_in, refs = refs[:24], refs[24:]
    q_in, refs = refs[:4], refs[4:]
    outs, refs = refs[:4], refs[4:]
    kv_held, q_held, q_raw, peak, mixed, arrived = refs
    z, core, x = place[0], place[1], place[2]
    has_outer = core == 1

    def copies(head):
        kv = [
            pltpu.make_async_copy(kv_in[t].at[head], kv_held.at[t], arrived.at[t])
            for t in range(24)
        ]
        return kv

    ones = jnp.ones((TILE, HD), BF16)

    def update(side, tiles):
        q = q_held[side]
        keys = jnp.concatenate([kv_held[t, 0] for t in tiles], axis=0)
        values = jnp.concatenate(
            [jnp.concatenate([kv_held[t, 1], ones], axis=1) for t in tiles], axis=0
        )
        scores = lax.dot_general(q, keys, (((1,), (1,)), ((), ())), preferred_element_type=F32)
        scores = scores * SCALE
        before = peak[side]
        now = jnp.maximum(before, jnp.max(scores, axis=1, keepdims=True))
        peak[side] = now
        shrink = jnp.exp2(before - now)
        probs = jnp.exp2(scores - jnp.tile(now, (1, len(tiles) * TILE // HD)))
        fresh = jnp.dot(probs.astype(BF16), values, preferred_element_type=F32)
        mixed[side] = mixed[side] * jnp.concatenate([shrink, shrink], axis=1) + fresh

    for head in range(count):
        kv = copies(head)
        for c in kv:
            c.start()
        for step in range(4):
            z_from = (z - step + 4) % 4
            q_held[z_from // 2, pl.ds(pl.multiple_of((z_from % 2) * TILE, TILE), TILE), :] = q_in[
                step
            ][head]
        peak[...] = jnp.full_like(peak, -1e30)
        mixed[...] = jnp.zeros_like(mixed)
        for c in kv:
            c.wait()

        def main(side, carry):
            update(side, (0, 1, 2, 3))
            update(side, (4, 5, 6, 7))

            @pl.when(has_outer)
            def _():
                update(side, (8, 9, 10, 11))

            return carry

        lax.fori_loop(0, 2, main, 0)

        def edges(step, carry):
            z_from = (z - step + 4) % 4
            side = 1 - z_from // 2
            live = jnp.where(side == 0, x > 0, x < 3)

            @pl.when(live)
            def _():
                update(side, (12 + step, 16 + step))

                @pl.when(has_outer)
                def _():
                    update(side, (20 + step,))

            return carry

        lax.fori_loop(0, 4, edges, 0)

        for step in range(4):
            z_from = (z - step + 4) % 4
            rows = pl.ds(pl.multiple_of((z_from % 2) * TILE, TILE), TILE)
            total = mixed[z_from // 2, rows, HD:]
            outs[step][:, head * HD : (head + 1) * HD] = (
                mixed[z_from // 2, rows, :HD] / total
            ).astype(BF16)


def attend(place, count, tiles, queries):
    hbm = pl.BlockSpec(memory_space=pltpu.MemorySpace.HBM)
    whole = pl.BlockSpec(memory_space=pltpu.MemorySpace.VMEM)
    smem = pl.BlockSpec(memory_space=pltpu.MemorySpace.SMEM)
    keys_seen = 18 * TILE
    return pl.pallas_call(
        functools.partial(attend_body, count),
        in_specs=[smem] + [hbm] * 24 + [whole] * 4,
        out_specs=[whole] * 4,
        out_shape=[jax.ShapeDtypeStruct((TILE, count * HD), BF16)] * 4,
        scratch_shapes=[
            pltpu.VMEM((24, 2, TILE, HD), BF16),
            pltpu.VMEM((2, 2 * TILE, HD), BF16),
            pltpu.VMEM((4, TILE, HD), BF16),
            pltpu.VMEM((2, 2 * TILE, HD), F32),
            pltpu.VMEM((2, 2 * TILE, 2 * HD), F32),
            pltpu.SemaphoreType.DMA((24,)),
        ],
        cost_estimate=pl.CostEstimate(
            flops=count * 4 * 1024 * keys_seen * HD,
            bytes_accessed=count * 24 * 2 * TILE * HD * 2,
            transcendentals=count * 1024 * keys_seen,
        ),
        compiler_params=pltpu.CompilerParams(vmem_limit_bytes=48 * 1024 * 1024),
        name="attend",
    )(place, *tiles, *queries)


def project_body(groups, place, *refs):
    own, refs = refs[: 4 * groups], refs[4 * groups :]
    other, refs = refs[: 4 * groups], refs[4 * groups :]
    w_own, w_other, gate, out = refs
    z = place[0]
    total = None
    for chunks, weight in ((own, w_own), (other, w_other)):
        for step in range(4):
            rows = pl.ds(pl.multiple_of(((z + step) % 4) * 3 * HD, 3 * HD), 3 * HD)
            left = jnp.concatenate([chunks[4 * g + step][...] for g in range(groups)], axis=1)
            term = jnp.dot(left, weight[rows, :], preferred_element_type=F32)
            total = term if total is None else total + term
    out[...] = (gate[...].astype(F32) * total).astype(BF16)


def project(place, own, other, weight, weight_other, gate):
    groups = len(own) // 4
    features = weight.shape[0]
    cols = features // 3
    chunk = [pl.BlockSpec(a.shape, lambda i, place: (0, 0)) for a in own]
    return pl.pallas_call(
        functools.partial(project_body, groups),
        grid_spec=pltpu.PrefetchScalarGridSpec(
            num_scalar_prefetch=1,
            grid=(3,),
            in_specs=chunk
            + chunk
            + [
                pl.BlockSpec((features, cols), lambda i, place: (0, place[1] * 3 + i)),
                pl.BlockSpec((features, cols), lambda i, place: (0, i)),
                pl.BlockSpec((1, cols), lambda i, place: (0, i)),
            ],
            out_specs=pl.BlockSpec((TILE, cols), lambda i, place: (0, i)),
        ),
        out_shape=jax.ShapeDtypeStruct((TILE, features), BF16),
        cost_estimate=pl.CostEstimate(
            flops=2 * TILE * 2 * features * features,
            bytes_accessed=4 * features * features,
            transcendentals=0,
        ),
        compiler_params=pltpu.CompilerParams(vmem_limit_bytes=48 * 1024 * 1024),
        name="project",
    )(place, *own, *other, weight, weight_other, gate)


def shards(query_tiles, key_tiles, value_tiles, out_weight, gate):
    features = query_tiles.shape[4]
    q, k, v = (a.reshape(TILE, features) for a in (query_tiles, key_tiles, value_tiles))
    core, y = lax.axis_index("grp"), lax.axis_index("ta")
    wide = lax.axis_index("wa")
    z, x = (wide % 2) * 2 + lax.axis_index("ha"), wide // 2
    place = jnp.stack([z, core, x, y]).astype(jnp.int32)
    partner = pairs(to_partner)
    outer = pairs(to_outer)
    weight_away = lax.dynamic_slice_in_dim(out_weight, (1 - core) * features, features, axis=1)
    weight_other = send(weight_away, partner)
    packed = pack(place, q, k, v)
    attended, attended_other = [], []
    for group, blocks in zip(SPLITS, packed):
        kv_own = [send(blocks[s][0], out_to_heads(s)) for s in range(4)]
        queries = [send(blocks[s][1], out_to_heads(s)) for s in range(4)]
        kv_outer = [send(a, outer) for a in kv_own]
        edge_own = [send(kv_own[s], to_edge(s)) for s in range(4)]
        kv_inner = [send(a, partner) for a in kv_own]
        edge_outer = [send(kv_outer[s], to_edge(s)) for s in range(4)]
        edge_inner = [send(a, partner) for a in edge_own]
        tiles = kv_own + kv_inner + kv_outer + edge_own + edge_inner + edge_outer
        outs = attend(place, len(group), tiles, queries)
        outs = [send(outs[s], back_to_tiles(s)) for s in range(4)]
        attended += outs
        attended_other += [send(a, partner) for a in outs]
    branch = project(place, attended, attended_other, out_weight, weight_other, gate.reshape(1, -1))
    return branch.reshape(1, 1, 1, TILE, features)


def solution(mesh):
    spec = P("ta", "ha", "wa", None, "grp")
    return jax.shard_map(
        shards,
        mesh=mesh,
        in_specs=(spec, spec, spec, P("grp", None), P("grp")),
        out_specs=spec,
        check_vma=False,
    )
```

time: 1050 us -> 172 us (0.16)
  waiting for transfers between devices: 728 us -> 39.5 us
  local copies, waits for them, and re-layouts: 169 us -> 6.27 us
  matrix products: 73.7 us -> 0 us
  Pallas kernels: 0 us -> 58.8 us
  other arithmetic: 51.7 us -> 0.61 us
  starting transfers between devices: 17.6 us -> 63.9 us
    ppermute x6 -> x37, waiting for transfers between devices: 728 us -> 39.5 us  [send(): return lax.ppermute(x, AXES, perm)]
    reshape x2 -> x1, local copies, waits for them, and re-layouts: 76.6 us -> 0.01 us  [shards(): gate.reshape(1, -1)]
    dot_general x25 -> x0, matrix products: 73.7 us -> none  [the longest x12 34.7 us: attend_head(): jnp.einsum('qd,kd->qk', queries, keys_here, preferred_element_type=jnp.fl...]
    pallas_call x0 -> x3, Pallas kernels: none -> 58.8 us  [the longest x1 46.8 us: attend(): pl.pallas_call(functools.partial(attend_body, count), in_specs=[smem] + [...]
    ppermute x6 -> x37, starting transfers between devices: 17.6 us -> 63.9 us  [send(): return lax.ppermute(x, AXES, perm)]
    unnamed x14 -> x30, local copies, waits for them, and re-layouts: 47.5 us -> 1.47 us
    concatenate x3 -> x0, other arithmetic: 33.9 us -> none  [extended(): jnp.concatenate([lax.ppermute(tail, axis, [(i, (i + 1) % count) for i in...]
    slice x1 -> x0, local copies, waits for them, and re-layouts: 28.3 us -> none  [shards(): window[..., features:].reshape(27 * tile_rows, head_count, HD)]
  transfers between devices with their start and end apart: 6 -> 37, of which waited for: 6 -> 16; matrix products, arithmetic and copies ran while one was open for 1% -> 0% of each run, Pallas kernels for 0% -> 30%
where the time goes in v1:
time: 172 us; the launch traced here: 169 us
  starting transfers between devices  63.9 us (37%)
  Pallas kernels  58.8 us (34%)
  waiting for transfers between devices  39.5 us (23%)
  local copies, waits for them, and re-layouts  6.27 us (4%)
    ppermute x37, starting transfers between devices, send(): return lax.ppermute(x, AXES, perm)  63.9 us
    pallas_call x1, Pallas kernels, attend(): pl.pallas_call(functools.partial(attend_body, count), in_specs=[smem] + [...  46.8 us
    ppermute x37, waiting for transfers between devices, send(): return lax.ppermute(x, AXES, perm)  39.5 us
    pallas_call x1, Pallas kernels, project(): pl.pallas_call(functools.partial(project_body, groups), grid_spec=pltpu.P...  7.64 us
    dynamic_slice x1, local copies, waits for them, and re-layouts, shards(): lax.dynamic_slice_in_dim(out_weight, (1 - core) * features, features, axi...  4.8 us
    pallas_call x1, Pallas kernels, pack(): pl.pallas_call(pack_body, grid_spec=pltpu.PrefetchScalarGridSpec(num_scal...  4.32 us
  transfers between devices with their start and end apart: 37, of which 16 were waited for; matrix products, arithmetic and copies ran while one was open for 0% of the time, Pallas kernels for 30%

profile of v1, /device:TPU:5, one launch (start us, length us, event | category | flops | bytes accessed | tf_op | source)
XLA Modules:
  0.0 169.5 jit_solution(15569935862788961944)
XLA Ops:
  0.0 4.8 %constant_dynamic-slice_fusion = bf16[1536,1536]{1,0:T(8,128)(2,1)} fusion(bf16[1536,3072]{1,0:T(8,128)(2,1)} %refs_8_.1, s32[]{:T(128)S(6)} %select_n.16), kind=kLoop, calls=%fused_computation.1 | loop fusion | bytes 9437188 | tf_op jit(solution)/shard_map/dynamic_slice | solution.py:276
  4.8 0.7 collective-permute-start.36
  5.5 0.6 pad_add_fusion.place
  6.1 4.3 %pack.1 = (bf16[3,2,256,128]{3,2,1,0:T(8,128)(2,1)}, bf16[3,256,128]{2,1,0:T(8,128)(2,1)}, bf16[3,2,256,128]{3,2,1,0:T(8,128)(2,1)}, bf16[3,256,128]{2,1,0:T(8,1...) custom-call(s32[4]{0:T(128)} %pad_add_fusion.place, ...), custom_call_target="tpu_custom_call" | custom-call | tf_op jit(solution)/shard_map/pack/pallas_call | solution.py:95
  10.4 3.1 %collective-permute-start.24 = (bf16[3,256,128]{2,1,0:T(8,128)(2,1)}, bf16[3,256,128]{2,1,0:T(8,128)(2,1)S(1)}, u32[]{:S(2)}, u32[]{:S(2)}) collective-permute-start(bf16[3,256,128]{2,1,0:T(8,128)(2,1)} %get-tuple-element.21), channel_id=1, source_target_pairs={{0,0},{1,1},{2,2},{3,3},{4,4},{5,5},{6,6},{7,7},{8,8},{9,9},{10,10... | collective-permute-start | bytes 589832 | tf_op jit(solution)/shard_map/ppermute | solution.py:66
  13.5 2.0 %collective-permute-start.25 = (bf16[3,256,128]{2,1,0:T(8,128)(2,1)}, bf16[3,256,128]{2,1,0:T(8,128)(2,1)S(1)}, u32[]{:S(2)}, u32[]{:S(2)}) collective-permute-start(bf16[3,256,128]{2,1,0:T(8,128)(2,1)} %get-tuple-element.22), channel_id=1, source_target_pairs={{0,8},{1,9},{2,10},{3,11},{4,12},{5,13},{6,14},{7,15},{8,1},{9,0},... | collective-permute-start | bytes 589832 | tf_op jit(solution)/shard_map/ppermute | solution.py:66
  15.5 4.2 %collective-permute-start.26 = (bf16[3,256,128]{2,1,0:T(8,128)(2,1)}, bf16[3,256,128]{2,1,0:T(8,128)(2,1)S(1)}, u32[]{:S(2)}, u32[]{:S(2)}) collective-permute-start(bf16[3,256,128]{2,1,0:T(8,128)(2,1)} %get-tuple-element.23), channel_id=1, source_target_pairs={{0,1},{1,0},{2,3},{3,2},{4,5},{5,4},{6,7},{7,6},{8,9},{9,8},{10,11... | collective-permute-start | bytes 589832 | tf_op jit(solution)/shard_map/ppermute | solution.py:66
  19.7 1.0 collective-permute-start.27
  20.7 0.0 collective-permute-done.24.refs_24_
  20.7 3.1 %collective-permute-start = (bf16[3,2,256,128]{3,2,1,0:T(8,128)(2,1)}, bf16[3,2,256,128]{3,2,1,0:T(8,128)(2,1)S(1)}, u32[]{:S(2)}, u32[]{:S(2)}) collective-permute-start(bf16[3,2,256,128]{3,2,1,0:T(8,128)(2,1)} %get-tuple-element.17), channel_id=1, source_target_pairs={{0,0},{1,1},{2,2},{3,3},{4,4},{5,5},{6,6},{7,7},{8,8},{9,9},{10,10... | collective-permute-start | bytes 1179656 | tf_op jit(solution)/shard_map/ppermute | solution.py:66
  23.8 0.0 collective-permute-done.25.refs_25_
  23.8 1.1 collective-permute-start.1
  24.9 0.7 collective-permute-done.26.refs_26_
  25.5 2.0 %collective-permute-start.2 = (bf16[3,2,256,128]{3,2,1,0:T(8,128)(2,1)}, bf16[3,2,256,128]{3,2,1,0:T(8,128)(2,1)S(1)}, u32[]{:S(2)}, u32[]{:S(2)}) collective-permute-start(bf16[3,2,256,128]{3,2,1,0:T(8,128)(2,1)} %get-tuple-element.19), channel_id=1, source_target_pairs={{0,1},{1,0},{2,3},{3,2},{4,5},{5,4},{6,7},{7,6},{8,9},{9,8},{10,11... | collective-permute-start | bytes 1179656 | tf_op jit(solution)/shard_map/ppermute | solution.py:66
  27.6 3.1 %collective-permute-start.3 = (bf16[3,2,256,128]{3,2,1,0:T(8,128)(2,1)}, bf16[3,2,256,128]{3,2,1,0:T(8,128)(2,1)S(1)}, u32[]{:S(2)}, u32[]{:S(2)}) collective-permute-start(bf16[3,2,256,128]{3,2,1,0:T(8,128)(2,1)} %get-tuple-element.20), channel_id=1, source_target_pairs={{0,9},{1,8},{2,11},{3,10},{4,13},{5,12},{6,15},{7,14},{8,0},{9,1},... | collective-permute-start | bytes 1179656 | tf_op jit(solution)/shard_map/ppermute | solution.py:66
  30.6 0.1 collective-permute-done.refs_0_
  30.7 2.2 %collective-permute-start.12 = (bf16[3,2,256,128]{3,2,1,0:T(8,128)(2,1)S(1)}, bf16[3,2,256,128]{3,2,1,0:T(8,128)(2,1)S(1)}, u32[]{:S(2)}, u32[]{:S(2)}) collective-permute-start(bf16[3,2,256,128]{3,2,1,0:T(8,128)(2,1)S(1)} %collective-permute-done.refs_0_), channel_id=1, source_target_pairs={{1,3},{2,0},{3,5},{4,2},{5,7},{6,4},{9,11},{10,8},{11,13},{12,10},... | collective-permute-start | bytes 1179656 | tf_op jit(solution)/shard_map/ppermute | solution.py:66
  32.8 3.8 %collective-permute-done.1.refs_1_ = bf16[3,2,256,128]{3,2,1,0:T(8,128)(2,1)S(1)} collective-permute-done((bf16[3,2,256,128]{3,2,1,0:T(8,128)(2,1)}, bf16[3,2,256,128]{3,2,1,0:T(8,128)(2,1)S(1)}, u32[]{:S(2)}, u32[]{:S(2)}) %collective-permute-start.1) | collective-permute-done | bytes 393248 | tf_op jit(solution)/shard_map/ppermute | solution.py:66
  36.6 2.8 %collective-permute-start.13 = (bf16[3,2,256,128]{3,2,1,0:T(8,128)(2,1)S(1)}, bf16[3,2,256,128]{3,2,1,0:T(8,128)(2,1)S(1)}, u32[]{:S(2)}, u32[]{:S(2)}) collective-permute-start(bf16[3,2,256,128]{3,2,1,0:T(8,128)(2,1)S(1)} %collective-permute-done.1.refs_1_), channel_id=1, source_target_pairs={{0,2},{2,4},{3,1},{4,6},{5,3},{7,5},{9,11},{10,8},{11,13},{12,10},... | collective-permute-start | bytes 1179656 | tf_op jit(solution)/shard_map/ppermute | solution.py:66
  39.4 1.7 %collective-permute-done.2.refs_2_ = bf16[3,2,256,128]{3,2,1,0:T(8,128)(2,1)S(1)} collective-permute-done((bf16[3,2,256,128]{3,2,1,0:T(8,128)(2,1)}, bf16[3,2,256,128]{3,2,1,0:T(8,128)(2,1)S(1)}, u32[]{:S(2)}, u32[]{:S(2)}) %collective-permute-start.2) | collective-permute-done | bytes 393248 | tf_op jit(solution)/shard_map/ppermute | solution.py:66
  41.2 2.8 %collective-permute-start.14 = (bf16[3,2,256,128]{3,2,1,0:T(8,128)(2,1)S(1)}, bf16[3,2,256,128]{3,2,1,0:T(8,128)(2,1)S(1)}, u32[]{:S(2)}, u32[]{:S(2)}) collective-permute-start(bf16[3,2,256,128]{3,2,1,0:T(8,128)(2,1)S(1)} %collective-permute-done.2.refs_2_), channel_id=1, source_target_pairs={{0,2},{2,4},{3,1},{4,6},{5,3},{7,5},{8,10},{10,12},{11,9},{12,14},... | collective-permute-start | bytes 1179656 | tf_op jit(solution)/shard_map/ppermute | solution.py:66
  44.0 0.0 collective-permute-done.3.refs_3_
  44.0 2.5 %collective-permute-start.15 = (bf16[3,2,256,128]{3,2,1,0:T(8,128)(2,1)S(1)}, bf16[3,2,256,128]{3,2,1,0:T(8,128)(2,1)S(1)}, u32[]{:S(2)}, u32[]{:S(2)}) collective-permute-start(bf16[3,2,256,128]{3,2,1,0:T(8,128)(2,1)S(1)} %collective-permute-done.3.refs_3_), channel_id=1, source_target_pairs={{1,3},{2,0},{3,5},{4,2},{5,7},{6,4},{8,10},{10,12},{11,9},{12,14},... | collective-permute-start | bytes 1179656 | tf_op jit(solution)/shard_map/ppermute | solution.py:66
  46.5 4.5 %collective-permute-start.8 = (bf16[3,2,256,128]{3,2,1,0:T(8,128)(2,1)S(1)}, bf16[3,2,256,128]{3,2,1,0:T(8,128)(2,1)S(1)}, u32[]{:S(2)}, u32[]{:S(2)}) collective-permute-start(bf16[3,2,256,128]{3,2,1,0:T(8,128)(2,1)S(1)} %collective-permute-done.refs_0_), channel_id=1, source_target_pairs={{64,112},{65,113},{66,114},{67,115},{68,116},{69,117},{70,118},{71... | collective-permute-start | bytes 1179656 | tf_op jit(solution)/shard_map/ppermute | solution.py:66
  51.1 2.0 %collective-permute-start.9 = (bf16[3,2,256,128]{3,2,1,0:T(8,128)(2,1)S(1)}, bf16[3,2,256,128]{3,2,1,0:T(8,128)(2,1)S(1)}, u32[]{:S(2)}, u32[]{:S(2)}) collective-permute-start(bf16[3,2,256,128]{3,2,1,0:T(8,128)(2,1)S(1)} %collective-permute-done.1.refs_1_), channel_id=1, source_target_pairs={{64,112},{65,113},{66,114},{67,115},{68,116},{69,117},{70,118},{71... | collective-permute-start | bytes 1179656 | tf_op jit(solution)/shard_map/ppermute | solution.py:66
  53.1 4.5 %collective-permute-start.10 = (bf16[3,2,256,128]{3,2,1,0:T(8,128)(2,1)S(1)}, bf16[3,2,256,128]{3,2,1,0:T(8,128)(2,1)S(1)}, u32[]{:S(2)}, u32[]{:S(2)}) collective-permute-start(bf16[3,2,256,128]{3,2,1,0:T(8,128)(2,1)S(1)} %collective-permute-done.2.refs_2_), channel_id=1, source_target_pairs={{64,112},{65,113},{66,114},{67,115},{68,116},{69,117},{70,118},{71... | collective-permute-start | bytes 1179656 | tf_op jit(solution)/shard_map/ppermute | solution.py:66
  57.6 2.0 %collective-permute-start.11 = (bf16[3,2,256,128]{3,2,1,0:T(8,128)(2,1)S(1)}, bf16[3,2,256,128]{3,2,1,0:T(8,128)(2,1)S(1)}, u32[]{:S(2)}, u32[]{:S(2)}) collective-permute-start(bf16[3,2,256,128]{3,2,1,0:T(8,128)(2,1)S(1)} %collective-permute-done.3.refs_3_), channel_id=1, source_target_pairs={{64,112},{65,113},{66,114},{67,115},{68,116},{69,117},{70,118},{71... | collective-permute-start | bytes 1179656 | tf_op jit(solution)/shard_map/ppermute | solution.py:66
  59.6 0.1 collective-permute-start.4
  59.7 1.1 collective-permute-done.9.refs_9_
  60.8 0.0 collective-permute-start.5
  60.8 4.2 %collective-permute-done.10.refs_10_ = bf16[3,2,256,128]{3,2,1,0:T(8,128)(2,1)S(1)} collective-permute-done((bf16[3,2,256,128]{3,2,1,0:T(8,128)(2,1)S(1)}, bf16[3,2,256,128]{3,2,1,0:T(8,128)(2,1)S(1)}, u32[]{:S(2)}, u32[]{:S(2)}) %collective-permute-start.10) | collective-permute-done | bytes 393248 | tf_op jit(solution)/shard_map/ppermute | solution.py:66
  65.0 0.0 collective-permute-start.6
  65.0 4.2 %collective-permute-done.11.refs_11_ = bf16[3,2,256,128]{3,2,1,0:T(8,128)(2,1)S(1)} collective-permute-done((bf16[3,2,256,128]{3,2,1,0:T(8,128)(2,1)S(1)}, bf16[3,2,256,128]{3,2,1,0:T(8,128)(2,1)S(1)}, u32[]{:S(2)}, u32[]{:S(2)}) %collective-permute-start.11) | collective-permute-done | bytes 393248 | tf_op jit(solution)/shard_map/ppermute | solution.py:66
  69.2 0.0 collective-permute-start.7
  69.2 0.0 collective-permute-done.4.refs_4_
  69.2 0.5 collective-permute-start.16
  69.7 0.0 collective-permute-done.5.refs_5_
  69.7 0.1 collective-permute-start.17
  69.8 0.0 collective-permute-done.6.refs_6_
  69.8 0.4 collective-permute-start.18
  70.3 0.7 collective-permute-done.7.refs_7_
  71.0 0.1 collective-permute-start.19
  71.1 0.4 collective-permute-done.16.refs_16_
  71.5 2.2 %collective-permute-start.20 = (bf16[3,2,256,128]{3,2,1,0:T(8,128)(2,1)S(1)}, bf16[3,2,256,128]{3,2,1,0:T(8,128)(2,1)S(1)}, u32[]{:S(2)}, u32[]{:S(2)}) collective-permute-start(bf16[3,2,256,128]{3,2,1,0:T(8,128)(2,1)S(1)} %collective-permute-done.8.refs_8_), channel_id=1, source_target_pairs={{1,3},{2,0},{3,5},{4,2},{5,7},{6,4},{9,11},{10,8},{11,13},{12,10},... | collective-permute-start | bytes 1179656 | tf_op jit(solution)/shard_map/ppermute | solution.py:66
  73.7 0.0 collective-permute-done.17.refs_17_
  73.7 3.1 %collective-permute-start.21 = (bf16[3,2,256,128]{3,2,1,0:T(8,128)(2,1)S(1)}, bf16[3,2,256,128]{3,2,1,0:T(8,128)(2,1)S(1)}, u32[]{:S(2)}, u32[]{:S(2)}) collective-permute-start(bf16[3,2,256,128]{3,2,1,0:T(8,128)(2,1)S(1)} %collective-permute-done.9.refs_9_), channel_id=1, source_target_pairs={{0,2},{2,4},{3,1},{4,6},{5,3},{7,5},{9,11},{10,8},{11,13},{12,10},... | collective-permute-start | bytes 1179656 | tf_op jit(solution)/shard_map/ppermute | solution.py:66
  76.9 1.9 %collective-permute-start.22 = (bf16[3,2,256,128]{3,2,1,0:T(8,128)(2,1)S(1)}, bf16[3,2,256,128]{3,2,1,0:T(8,128)(2,1)S(1)}, u32[]{:S(2)}, u32[]{:S(2)}) collective-permute-start(bf16[3,2,256,128]{3,2,1,0:T(8,128)(2,1)S(1)} %collective-permute-done.10.refs_10_), channel_id=1, source_target_pairs={{0,2},{2,4},{3,1},{4,6},{5,3},{7,5},{8,10},{10,12},{11,9},{12,14},... | collective-permute-start | bytes 1179656 | tf_op jit(solution)/shard_map/ppermute | solution.py:66
  78.8 0.0 collective-permute-done.19.refs_19_
  78.8 3.5 %collective-permute-start.23 = (bf16[3,2,256,128]{3,2,1,0:T(8,128)(2,1)S(1)}, bf16[3,2,256,128]{3,2,1,0:T(8,128)(2,1)S(1)}, u32[]{:S(2)}, u32[]{:S(2)}) collective-permute-start(bf16[3,2,256,128]{3,2,1,0:T(8,128)(2,1)S(1)} %collective-permute-done.11.refs_11_), channel_id=1, source_target_pairs={{1,3},{2,0},{3,5},{4,2},{5,7},{6,4},{8,10},{10,12},{11,9},{12,14},... | collective-permute-start | bytes 1179656 | tf_op jit(solution)/shard_map/ppermute | solution.py:66
  82.4 1.6 collective-permute-done.20.refs_20_
  83.9 1.9 %collective-permute-done.21.refs_21_ = bf16[3,2,256,128]{3,2,1,0:T(8,128)(2,1)S(1)} collective-permute-done((bf16[3,2,256,128]{3,2,1,0:T(8,128)(2,1)S(1)}, bf16[3,2,256,128]{3,2,1,0:T(8,128)(2,1)S(1)}, u32[]{:S(2)}, u32[]{:S(2)}) %collective-permute-start.21) | collective-permute-done | bytes 393248 | tf_op jit(solution)/shard_map/ppermute | solution.py:66
  85.9 8.4 %collective-permute-done.22.refs_22_ = bf16[3,2,256,128]{3,2,1,0:T(8,128)(2,1)S(1)} collective-permute-done((bf16[3,2,256,128]{3,2,1,0:T(8,128)(2,1)S(1)}, bf16[3,2,256,128]{3,2,1,0:T(8,128)(2,1)S(1)}, u32[]{:S(2)}, u32[]{:S(2)}) %collective-permute-start.22) | collective-permute-done | bytes 393248 | tf_op jit(solution)/shard_map/ppermute | solution.py:66
  94.4 0.6 copy-done.13
  95.0 0.8 copy-done.14
  95.8 46.8 %attend.1 = (bf16[256,384]{1,0:T(8,128)(2,1)S(1)}, bf16[256,384]{1,0:T(8,128)(2,1)S(1)}, bf16[256,384]{1,0:T(8,128)(2,1)S(1)}, bf16[256,384]{1,0:T(8,128)(2,1)S(1)}) custom-call(s32[4]{0:T(128)S(1)} %copy-done, bf16[3,2,256,128]{3,2,1,0:T(8,128)(2,1)S(1)} %collective-permute-done.refs_0_, bf16[3,2,256,128]{3,2,1,0:T(8,128)(2,1)S(1)} %collective-permute-done.1.refs_1_, ...), custom_call_target="tpu_custom_call" | custom-call | flops 7247757312 | bytes 9437184 | tf_op jit(solution)/shard_map/attend/pallas_call | solution.py:199
  142.6 1.9 %collective-permute-start.28 = (bf16[256,384]{1,0:T(8,128)(2,1)S(1)}, bf16[256,384]{1,0:T(8,128)(2,1)S(1)}, u32[]{:S(2)}, u32[]{:S(2)}) collective-permute-start(bf16[256,384]{1,0:T(8,128)(2,1)S(1)} %get-tuple-element.25), channel_id=1, source_target_pairs={{0,0},{1,1},{2,2},{3,3},{4,4},{5,5},{6,6},{7,7},{8,8},{9,9},{10,10... | collective-permute-start | bytes 589832 | tf_op jit(solution)/shard_map/ppermute | solution.py:66
  144.6 6.2 %collective-permute-start.29 = (bf16[256,384]{1,0:T(8,128)(2,1)S(1)}, bf16[256,384]{1,0:T(8,128)(2,1)S(1)}, u32[]{:S(2)}, u32[]{:S(2)}) collective-permute-start(bf16[256,384]{1,0:T(8,128)(2,1)S(1)} %get-tuple-element.26), channel_id=1, source_target_pairs={{0,9},{1,8},{2,11},{3,10},{4,13},{5,12},{6,15},{7,14},{8,0},{9,1},... | collective-permute-start | bytes 589832 | tf_op jit(solution)/shard_map/ppermute | solution.py:66
  150.8 0.1 collective-permute-start.30
  150.9 0.3 collective-permute-start.31
  151.2 3.5 %collective-permute-done.29.refs_1_ = bf16[256,384]{1,0:T(8,128)(2,1)S(1)} collective-permute-done((bf16[256,384]{1,0:T(8,128)(2,1)S(1)}, bf16[256,384]{1,0:T(8,128)(2,1)S(1)}, u32[]{:S(2)}, u32[]{:S(2)}) %collective-permute-start.29) | collective-permute-done | bytes 196640 | tf_op jit(solution)/shard_map/ppermute | solution.py:66
  154.7 3.6 %collective-permute-done.30.refs_2_ = bf16[256,384]{1,0:T(8,128)(2,1)S(1)} collective-permute-done((bf16[256,384]{1,0:T(8,128)(2,1)S(1)}, bf16[256,384]{1,0:T(8,128)(2,1)S(1)}, u32[]{:S(2)}, u32[]{:S(2)}) %collective-permute-start.30) | collective-permute-done | bytes 196640 | tf_op jit(solution)/shard_map/ppermute | solution.py:66
  158.3 2.1 %collective-permute-done.31.refs_3_ = bf16[256,384]{1,0:T(8,128)(2,1)S(1)} collective-permute-done((bf16[256,384]{1,0:T(8,128)(2,1)S(1)}, bf16[256,384]{1,0:T(8,128)(2,1)S(1)}, u32[]{:S(2)}, u32[]{:S(2)}) %collective-permute-start.31) | collective-permute-done | bytes 196640 | tf_op jit(solution)/shard_map/ppermute | solution.py:66
  160.4 1.4 collective-permute-done.35.refs_7_
  161.8 7.6 %project.1 = bf16[256,1536]{1,0:T(8,128)(2,1)} custom-call(s32[4]{0:T(128)S(1)} %copy-done, bf16[256,384]{1,0:T(8,128)(2,1)S(1)} %collective-permute-done.28.refs_0_, bf16[256,384]{1,0:T(8,128)(2,1)S(1)} %collective-permute-done.29.refs_1_, bf16[256,384]{1,0:T(8,128)(2,1)S(1)} %collective-permute-done.30.refs_2_, ...), custom_call_target="tpu_custom_call" | custom-call | flops 2415919104 | bytes 9437184 | tf_op jit(solution)/shard_map/project/pallas_call | solution.py:242
  (46 shorter events, 0.1 us)
Async XLA Ops:
  4.8 157.0 %collective-permute-start.36 = (bf16[1536,1536]{1,0:T(8,128)(2,1)}, bf16[1536,1536]{1,0:T(8,128)(2,1)}, u32[]{:S(2)}, u32[]{:S(2)}) collective-permute-start(bf16[1536,1536]{1,0:T(8,128)(2,1)} %constant_dynamic-slice_fusion), channel_id=1, source_target_pairs={{0,64},{1,65},{2,66},{3,67},{4,68},{5,69},{6,70},{7,71},{8,72},{9,... | collective-permute-start | bytes 14155784 | tf_op jit(solution)/shard_map/ppermute | solution.py:66
  6.1 89.7 %copy-start = (s32[4]{0:T(128)S(1)}, s32[4]{0:T(128)}, u32[]{:S(2)}) copy-start(s32[4]{0:T(128)} %pad_add_fusion.place) | copy-start | bytes 52
  10.4 10.3 %collective-permute-start.24 = (bf16[3,256,128]{2,1,0:T(8,128)(2,1)}, bf16[3,256,128]{2,1,0:T(8,128)(2,1)S(1)}, u32[]{:S(2)}, u32[]{:S(2)}) collective-permute-start(bf16[3,256,128]{2,1,0:T(8,128)(2,1)} %get-tuple-element.21), channel_id=1, source_target_pairs={{0,0},{1,1},{2,2},{3,3},{4,4},{5,5},{6,6},{7,7},{8,8},{9,9},{10,10... | collective-permute-start | bytes 589832 | tf_op jit(solution)/shard_map/ppermute | solution.py:66
  13.5 10.3 %collective-permute-start.25 = (bf16[3,256,128]{2,1,0:T(8,128)(2,1)}, bf16[3,256,128]{2,1,0:T(8,128)(2,1)S(1)}, u32[]{:S(2)}, u32[]{:S(2)}) collective-permute-start(bf16[3,256,128]{2,1,0:T(8,128)(2,1)} %get-tuple-element.22), channel_id=1, source_target_pairs={{0,8},{1,9},{2,10},{3,11},{4,12},{5,13},{6,14},{7,15},{8,1},{9,0},... | collective-permute-start | bytes 589832 | tf_op jit(solution)/shard_map/ppermute | solution.py:66
  15.5 10.1 %collective-permute-start.26 = (bf16[3,256,128]{2,1,0:T(8,128)(2,1)}, bf16[3,256,128]{2,1,0:T(8,128)(2,1)S(1)}, u32[]{:S(2)}, u32[]{:S(2)}) collective-permute-start(bf16[3,256,128]{2,1,0:T(8,128)(2,1)} %get-tuple-element.23), channel_id=1, source_target_pairs={{0,1},{1,0},{2,3},{3,2},{4,5},{5,4},{6,7},{7,6},{8,9},{9,8},{10,11... | collective-permute-start | bytes 589832 | tf_op jit(solution)/shard_map/ppermute | solution.py:66
  19.7 7.9 %collective-permute-start.27 = (bf16[3,256,128]{2,1,0:T(8,128)(2,1)}, bf16[3,256,128]{2,1,0:T(8,128)(2,1)S(1)}, u32[]{:S(2)}, u32[]{:S(2)}) collective-permute-start(bf16[3,256,128]{2,1,0:T(8,128)(2,1)} %get-tuple-element.24), channel_id=1, source_target_pairs={{0,9},{1,8},{2,11},{3,10},{4,13},{5,12},{6,15},{7,14},{8,0},{9,1},... | collective-permute-start | bytes 589832 | tf_op jit(solution)/shard_map/ppermute | solution.py:66
  20.7 10.0 %collective-permute-start = (bf16[3,2,256,128]{3,2,1,0:T(8,128)(2,1)}, bf16[3,2,256,128]{3,2,1,0:T(8,128)(2,1)S(1)}, u32[]{:S(2)}, u32[]{:S(2)}) collective-permute-start(bf16[3,2,256,128]{3,2,1,0:T(8,128)(2,1)} %get-tuple-element.17), channel_id=1, source_target_pairs={{0,0},{1,1},{2,2},{3,3},{4,4},{5,5},{6,6},{7,7},{8,8},{9,9},{10,10... | collective-permute-start | bytes 1179656 | tf_op jit(solution)/shard_map/ppermute | solution.py:66
  23.8 12.8 %collective-permute-start.1 = (bf16[3,2,256,128]{3,2,1,0:T(8,128)(2,1)}, bf16[3,2,256,128]{3,2,1,0:T(8,128)(2,1)S(1)}, u32[]{:S(2)}, u32[]{:S(2)}) collective-permute-start(bf16[3,2,256,128]{3,2,1,0:T(8,128)(2,1)} %get-tuple-element.18), channel_id=1, source_target_pairs={{0,8},{1,9},{2,10},{3,11},{4,12},{5,13},{6,14},{7,15},{8,1},{9,0},... | collective-permute-start | bytes 1179656 | tf_op jit(solution)/shard_map/ppermute | solution.py:66
  25.5 15.6 %collective-permute-start.2 = (bf16[3,2,256,128]{3,2,1,0:T(8,128)(2,1)}, bf16[3,2,256,128]{3,2,1,0:T(8,128)(2,1)S(1)}, u32[]{:S(2)}, u32[]{:S(2)}) collective-permute-start(bf16[3,2,256,128]{3,2,1,0:T(8,128)(2,1)} %get-tuple-element.19), channel_id=1, source_target_pairs={{0,1},{1,0},{2,3},{3,2},{4,5},{5,4},{6,7},{7,6},{8,9},{9,8},{10,11... | collective-permute-start | bytes 1179656 | tf_op jit(solution)/shard_map/ppermute | solution.py:66
  27.6 132.8 %copy-start.1 = (bf16[1536]{0:T(1024)(128)(2,1)S(1)}, bf16[1536]{0:T(1024)(128)(2,1)}, u32[]{:S(2)}) copy-start(bf16[1536]{0:T(1024)(128)(2,1)} %param.9) | copy-start | bytes 9220
  27.6 16.5 %collective-permute-start.3 = (bf16[3,2,256,128]{3,2,1,0:T(8,128)(2,1)}, bf16[3,2,256,128]{3,2,1,0:T(8,128)(2,1)S(1)}, u32[]{:S(2)}, u32[]{:S(2)}) collective-permute-start(bf16[3,2,256,128]{3,2,1,0:T(8,128)(2,1)} %get-tuple-element.20), channel_id=1, source_target_pairs={{0,9},{1,8},{2,11},{3,10},{4,13},{5,12},{6,15},{7,14},{8,0},{9,1},... | collective-permute-start | bytes 1179656 | tf_op jit(solution)/shard_map/ppermute | solution.py:66
  30.7 15.8 %collective-permute-start.12 = (bf16[3,2,256,128]{3,2,1,0:T(8,128)(2,1)S(1)}, bf16[3,2,256,128]{3,2,1,0:T(8,128)(2,1)S(1)}, u32[]{:S(2)}, u32[]{:S(2)}) collective-permute-start(bf16[3,2,256,128]{3,2,1,0:T(8,128)(2,1)S(1)} %collective-permute-done.refs_0_), channel_id=1, source_target_pairs={{1,3},{2,0},{3,5},{4,2},{5,7},{6,4},{9,11},{10,8},{11,13},{12,10},... | collective-permute-start | bytes 1179656 | tf_op jit(solution)/shard_map/ppermute | solution.py:66
  36.6 14.4 %collective-permute-start.13 = (bf16[3,2,256,128]{3,2,1,0:T(8,128)(2,1)S(1)}, bf16[3,2,256,128]{3,2,1,0:T(8,128)(2,1)S(1)}, u32[]{:S(2)}, u32[]{:S(2)}) collective-permute-start(bf16[3,2,256,128]{3,2,1,0:T(8,128)(2,1)S(1)} %collective-permute-done.1.refs_1_), channel_id=1, source_target_pairs={{0,2},{2,4},{3,1},{4,6},{5,3},{7,5},{9,11},{10,8},{11,13},{12,10},... | collective-permute-start | bytes 1179656 | tf_op jit(solution)/shard_map/ppermute | solution.py:66
  41.2 11.8 %collective-permute-start.14 = (bf16[3,2,256,128]{3,2,1,0:T(8,128)(2,1)S(1)}, bf16[3,2,256,128]{3,2,1,0:T(8,128)(2,1)S(1)}, u32[]{:S(2)}, u32[]{:S(2)}) collective-permute-start(bf16[3,2,256,128]{3,2,1,0:T(8,128)(2,1)S(1)} %collective-permute-done.2.refs_2_), channel_id=1, source_target_pairs={{0,2},{2,4},{3,1},{4,6},{5,3},{7,5},{8,10},{10,12},{11,9},{12,14},... | collective-permute-start | bytes 1179656 | tf_op jit(solution)/shard_map/ppermute | solution.py:66
  44.0 13.6 %collective-permute-start.15 = (bf16[3,2,256,128]{3,2,1,0:T(8,128)(2,1)S(1)}, bf16[3,2,256,128]{3,2,1,0:T(8,128)(2,1)S(1)}, u32[]{:S(2)}, u32[]{:S(2)}) collective-permute-start(bf16[3,2,256,128]{3,2,1,0:T(8,128)(2,1)S(1)} %collective-permute-done.3.refs_3_), channel_id=1, source_target_pairs={{1,3},{2,0},{3,5},{4,2},{5,7},{6,4},{8,10},{10,12},{11,9},{12,14},... | collective-permute-start | bytes 1179656 | tf_op jit(solution)/shard_map/ppermute | solution.py:66
  46.5 47.8 %copy-start.2 = (bf16[3,2,256,128]{3,2,1,0:T(8,128)(2,1)}, bf16[3,2,256,128]{3,2,1,0:T(8,128)(2,1)S(1)}, u32[]{:S(2)}) copy-start(bf16[3,2,256,128]{3,2,1,0:T(8,128)(2,1)S(1)} %collective-permute-done.12.refs_12_) | copy-start | bytes 1179652
  46.5 13.1 %collective-permute-start.8 = (bf16[3,2,256,128]{3,2,1,0:T(8,128)(2,1)S(1)}, bf16[3,2,256,128]{3,2,1,0:T(8,128)(2,1)S(1)}, u32[]{:S(2)}, u32[]{:S(2)}) collective-permute-start(bf16[3,2,256,128]{3,2,1,0:T(8,128)(2,1)S(1)} %collective-permute-done.refs_0_), channel_id=1, source_target_pairs={{64,112},{65,113},{66,114},{67,115},{68,116},{69,117},{70,118},{71... | collective-permute-start | bytes 1179656 | tf_op jit(solution)/shard_map/ppermute | solution.py:66
  51.1 43.2 %copy-start.3 = (bf16[3,2,256,128]{3,2,1,0:T(8,128)(2,1)}, bf16[3,2,256,128]{3,2,1,0:T(8,128)(2,1)S(1)}, u32[]{:S(2)}) copy-start(bf16[3,2,256,128]{3,2,1,0:T(8,128)(2,1)S(1)} %collective-permute-done.13.refs_13_) | copy-start | bytes 1179652
  51.1 9.7 %collective-permute-start.9 = (bf16[3,2,256,128]{3,2,1,0:T(8,128)(2,1)S(1)}, bf16[3,2,256,128]{3,2,1,0:T(8,128)(2,1)S(1)}, u32[]{:S(2)}, u32[]{:S(2)}) collective-permute-start(bf16[3,2,256,128]{3,2,1,0:T(8,128)(2,1)S(1)} %collective-permute-done.1.refs_1_), channel_id=1, source_target_pairs={{64,112},{65,113},{66,114},{67,115},{68,116},{69,117},{70,118},{71... | collective-permute-start | bytes 1179656 | tf_op jit(solution)/shard_map/ppermute | solution.py:66
  53.0 41.3 %copy-start.4 = (bf16[3,2,256,128]{3,2,1,0:T(8,128)(2,1)}, bf16[3,2,256,128]{3,2,1,0:T(8,128)(2,1)S(1)}, u32[]{:S(2)}) copy-start(bf16[3,2,256,128]{3,2,1,0:T(8,128)(2,1)S(1)} %collective-permute-done.14.refs_14_) | copy-start | bytes 1179652
  53.1 12.0 %collective-permute-start.10 = (bf16[3,2,256,128]{3,2,1,0:T(8,128)(2,1)S(1)}, bf16[3,2,256,128]{3,2,1,0:T(8,128)(2,1)S(1)}, u32[]{:S(2)}, u32[]{:S(2)}) collective-permute-start(bf16[3,2,256,128]{3,2,1,0:T(8,128)(2,1)S(1)} %collective-permute-done.2.refs_2_), channel_id=1, source_target_pairs={{64,112},{65,113},{66,114},{67,115},{68,116},{69,117},{70,118},{71... | collective-permute-start | bytes 1179656 | tf_op jit(solution)/shard_map/ppermute | solution.py:66
  57.6 36.7 %copy-start.5 = (bf16[3,2,256,128]{3,2,1,0:T(8,128)(2,1)}, bf16[3,2,256,128]{3,2,1,0:T(8,128)(2,1)S(1)}, u32[]{:S(2)}) copy-start(bf16[3,2,256,128]{3,2,1,0:T(8,128)(2,1)S(1)} %collective-permute-done.15.refs_15_) | copy-start | bytes 1179652
  57.6 11.6 %collective-permute-start.11 = (bf16[3,2,256,128]{3,2,1,0:T(8,128)(2,1)S(1)}, bf16[3,2,256,128]{3,2,1,0:T(8,128)(2,1)S(1)}, u32[]{:S(2)}, u32[]{:S(2)}) collective-permute-start(bf16[3,2,256,128]{3,2,1,0:T(8,128)(2,1)S(1)} %collective-permute-done.3.refs_3_), channel_id=1, source_target_pairs={{64,112},{65,113},{66,114},{67,115},{68,116},{69,117},{70,118},{71... | collective-permute-start | bytes 1179656 | tf_op jit(solution)/shard_map/ppermute | solution.py:66
  59.6 9.6 %collective-permute-start.4 = (bf16[3,2,256,128]{3,2,1,0:T(8,128)(2,1)S(1)}, bf16[3,2,256,128]{3,2,1,0:T(8,128)(2,1)S(1)}, u32[]{:S(2)}, u32[]{:S(2)}) collective-permute-start(bf16[3,2,256,128]{3,2,1,0:T(8,128)(2,1)S(1)} %collective-permute-done.refs_0_), channel_id=1, source_target_pairs={{0,64},{1,65},{2,66},{3,67},{4,68},{5,69},{6,70},{7,71},{8,72},{9,... | collective-permute-start | bytes 1179656 | tf_op jit(solution)/shard_map/ppermute | solution.py:66
  60.8 8.9 %collective-permute-start.5 = (bf16[3,2,256,128]{3,2,1,0:T(8,128)(2,1)S(1)}, bf16[3,2,256,128]{3,2,1,0:T(8,128)(2,1)S(1)}, u32[]{:S(2)}, u32[]{:S(2)}) collective-permute-start(bf16[3,2,256,128]{3,2,1,0:T(8,128)(2,1)S(1)} %collective-permute-done.1.refs_1_), channel_id=1, source_target_pairs={{0,64},{1,65},{2,66},{3,67},{4,68},{5,69},{6,70},{7,71},{8,72},{9,... | collective-permute-start | bytes 1179656 | tf_op jit(solution)/shard_map/ppermute | solution.py:66
  65.0 4.8 %collective-permute-start.6 = (bf16[3,2,256,128]{3,2,1,0:T(8,128)(2,1)S(1)}, bf16[3,2,256,128]{3,2,1,0:T(8,128)(2,1)S(1)}, u32[]{:S(2)}, u32[]{:S(2)}) collective-permute-start(bf16[3,2,256,128]{3,2,1,0:T(8,128)(2,1)S(1)} %collective-permute-done.2.refs_2_), channel_id=1, source_target_pairs={{0,64},{1,65},{2,66},{3,67},{4,68},{5,69},{6,70},{7,71},{8,72},{9,... | collective-permute-start | bytes 1179656 | tf_op jit(solution)/shard_map/ppermute | solution.py:66
  69.2 25.1 %copy-start.6 = (bf16[3,2,256,128]{3,2,1,0:T(8,128)(2,1)}, bf16[3,2,256,128]{3,2,1,0:T(8,128)(2,1)S(1)}, u32[]{:S(2)}) copy-start(bf16[3,2,256,128]{3,2,1,0:T(8,128)(2,1)S(1)} %collective-permute-done.11.refs_11_) | copy-start | bytes 1179652
  69.2 1.7 %collective-permute-start.7 = (bf16[3,2,256,128]{3,2,1,0:T(8,128)(2,1)S(1)}, bf16[3,2,256,128]{3,2,1,0:T(8,128)(2,1)S(1)}, u32[]{:S(2)}, u32[]{:S(2)}) collective-permute-start(bf16[3,2,256,128]{3,2,1,0:T(8,128)(2,1)S(1)} %collective-permute-done.3.refs_3_), channel_id=1, source_target_pairs={{0,64},{1,65},{2,66},{3,67},{4,68},{5,69},{6,70},{7,71},{8,72},{9,... | collective-permute-start | bytes 1179656 | tf_op jit(solution)/shard_map/ppermute | solution.py:66
  69.2 2.3 %collective-permute-start.16 = (bf16[3,2,256,128]{3,2,1,0:T(8,128)(2,1)S(1)}, bf16[3,2,256,128]{3,2,1,0:T(8,128)(2,1)S(1)}, u32[]{:S(2)}, u32[]{:S(2)}) collective-permute-start(bf16[3,2,256,128]{3,2,1,0:T(8,128)(2,1)S(1)} %collective-permute-done.12.refs_12_), channel_id=1, source_target_pairs={{0,64},{1,65},{2,66},{3,67},{4,68},{5,69},{6,70},{7,71},{8,72},{9,... | collective-permute-start | bytes 1179656 | tf_op jit(solution)/shard_map/ppermute | solution.py:66
  69.7 4.0 %collective-permute-start.17 = (bf16[3,2,256,128]{3,2,1,0:T(8,128)(2,1)S(1)}, bf16[3,2,256,128]{3,2,1,0:T(8,128)(2,1)S(1)}, u32[]{:S(2)}, u32[]{:S(2)}) collective-permute-start(bf16[3,2,256,128]{3,2,1,0:T(8,128)(2,1)S(1)} %collective-permute-done.13.refs_13_), channel_id=1, source_target_pairs={{0,64},{1,65},{2,66},{3,67},{4,68},{5,69},{6,70},{7,71},{8,72},{9,... | collective-permute-start | bytes 1179656 | tf_op jit(solution)/shard_map/ppermute | solution.py:66
  69.8 7.0 %collective-permute-start.18 = (bf16[3,2,256,128]{3,2,1,0:T(8,128)(2,1)S(1)}, bf16[3,2,256,128]{3,2,1,0:T(8,128)(2,1)S(1)}, u32[]{:S(2)}, u32[]{:S(2)}) collective-permute-start(bf16[3,2,256,128]{3,2,1,0:T(8,128)(2,1)S(1)} %collective-permute-done.14.refs_14_), channel_id=1, source_target_pairs={{0,64},{1,65},{2,66},{3,67},{4,68},{5,69},{6,70},{7,71},{8,72},{9,... | collective-permute-start | bytes 1179656 | tf_op jit(solution)/shard_map/ppermute | solution.py:66
  71.0 7.8 %collective-permute-start.19 = (bf16[3,2,256,128]{3,2,1,0:T(8,128)(2,1)S(1)}, bf16[3,2,256,128]{3,2,1,0:T(8,128)(2,1)S(1)}, u32[]{:S(2)}, u32[]{:S(2)}) collective-permute-start(bf16[3,2,256,128]{3,2,1,0:T(8,128)(2,1)S(1)} %collective-permute-done.15.refs_15_), channel_id=1, source_target_pairs={{0,64},{1,65},{2,66},{3,67},{4,68},{5,69},{6,70},{7,71},{8,72},{9,... | collective-permute-start | bytes 1179656 | tf_op jit(solution)/shard_map/ppermute | solution.py:66
  71.5 22.8 %copy-start.7 = (bf16[3,2,256,128]{3,2,1,0:T(8,128)(2,1)}, bf16[3,2,256,128]{3,2,1,0:T(8,128)(2,1)S(1)}, u32[]{:S(2)}) copy-start(bf16[3,2,256,128]{3,2,1,0:T(8,128)(2,1)S(1)} %collective-permute-done.16.refs_16_) | copy-start | bytes 1179652
  71.5 12.4 %collective-permute-start.20 = (bf16[3,2,256,128]{3,2,1,0:T(8,128)(2,1)S(1)}, bf16[3,2,256,128]{3,2,1,0:T(8,128)(2,1)S(1)}, u32[]{:S(2)}, u32[]{:S(2)}) collective-permute-start(bf16[3,2,256,128]{3,2,1,0:T(8,128)(2,1)S(1)} %collective-permute-done.8.refs_8_), channel_id=1, source_target_pairs={{1,3},{2,0},{3,5},{4,2},{5,7},{6,4},{9,11},{10,8},{11,13},{12,10},... | collective-permute-start | bytes 1179656 | tf_op jit(solution)/shard_map/ppermute | solution.py:66
  73.7 20.7 %copy-start.8 = (bf16[3,2,256,128]{3,2,1,0:T(8,128)(2,1)}, bf16[3,2,256,128]{3,2,1,0:T(8,128)(2,1)S(1)}, u32[]{:S(2)}) copy-start(bf16[3,2,256,128]{3,2,1,0:T(8,128)(2,1)S(1)} %collective-permute-done.17.refs_17_) | copy-start | bytes 1179652
  73.7 12.2 %collective-permute-start.21 = (bf16[3,2,256,128]{3,2,1,0:T(8,128)(2,1)S(1)}, bf16[3,2,256,128]{3,2,1,0:T(8,128)(2,1)S(1)}, u32[]{:S(2)}, u32[]{:S(2)}) collective-permute-start(bf16[3,2,256,128]{3,2,1,0:T(8,128)(2,1)S(1)} %collective-permute-done.9.refs_9_), channel_id=1, source_target_pairs={{0,2},{2,4},{3,1},{4,6},{5,3},{7,5},{9,11},{10,8},{11,13},{12,10},... | collective-permute-start | bytes 1179656 | tf_op jit(solution)/shard_map/ppermute | solution.py:66
  76.9 17.5 %copy-start.9 = (bf16[3,2,256,128]{3,2,1,0:T(8,128)(2,1)}, bf16[3,2,256,128]{3,2,1,0:T(8,128)(2,1)S(1)}, u32[]{:S(2)}) copy-start(bf16[3,2,256,128]{3,2,1,0:T(8,128)(2,1)S(1)} %collective-permute-done.18.refs_18_) | copy-start | bytes 1179652
  76.9 17.4 %collective-permute-start.22 = (bf16[3,2,256,128]{3,2,1,0:T(8,128)(2,1)S(1)}, bf16[3,2,256,128]{3,2,1,0:T(8,128)(2,1)S(1)}, u32[]{:S(2)}, u32[]{:S(2)}) collective-permute-start(bf16[3,2,256,128]{3,2,1,0:T(8,128)(2,1)S(1)} %collective-permute-done.10.refs_10_), channel_id=1, source_target_pairs={{0,2},{2,4},{3,1},{4,6},{5,3},{7,5},{8,10},{10,12},{11,9},{12,14},... | collective-permute-start | bytes 1179656 | tf_op jit(solution)/shard_map/ppermute | solution.py:66
  78.8 15.6 %copy-start.10 = (bf16[3,2,256,128]{3,2,1,0:T(8,128)(2,1)}, bf16[3,2,256,128]{3,2,1,0:T(8,128)(2,1)S(1)}, u32[]{:S(2)}) copy-start(bf16[3,2,256,128]{3,2,1,0:T(8,128)(2,1)S(1)} %collective-permute-done.19.refs_19_) | copy-start | bytes 1179652
  78.8 15.5 %collective-permute-start.23 = (bf16[3,2,256,128]{3,2,1,0:T(8,128)(2,1)S(1)}, bf16[3,2,256,128]{3,2,1,0:T(8,128)(2,1)S(1)}, u32[]{:S(2)}, u32[]{:S(2)}) collective-permute-start(bf16[3,2,256,128]{3,2,1,0:T(8,128)(2,1)S(1)} %collective-permute-done.11.refs_11_), channel_id=1, source_target_pairs={{1,3},{2,0},{3,5},{4,2},{5,7},{6,4},{8,10},{10,12},{11,9},{12,14},... | collective-permute-start | bytes 1179656 | tf_op jit(solution)/shard_map/ppermute | solution.py:66
  83.9 10.5 %copy-start.11 = (bf16[3,2,256,128]{3,2,1,0:T(8,128)(2,1)}, bf16[3,2,256,128]{3,2,1,0:T(8,128)(2,1)S(1)}, u32[]{:S(2)}) copy-start(bf16[3,2,256,128]{3,2,1,0:T(8,128)(2,1)S(1)} %collective-permute-done.20.refs_20_) | copy-start | bytes 1179652
  85.9 8.5 %copy-start.12 = (bf16[3,2,256,128]{3,2,1,0:T(8,128)(2,1)}, bf16[3,2,256,128]{3,2,1,0:T(8,128)(2,1)S(1)}, u32[]{:S(2)}) copy-start(bf16[3,2,256,128]{3,2,1,0:T(8,128)(2,1)S(1)} %collective-permute-done.21.refs_21_) | copy-start | bytes 1179652
  94.3 0.7 copy-start.13
  95.0 0.8 copy-start.14
  142.6 8.5 %collective-permute-start.28 = (bf16[256,384]{1,0:T(8,128)(2,1)S(1)}, bf16[256,384]{1,0:T(8,128)(2,1)S(1)}, u32[]{:S(2)}, u32[]{:S(2)}) collective-permute-start(bf16[256,384]{1,0:T(8,128)(2,1)S(1)} %get-tuple-element.25), channel_id=1, source_target_pairs={{0,0},{1,1},{2,2},{3,3},{4,4},{5,5},{6,6},{7,7},{8,8},{9,9},{10,10... | collective-permute-start | bytes 589832 | tf_op jit(solution)/shard_map/ppermute | solution.py:66
  144.6 10.1 %collective-permute-start.29 = (bf16[256,384]{1,0:T(8,128)(2,1)S(1)}, bf16[256,384]{1,0:T(8,128)(2,1)S(1)}, u32[]{:S(2)}, u32[]{:S(2)}) collective-permute-start(bf16[256,384]{1,0:T(8,128)(2,1)S(1)} %get-tuple-element.26), channel_id=1, source_target_pairs={{0,9},{1,8},{2,11},{3,10},{4,13},{5,12},{6,15},{7,14},{8,0},{9,1},... | collective-permute-start | bytes 589832 | tf_op jit(solution)/shard_map/ppermute | solution.py:66
  150.8 7.5 %collective-permute-start.30 = (bf16[256,384]{1,0:T(8,128)(2,1)S(1)}, bf16[256,384]{1,0:T(8,128)(2,1)S(1)}, u32[]{:S(2)}, u32[]{:S(2)}) collective-permute-start(bf16[256,384]{1,0:T(8,128)(2,1)S(1)} %get-tuple-element.27), channel_id=1, source_target_pairs={{0,1},{1,0},{2,3},{3,2},{4,5},{5,4},{6,7},{7,6},{8,9},{9,8},{10,11... | collective-permute-start | bytes 589832 | tf_op jit(solution)/shard_map/ppermute | solution.py:66
  150.9 9.5 %collective-permute-start.31 = (bf16[256,384]{1,0:T(8,128)(2,1)S(1)}, bf16[256,384]{1,0:T(8,128)(2,1)S(1)}, u32[]{:S(2)}, u32[]{:S(2)}) collective-permute-start(bf16[256,384]{1,0:T(8,128)(2,1)S(1)} %get-tuple-element.28), channel_id=1, source_target_pairs={{0,8},{1,9},{2,10},{3,11},{4,12},{5,13},{6,14},{7,15},{8,1},{9,0},... | collective-permute-start | bytes 589832 | tf_op jit(solution)/shard_map/ppermute | solution.py:66
  151.2 9.2 %collective-permute-start.32 = (bf16[256,384]{1,0:T(8,128)(2,1)S(1)}, bf16[256,384]{1,0:T(8,128)(2,1)S(1)}, u32[]{:S(2)}, u32[]{:S(2)}) collective-permute-start(bf16[256,384]{1,0:T(8,128)(2,1)S(1)} %collective-permute-done.28.refs_0_), channel_id=1, source_target_pairs={{0,64},{1,65},{2,66},{3,67},{4,68},{5,69},{6,70},{7,71},{8,72},{9,... | collective-permute-start | bytes 589832 | tf_op jit(solution)/shard_map/ppermute | solution.py:66
  154.7 5.7 %collective-permute-start.33 = (bf16[256,384]{1,0:T(8,128)(2,1)S(1)}, bf16[256,384]{1,0:T(8,128)(2,1)S(1)}, u32[]{:S(2)}, u32[]{:S(2)}) collective-permute-start(bf16[256,384]{1,0:T(8,128)(2,1)S(1)} %collective-permute-done.29.refs_1_), channel_id=1, source_target_pairs={{0,64},{1,65},{2,66},{3,67},{4,68},{5,69},{6,70},{7,71},{8,72},{9,... | collective-permute-start | bytes 589832 | tf_op jit(solution)/shard_map/ppermute | solution.py:66
  158.3 2.1 %collective-permute-start.34 = (bf16[256,384]{1,0:T(8,128)(2,1)S(1)}, bf16[256,384]{1,0:T(8,128)(2,1)S(1)}, u32[]{:S(2)}, u32[]{:S(2)}) collective-permute-start(bf16[256,384]{1,0:T(8,128)(2,1)S(1)} %collective-permute-done.30.refs_2_), channel_id=1, source_target_pairs={{0,64},{1,65},{2,66},{3,67},{4,68},{5,69},{6,70},{7,71},{8,72},{9,... | collective-permute-start | bytes 589832 | tf_op jit(solution)/shard_map/ppermute | solution.py:66
  160.4 1.4 collective-permute-start.35

commit v2 on v0

v2 whole, which is shorter than its diff:
```python
import functools
import math

import jax
import jax.numpy as jnp
from jax import lax
from jax.experimental import pallas as pl
from jax.experimental.pallas import tpu as pltpu
from jax.sharding import PartitionSpec as P


HD = 128
TILE = 256
AXES = ("grp", "ta", "ha", "wa")
FLIP = (0, 1, 1, 0)
HEADS = 3
ROWS = 144
LIMIT = 2.0**100
SCALE = HD**-0.5 * math.log2(math.e)
F32 = jnp.float32
BF16 = jnp.bfloat16


def flat(core, y, z, x):
    return ((core * 4 + y) * 2 + z % 2) * 8 + x * 2 + z // 2


def pairs(move):
    found = []
    for core in range(2):
        for y in range(4):
            for z in range(4):
                for x in range(4):
                    there = move(core, y, z, x)
                    if there is not None:
                        found.append((flat(core, y, z, x), flat(*there)))
    return sorted(found)


def out_to_heads(step):
    def move(core, y, z, x):
        half = y // 2
        return FLIP[y], (core if half == 0 else 3 - core), (z + step) % 4, x

    return pairs(move)


def back_to_tiles(step):
    return sorted((b, a) for a, b in out_to_heads(step))


def to_partner(core, y, z, x):
    return 1 - core, y, z, x


def to_outer(core, y, z, x):
    return (core, 3 - y, z, x) if core == 1 else None


def send(x, perm):
    return lax.ppermute(x, AXES, perm)


def turned(block):
    across = block.T
    return across[:, :HD], across[:, HD:]


def pack_body(place, *refs):
    ins, outs = refs[:12], refs[12:]
    for step in range(4):
        q_in, k_in, v_in = ins[3 * step : 3 * step + 3]
        kv_out, q_out = outs[2 * step : 2 * step + 2]
        for head in range(HEADS):
            cols = slice(head * HD, (head + 1) * HD)
            kv_out[head, 0] = k_in[:, cols]
            kv_out[head, 1, :HD], kv_out[head, 1, HD:] = turned(v_in[:, cols])
            q_out[head, :HD], q_out[head, HD:] = turned(q_in[:, cols])


def pack(place, q, k, v):
    specs, shapes, out_specs = [], [], []
    for step in range(4):
        spec = pl.BlockSpec((TILE, 3 * HD), lambda i, place, step=step: (0, (place[0] + step) % 4))
        specs += [spec] * 3
        for dims in ((HEADS, 2, TILE, HD), (HEADS, TILE, HD)):
            shapes.append(jax.ShapeDtypeStruct(dims, BF16))
            out_specs.append(pl.BlockSpec(dims, lambda i, place, r=len(dims): (0,) * r))
    flat_out = pl.pallas_call(
        pack_body,
        grid_spec=pltpu.PrefetchScalarGridSpec(
            num_scalar_prefetch=1, grid=(1,), in_specs=specs, out_specs=out_specs
        ),
        out_shape=shapes,
        name="pack",
    )(place, *([q, k, v] * 4))
    return flat_out[0::2], flat_out[1::2]


VMEM = pl.BlockSpec(memory_space=pltpu.MemorySpace.VMEM)
SMEM = pl.BlockSpec(memory_space=pltpu.MemorySpace.SMEM)


def local_call(body, place, operands, shapes, flops=0, limit=24, aliases=None):
    single = not isinstance(shapes, (list, tuple))
    listed = [shapes] if single else list(shapes)
    moved = sum(math.prod(a.shape) * a.dtype.itemsize for a in list(operands) + listed)
    return pl.pallas_call(
        body,
        in_specs=[SMEM] + [VMEM] * len(operands),
        out_specs=VMEM if single else [VMEM] * len(listed),
        out_shape=shapes,
        cost_estimate=pl.CostEstimate(flops=flops, bytes_accessed=moved, transcendentals=0),
        compiler_params=pltpu.CompilerParams(vmem_limit_bytes=limit * 1024 * 1024),
        input_output_aliases=aliases or {},
    )(place, *operands)


def gather_body(place, *refs):
    chunks, outs = refs[:4], refs[4:]
    for step in range(4):
        z_from = (place[0] - step + 4) % 4
        for high in range(2):

            @pl.when(z_from // 2 == high)
            def _():
                outs[high][:, z_from % 2] = chunks[step][...]


def gather(place, chunks):
    shape = jax.ShapeDtypeStruct((HEADS, 2, 2, TILE, HD), BF16)
    return local_call(gather_body, place, chunks, [shape] * 2)


MIXED = jax.ShapeDtypeStruct((HEADS, 2, ROWS, 2 * TILE), F32)
PEAK = jax.ShapeDtypeStruct((HEADS, 2, 1, 2 * TILE), F32)
TURNED = jax.ShapeDtypeStruct((HEADS, 4, 2 * HD, TILE), BF16)


def spread(place, q_in, turned_q):
    for step in range(4):
        z_from = (place[0] - step + 4) % 4
        for head in range(HEADS):
            both = jnp.concatenate([q_in[step][head, :HD], q_in[step][head, HD:]], axis=1)
            scaled = both.astype(F32) * SCALE
            high = scaled.astype(BF16)
            turned_q[head, z_from, :HD] = high
            turned_q[head, z_from, HD:] = (scaled - high.astype(F32)).astype(BF16)


def loaded(tiles):
    keys = jnp.concatenate([ref[head, low, 0] for ref, head, low in tiles], axis=0)
    values = jnp.concatenate(
        [
            ref[head, low, 1, half * HD : (half + 1) * HD]
            for ref, head, low in tiles
            for half in range(2)
        ],
        axis=1,
    )
    return keys, jnp.concatenate([values, jnp.ones((ROWS - HD, values.shape[1]), BF16)], axis=0)


def queries_of(turned_q, head, side):
    return jnp.concatenate([turned_q[head, 2 * side], turned_q[head, 2 * side + 1]], axis=1)


def scored(keys, queries):
    return jnp.dot(jnp.concatenate([keys, keys], axis=1), queries, preferred_element_type=F32)


def quick(queries, tiles, level, bias=None):
    keys, values = loaded(tiles)
    scores = scored(keys, queries) - (level if bias is None else level - bias)
    return jnp.dot(values, jnp.exp2(scores).astype(BF16), preferred_element_type=F32)


def careful(turned_q, mixed, peak, head, side, ref, bias=0.0):
    def one(low, carry):
        keys, values = loaded([(ref, head, low)])
        scores = scored(keys, queries_of(turned_q, head, side)) + bias
        before = peak[head, side]
        top = jnp.maximum(before, jnp.max(scores, axis=0, keepdims=True))
        probs = jnp.exp2(scores - top).astype(BF16)
        fresh = jnp.dot(values, probs, preferred_element_type=F32)
        mixed[head, side] = mixed[head, side] * jnp.exp2(before - top) + fresh
        peak[head, side] = top
        return carry

    lax.fori_loop(0, 2, one, 0)


def both_lows(head, *refs):
    return [(ref, head, low) for ref in refs for low in range(2)]


def within(sums):
    return jnp.max(sums) < LIMIT


def first_body(place, *refs):
    own, inner, q_in, (turned_q, mixed, peak) = refs[:2], refs[2:4], refs[4:8], refs[8:]
    spread(place, q_in, turned_q)

    def one(head, carry):
        fresh = []
        for side in range(2):
            queries = queries_of(turned_q, head, side)
            level = jnp.max(scored(own[0][head, 0, 0, :HD], queries), axis=0, keepdims=True)
            peak[head, side] = level
            fresh.append(
                quick(queries, both_lows(head, *own), level)
                + quick(queries, both_lows(head, *inner), level)
            )
        good = within(jnp.maximum(fresh[0][HD : HD + 1], fresh[1][HD : HD + 1]))

        @pl.when(good)
        def _():
            mixed[head, 0], mixed[head, 1] = fresh

        @pl.when(jnp.logical_not(good))
        def _():
            def redo(side, carry):
                mixed[head, side] = jnp.zeros((ROWS, 2 * TILE), F32)
                for ref in (*own, *inner):
                    careful(turned_q, mixed, peak, head, side, ref)
                return carry

            lax.fori_loop(0, 2, redo, 0)

        return carry

    lax.fori_loop(0, HEADS, one, 0)


def more(turned_q, mixed, peak, head, shares, biases=(None, None)):
    fresh = []
    for side in range(2):
        queries = queries_of(turned_q, head, side)
        fresh.append(
            mixed[head, side]
            + quick(queries, both_lows(head, *shares[side]), peak[head, side], biases[side])
        )
    good = within(jnp.maximum(fresh[0][HD : HD + 1], fresh[1][HD : HD + 1]))

    @pl.when(good)
    def _():
        mixed[head, 0], mixed[head, 1] = fresh

    @pl.when(jnp.logical_not(good))
    def _():
        for side in range(2):
            for ref in shares[side]:
                careful(
                    turned_q, mixed, peak, head, side, ref, 0.0 if biases[side] is None else biases[side]
                )


def edge_biases(place):
    return [jnp.where(place[2] == end, -1e30, 0.0).astype(F32) for end in (0, 3)]


def second_body(place, *refs):
    outer, (turned_q, _, _, mixed, peak) = refs[:2], refs[2:]

    @pl.when(place[1] == 1)
    def _():
        def one(head, carry):
            more(turned_q, mixed, peak, head, (outer, outer))
            return carry

        lax.fori_loop(0, HEADS, one, 0)


def third_body(place, *refs):
    left, right, (turned_q, _, _, mixed, peak) = refs[:2], refs[2:4], refs[4:]
    biases = edge_biases(place)

    def one(head, carry):
        more(turned_q, mixed, peak, head, (left, right), biases)
        return carry

    lax.fori_loop(0, HEADS, one, 0)


def last_body(place, *refs):
    left, right, turned_q, mixed_in, peak_in = refs[:5]
    outs, (done, mixed, peak) = refs[5:9], refs[9:]
    biases = edge_biases(place)
    mixed[...] = mixed_in[...]
    peak[...] = peak_in[...]

    @pl.when(place[1] == 1)
    def _():
        def one(head, carry):
            more(turned_q, mixed, peak, head, ((left,), (right,)), biases)
            return carry

        lax.fori_loop(0, HEADS, one, 0)

    def finish(head, carry):
        for side in range(2):
            total = mixed[head, side, HD : HD + 1]
            result = (mixed[head, side, :HD] / total).astype(BF16).T
            for low in range(2):
                done[2 * side + low, head] = result[low * TILE : (low + 1) * TILE]
        return carry

    lax.fori_loop(0, HEADS, finish, 0)

    for step in range(4):
        z_from = (place[0] - step + 4) % 4
        for head in range(HEADS):
            outs[step][:, head * HD : (head + 1) * HD] = done[z_from, head]


def last(place, operands, flops):
    out = jax.ShapeDtypeStruct((TILE, HEADS * HD), BF16)
    return pl.pallas_call(
        last_body,
        in_specs=[SMEM] + [VMEM] * len(operands),
        out_specs=[VMEM] * 4,
        out_shape=[out] * 4,
        scratch_shapes=[
            pltpu.VMEM((4, HEADS, TILE, HD), BF16),
            pltpu.VMEM(MIXED.shape, F32),
            pltpu.VMEM(PEAK.shape, F32),
        ],
        cost_estimate=pl.CostEstimate(flops=flops, bytes_accessed=1 << 20, transcendentals=0),
        compiler_params=pltpu.CompilerParams(vmem_limit_bytes=24 * 1024 * 1024),
        name="last",
    )(place, *operands)


def terms_body(mine, place, *refs):
    chunks, weight, out, joined = refs[:4], refs[4], refs[5], refs[6]
    width = out.shape[1]
    side = place[1] if mine else 1 - place[1]
    for step in range(4):
        slot = (place[0] + step) % 4
        for head in range(HEADS):
            joined[:, pl.ds(pl.multiple_of((slot * HEADS + head) * HD, HD), HD)] = chunks[step][
                :, head * HD : (head + 1) * HD
            ]
    cols = pl.ds(pl.multiple_of(side * width, width), width)
    out[...] = jnp.dot(joined[...], weight[:, cols], preferred_element_type=F32)


def terms(place, chunks, weight, mine):
    features = weight.shape[0]
    return pl.pallas_call(
        functools.partial(terms_body, mine),
        in_specs=[SMEM] + [VMEM] * 5,
        out_specs=VMEM,
        out_shape=jax.ShapeDtypeStruct((TILE, features), F32),
        scratch_shapes=[pltpu.VMEM((TILE, features), BF16)],
        cost_estimate=pl.CostEstimate(
            flops=2 * TILE * features * features, bytes_accessed=1 << 20, transcendentals=0
        ),
        compiler_params=pltpu.CompilerParams(vmem_limit_bytes=24 * 1024 * 1024),
        name="home" if mine else "away",
    )(place, *chunks, weight)


def close_body(place, here, arrived, gate, out):
    out[...] = (gate[...].astype(F32) * (here[...] + arrived[...])).astype(BF16)


def shards(query_tiles, key_tiles, value_tiles, out_weight, gate):
    features = query_tiles.shape[4]
    q, k, v = (a.reshape(TILE, features) for a in (query_tiles, key_tiles, value_tiles))
    core, y = lax.axis_index("grp"), lax.axis_index("ta")
    wide = lax.axis_index("wa")
    z, x = (wide % 2) * 2 + lax.axis_index("ha"), wide // 2
    place = jnp.stack([z, core, x, y]).astype(jnp.int32)
    partner, outer_pairs = pairs(to_partner), pairs(to_outer)
    to_right = pairs(lambda core, y, z, x: (core, y, z, x + 1) if x < 3 else None)
    to_left = pairs(lambda core, y, z, x: (core, y, z, x - 1) if x > 0 else None)
    flops_of = lambda tiles: HEADS * 4 * TILE * tiles * TILE * 6 * HD

    kv_sent, q_sent = pack(place, q, k, v)
    kv = [send(kv_sent[s], out_to_heads(s)) for s in range(4)]
    queries = [send(q_sent[s], out_to_heads(s)) for s in range(4)]
    own = gather(place, kv)
    outer = [send(own[i], outer_pairs) for i in range(2)]
    inner = [send(own[i], partner) for i in range(2)]
    right, left = send(own[0], to_left), send(own[1], to_right)
    state = local_call(
        first_body, place, [*own, *inner, *queries], [TURNED, MIXED, PEAK], flops_of(8)
    )
    turned_q, mixed, peak = state
    right_outer = send(outer[0], to_left)
    left_outer = send(outer[1], to_right)
    mixed, peak = local_call(
        second_body, place, [*outer, turned_q, mixed, peak], [MIXED, PEAK],
        flops_of(4), aliases={4: 0, 5: 1},
    )
    right_inner, left_inner = send(right, partner), send(left, partner)
    mixed, peak = local_call(
        third_body, place, [left, left_inner, right, right_inner, turned_q, mixed, peak],
        [MIXED, PEAK], flops_of(4), aliases={6: 0, 7: 1},
    )
    outs = last(place, [left_outer, right_outer, turned_q, mixed, peak], flops_of(1))
    chunks = [send(outs[s], back_to_tiles(s)) for s in range(4)]
    away = terms(place, chunks, out_weight, False)
    arrived = send(away, partner)
    here = terms(place, chunks, out_weight, True)
    branch = local_call(
        close_body, place, [here, arrived, gate.reshape(1, -1)],
        jax.ShapeDtypeStruct((TILE, features), BF16),
    )
    return branch.reshape(1, 1, 1, TILE, features)


def solution(mesh):
    spec = P("ta", "ha", "wa", None, "grp")

    return jax.shard_map(
        shards,
        mesh=mesh,
        in_specs=(spec, spec, spec, P("grp", None), P("grp")),
        out_specs=spec,
        check_vma=False,
    )
```

time: 1050 us -> 137 us (0.13)
  the two profiles are of different devices: /device:TPU:5 before, /device:TPU:3 now
where the time goes in v2:
time: 137 us; the launch traced here: 136 us
  Pallas kernels  54.2 us (40%)
  starting transfers between devices  45 us (33%)
  waiting for transfers between devices  36.2 us (26%)
    ppermute x23, starting transfers between devices, send(): return lax.ppermute(x, AXES, perm)  45 us
    pallas_call x5, Pallas kernels, local_call(): pl.pallas_call(body, in_specs=[SMEM] + [VMEM] * len(operands), out_specs=...  41.7 us
    ppermute x23, waiting for transfers between devices, send(): return lax.ppermute(x, AXES, perm)  36.2 us
    pallas_call x2, Pallas kernels, terms(): pl.pallas_call(functools.partial(terms_body, mine), in_specs=[SMEM] + [VM...  4.19 us
    pallas_call x1, Pallas kernels, pack(): pl.pallas_call(pack_body, grid_spec=pltpu.PrefetchScalarGridSpec(num_scal...  4.17 us
    pallas_call x1, Pallas kernels, last(): pl.pallas_call(last_body, in_specs=[SMEM] + [VMEM] * len(operands), out_s...  4.14 us
  transfers between devices with their start and end apart: 23, of which 11 were waited for; matrix products, arithmetic and copies ran while one was open for 0% of the time, Pallas kernels for 30%

profile of v2, /device:TPU:3, one launch (start us, length us, event | category | flops | bytes accessed | tf_op | source)
XLA Modules:
  0.0 136.3 jit_solution(4675356181816226089)
XLA Ops:
  0.0 0.6 pad_add_fusion.place
  0.6 4.2 %pack.1 = (bf16[3,2,256,128]{3,2,1,0:T(8,128)(2,1)}, bf16[3,256,128]{2,1,0:T(8,128)(2,1)}, bf16[3,2,256,128]{3,2,1,0:T(8,128)(2,1)}, bf16[3,256,128]{2,1,0:T(8,1...) custom-call(s32[4]{0:T(128)} %pad_add_fusion.place, ...), custom_call_target="tpu_custom_call" | custom-call | tf_op jit(solution)/shard_map/pack/pallas_call | solution.py:89
  4.8 3.8 %collective-permute-start = (bf16[3,2,256,128]{3,2,1,0:T(8,128)(2,1)}, bf16[3,2,256,128]{3,2,1,0:T(8,128)(2,1)S(1)}, u32[]{:S(2)}, u32[]{:S(2)}) collective-permute-start(bf16[3,2,256,128]{3,2,1,0:T(8,128)(2,1)} %get-tuple-element.26), channel_id=1, source_target_pairs={{0,0},{1,1},{2,2},{3,3},{4,4},{5,5},{6,6},{7,7},{8,8},{9,9},{10,10... | collective-permute-start | bytes 1179656 | tf_op jit(solution)/shard_map/ppermute | solution.py:61
  8.5 1.4 %collective-permute-start.1 = (bf16[3,2,256,128]{3,2,1,0:T(8,128)(2,1)}, bf16[3,2,256,128]{3,2,1,0:T(8,128)(2,1)S(1)}, u32[]{:S(2)}, u32[]{:S(2)}) collective-permute-start(bf16[3,2,256,128]{3,2,1,0:T(8,128)(2,1)} %get-tuple-element.27), channel_id=1, source_target_pairs={{0,8},{1,9},{2,10},{3,11},{4,12},{5,13},{6,14},{7,15},{8,1},{9,0},... | collective-permute-start | bytes 1179656 | tf_op jit(solution)/shard_map/ppermute | solution.py:61
  10.0 4.8 %collective-permute-start.2 = (bf16[3,2,256,128]{3,2,1,0:T(8,128)(2,1)}, bf16[3,2,256,128]{3,2,1,0:T(8,128)(2,1)S(1)}, u32[]{:S(2)}, u32[]{:S(2)}) collective-permute-start(bf16[3,2,256,128]{3,2,1,0:T(8,128)(2,1)} %get-tuple-element.28), channel_id=1, source_target_pairs={{0,1},{1,0},{2,3},{3,2},{4,5},{5,4},{6,7},{7,6},{8,9},{9,8},{10,11... | collective-permute-start | bytes 1179656 | tf_op jit(solution)/shard_map/ppermute | solution.py:61
  14.7 0.5 collective-permute-start.3
  15.2 0.0 collective-permute-done.refs_0_
  15.2 6.8 %collective-permute-done.1.refs_1_ = bf16[3,2,256,128]{3,2,1,0:T(8,128)(2,1)S(1)} collective-permute-done((bf16[3,2,256,128]{3,2,1,0:T(8,128)(2,1)}, bf16[3,2,256,128]{3,2,1,0:T(8,128)(2,1)S(1)}, u32[]{:S(2)}, u32[]{:S(2)}) %collective-permute-start.1) | collective-permute-done | bytes 393248 | tf_op jit(solution)/shard_map/ppermute | solution.py:61
  22.0 4.1 %collective-permute-done.2.refs_2_ = bf16[3,2,256,128]{3,2,1,0:T(8,128)(2,1)S(1)} collective-permute-done((bf16[3,2,256,128]{3,2,1,0:T(8,128)(2,1)}, bf16[3,2,256,128]{3,2,1,0:T(8,128)(2,1)S(1)}, u32[]{:S(2)}, u32[]{:S(2)}) %collective-permute-start.2) | collective-permute-done | bytes 393248 | tf_op jit(solution)/shard_map/ppermute | solution.py:61
  26.1 2.5 %collective-permute-done.3.refs_3_ = bf16[3,2,256,128]{3,2,1,0:T(8,128)(2,1)S(1)} collective-permute-done((bf16[3,2,256,128]{3,2,1,0:T(8,128)(2,1)}, bf16[3,2,256,128]{3,2,1,0:T(8,128)(2,1)S(1)}, u32[]{:S(2)}, u32[]{:S(2)}) %collective-permute-start.3) | collective-permute-done | bytes 393248 | tf_op jit(solution)/shard_map/ppermute | solution.py:61
  28.6 0.0 copy-done
  28.6 0.7 shard_map.55
  29.3 2.7 %collective-permute-start.8 = (bf16[3,2,2,256,128]{4,3,2,1,0:T(8,128)(2,1)S(1)}, bf16[3,2,2,256,128]{4,3,2,1,0:T(8,128)(2,1)S(1)}, u32[]{:S(2)}, u32[]{:S(2)}) collective-permute-start(bf16[3,2,2,256,128]{4,3,2,1,0:T(8,128)(2,1)S(1)} %get-tuple-element.31.refs_0_), channel_id=1, source_target_pairs={{0,64},{1,65},{2,66},{3,67},{4,68},{5,69},{6,70},{7,71},{8,72},{9,... | collective-permute-start | bytes 2359304 | tf_op jit(solution)/shard_map/ppermute | solution.py:61
  32.0 1.9 %collective-permute-start.10 = (bf16[3,256,128]{2,1,0:T(8,128)(2,1)}, bf16[3,256,128]{2,1,0:T(8,128)(2,1)S(1)}, u32[]{:S(2)}, u32[]{:S(2)}) collective-permute-start(bf16[3,256,128]{2,1,0:T(8,128)(2,1)} %get-tuple-element.32), channel_id=1, source_target_pairs={{0,0},{1,1},{2,2},{3,3},{4,4},{5,5},{6,6},{7,7},{8,8},{9,9},{10,10... | collective-permute-start | bytes 589832 | tf_op jit(solution)/shard_map/ppermute | solution.py:61
  33.9 2.7 %collective-permute-start.11 = (bf16[3,256,128]{2,1,0:T(8,128)(2,1)}, bf16[3,256,128]{2,1,0:T(8,128)(2,1)S(1)}, u32[]{:S(2)}, u32[]{:S(2)}) collective-permute-start(bf16[3,256,128]{2,1,0:T(8,128)(2,1)} %get-tuple-element.33), channel_id=1, source_target_pairs={{0,8},{1,9},{2,10},{3,11},{4,12},{5,13},{6,14},{7,15},{8,1},{9,0},... | collective-permute-start | bytes 589832 | tf_op jit(solution)/shard_map/ppermute | solution.py:61
  36.6 1.6 %collective-permute-start.12 = (bf16[3,256,128]{2,1,0:T(8,128)(2,1)}, bf16[3,256,128]{2,1,0:T(8,128)(2,1)S(1)}, u32[]{:S(2)}, u32[]{:S(2)}) collective-permute-start(bf16[3,256,128]{2,1,0:T(8,128)(2,1)} %get-tuple-element.34), channel_id=1, source_target_pairs={{0,1},{1,0},{2,3},{3,2},{4,5},{5,4},{6,7},{7,6},{8,9},{9,8},{10,11... | collective-permute-start | bytes 589832 | tf_op jit(solution)/shard_map/ppermute | solution.py:61
  38.2 2.8 %collective-permute-start.13 = (bf16[3,256,128]{2,1,0:T(8,128)(2,1)}, bf16[3,256,128]{2,1,0:T(8,128)(2,1)S(1)}, u32[]{:S(2)}, u32[]{:S(2)}) collective-permute-start(bf16[3,256,128]{2,1,0:T(8,128)(2,1)} %get-tuple-element.35), channel_id=1, source_target_pairs={{0,9},{1,8},{2,11},{3,10},{4,13},{5,12},{6,15},{7,14},{8,0},{9,1},... | collective-permute-start | bytes 589832 | tf_op jit(solution)/shard_map/ppermute | solution.py:61
  41.0 0.0 collective-permute-done.10.refs_4_
  41.0 3.1 %collective-permute-start.14 = (bf16[3,2,2,256,128]{4,3,2,1,0:T(8,128)(2,1)S(1)}, bf16[3,2,2,256,128]{4,3,2,1,0:T(8,128)(2,1)S(1)}, u32[]{:S(2)}, u32[]{:S(2)}) collective-permute-start(bf16[3,2,2,256,128]{4,3,2,1,0:T(8,128)(2,1)S(1)} %get-tuple-element.30.refs_1_), channel_id=1, source_target_pairs={{0,2},{1,3},{2,4},{3,5},{4,6},{5,7},{8,10},{9,11},{10,12},{11,13},... | collective-permute-start | bytes 2359304 | tf_op jit(solution)/shard_map/ppermute | solution.py:61
  44.1 0.0 collective-permute-done.11.refs_5_
  44.1 2.2 %collective-permute-start.16 = (bf16[3,2,2,256,128]{4,3,2,1,0:T(8,128)(2,1)S(1)}, bf16[3,2,2,256,128]{4,3,2,1,0:T(8,128)(2,1)S(1)}, u32[]{:S(2)}, u32[]{:S(2)}) collective-permute-start(bf16[3,2,2,256,128]{4,3,2,1,0:T(8,128)(2,1)S(1)} %get-tuple-element.31.refs_0_), channel_id=1, source_target_pairs={{2,0},{3,1},{4,2},{5,3},{6,4},{7,5},{10,8},{11,9},{12,10},{13,11},... | collective-permute-start | bytes 2359304 | tf_op jit(solution)/shard_map/ppermute | solution.py:61
  46.3 0.0 collective-permute-done.12.refs_6_
  46.3 4.6 %collective-permute-start.4 = (bf16[3,2,2,256,128]{4,3,2,1,0:T(8,128)(2,1)S(1)}, bf16[3,2,2,256,128]{4,3,2,1,0:T(8,128)(2,1)S(1)}, u32[]{:S(2)}, u32[]{:S(2)}) collective-permute-start(bf16[3,2,2,256,128]{4,3,2,1,0:T(8,128)(2,1)S(1)} %get-tuple-element.30.refs_1_), channel_id=1, source_target_pairs={{64,112},{65,113},{66,114},{67,115},{68,116},{69,117},{70,118},{71... | collective-permute-start | bytes 2359304 | tf_op jit(solution)/shard_map/ppermute | solution.py:61
  51.0 0.0 collective-permute-done.13.refs_7_
  51.0 1.9 %collective-permute-start.6 = (bf16[3,2,2,256,128]{4,3,2,1,0:T(8,128)(2,1)S(1)}, bf16[3,2,2,256,128]{4,3,2,1,0:T(8,128)(2,1)S(1)}, u32[]{:S(2)}, u32[]{:S(2)}) collective-permute-start(bf16[3,2,2,256,128]{4,3,2,1,0:T(8,128)(2,1)S(1)} %get-tuple-element.31.refs_0_), channel_id=1, source_target_pairs={{64,112},{65,113},{66,114},{67,115},{68,116},{69,117},{70,118},{71... | collective-permute-start | bytes 2359304 | tf_op jit(solution)/shard_map/ppermute | solution.py:61
  52.9 0.0 collective-permute-done.8.refs_2_
  52.9 0.1 collective-permute-start.9
  53.0 7.7 %collective-permute-done.14.refs_0_ = bf16[3,2,2,256,128]{4,3,2,1,0:T(8,128)(2,1)S(1)} collective-permute-done((bf16[3,2,2,256,128]{4,3,2,1,0:T(8,128)(2,1)S(1)}, bf16[3,2,2,256,128]{4,3,2,1,0:T(8,128)(2,1)S(1)}, u32[]{:S(2)}, u32[]{:S(2)}) %collective-permute-start.14) | collective-permute-done | bytes 786464 | tf_op jit(solution)/shard_map/ppermute | solution.py:61
  60.7 0.0 collective-permute-start.15
  60.7 3.1 %collective-permute-done.16.refs_2_ = bf16[3,2,2,256,128]{4,3,2,1,0:T(8,128)(2,1)S(1)} collective-permute-done((bf16[3,2,2,256,128]{4,3,2,1,0:T(8,128)(2,1)S(1)}, bf16[3,2,2,256,128]{4,3,2,1,0:T(8,128)(2,1)S(1)}, u32[]{:S(2)}, u32[]{:S(2)}) %collective-permute-start.16) | collective-permute-done | bytes 786464 | tf_op jit(solution)/shard_map/ppermute | solution.py:61
  63.8 0.0 collective-permute-start.17
  63.8 0.0 collective-permute-done.4.refs_1_
  63.8 2.8 %collective-permute-start.5 = (bf16[3,2,2,256,128]{4,3,2,1,0:T(8,128)(2,1)S(1)}, bf16[3,2,2,256,128]{4,3,2,1,0:T(8,128)(2,1)S(1)}, u32[]{:S(2)}, u32[]{:S(2)}) collective-permute-start(bf16[3,2,2,256,128]{4,3,2,1,0:T(8,128)(2,1)S(1)} %collective-permute-done.4.refs_1_), channel_id=1, source_target_pairs={{0,2},{1,3},{2,4},{3,5},{4,6},{5,7},{8,10},{9,11},{10,12},{11,13},... | collective-permute-start | bytes 2359304 | tf_op jit(solution)/shard_map/ppermute | solution.py:61
  66.6 2.1 %collective-permute-done.6.refs_0_ = bf16[3,2,2,256,128]{4,3,2,1,0:T(8,128)(2,1)S(1)} collective-permute-done((bf16[3,2,2,256,128]{4,3,2,1,0:T(8,128)(2,1)S(1)}, bf16[3,2,2,256,128]{4,3,2,1,0:T(8,128)(2,1)S(1)}, u32[]{:S(2)}, u32[]{:S(2)}) %collective-permute-start.6) | collective-permute-done | bytes 786464 | tf_op jit(solution)/shard_map/ppermute | solution.py:61
  68.8 1.9 %collective-permute-start.7 = (bf16[3,2,2,256,128]{4,3,2,1,0:T(8,128)(2,1)S(1)}, bf16[3,2,2,256,128]{4,3,2,1,0:T(8,128)(2,1)S(1)}, u32[]{:S(2)}, u32[]{:S(2)}) collective-permute-start(bf16[3,2,2,256,128]{4,3,2,1,0:T(8,128)(2,1)S(1)} %collective-permute-done.6.refs_0_), channel_id=1, source_target_pairs={{2,0},{3,1},{4,2},{5,3},{6,4},{7,5},{10,8},{11,9},{12,10},{13,11},... | collective-permute-start | bytes 2359304 | tf_op jit(solution)/shard_map/ppermute | solution.py:61
  70.7 0.0 collective-permute-done.9.refs_3_
  70.7 30.8 %shard_map.56 = (bf16[3,4,256,256]{3,2,1,0:T(8,128)(2,1)S(1)}, f32[3,2,144,512]{3,2,1,0:T(8,128)S(1)}, f32[3,2,1,512]{3,2,1,0:T(1,128)S(1)}) custom-call(s32[4]{0:T(128)S(1)} %copy-done, bf16[3,2,2,256,128]{4,3,2,1,0:T(8,128)(2,1)S(1)} %get-tuple-element.31.refs_0_, bf16[3,2,2,256,128]{4,3,2,1,0:T(8,128)(2,1)S(1)} %get-tuple-element.30.refs_1_, ...), custom_call_target="tpu_custom_call" | custom-call | flops 4831838208 | bytes 7286784 | tf_op jit(solution)/shard_map/pallas_call | solution.py:108
  101.5 0.0 slice-start
  101.5 0.0 slice-start.1
  101.5 4.4 %shard_map.57 = (f32[3,2,144,512]{3,2,1,0:T(8,128)S(1)}, f32[3,2,1,512]{3,2,1,0:T(1,128)S(1)}) custom-call(s32[4]{0:T(128)S(1)} %copy-done, bf16[3,2,2,256,128]{4,3,2,1,0:T(8,128)(2,1)S(1)} %collective-permute-done.6.refs_0_, bf16[3,2,2,256,128]{4,3,2,1,0:T(8,128)(2,1)S(1)} %collective-permute-done.4.refs_1_, ...), custom_call_target="tpu_custom_call", output_to_operand_aliasing={{0}: (4, {}), {1}: (5, {})} | custom-call | flops 2415919104 | bytes 6709248 | tf_op jit(solution)/shard_map/pallas_call | solution.py:108
  105.9 0.0 collective-permute-done.15.refs_1_
  105.9 0.0 collective-permute-done.17.refs_3_
  105.9 0.0 slice-start.2
  105.9 4.2 %shard_map.58 = (f32[3,2,144,512]{3,2,1,0:T(8,128)S(1)}, f32[3,2,1,512]{3,2,1,0:T(1,128)S(1)}) custom-call(s32[4]{0:T(128)S(1)} %copy-done, bf16[3,2,2,256,128]{4,3,2,1,0:T(8,128)(2,1)S(1)} %collective-permute-done.14.refs_0_, bf16[3,2,2,256,128]{4,3,2,1,0:T(8,128)(2,1)S(1)} %collective-permute-done.15.refs_1_, ...), custom_call_target="tpu_custom_call", output_to_operand_aliasing={{0}: (6, {}), {1}: (7, {})} | custom-call | flops 2415919104 | bytes 8282112 | tf_op jit(solution)/shard_map/pallas_call | solution.py:108
  110.1 0.0 collective-permute-done.5.refs_0_
  110.1 0.0 collective-permute-done.7.refs_1_
  110.2 4.1 %last.1 = (bf16[256,384]{1,0:T(8,128)(2,1)S(1)}, bf16[256,384]{1,0:T(8,128)(2,1)S(1)}, bf16[256,384]{1,0:T(8,128)(2,1)S(1)}, bf16[256,384]{1,0:T(8,128)(2,1)S(1)}) custom-call(s32[4]{0:T(128)S(1)} %copy-done, bf16[3,2,2,256,128]{4,3,2,1,0:T(8,128)(2,1)S(1)} %collective-permute-done.5.refs_0_, ...), custom_call_target="tpu_custom_call" | custom-call | flops 603979776 | bytes 1048576 | tf_op jit(solution)/shard_map/last/pallas_call | solution.py:319
  114.3 1.9 %collective-permute-start.18 = (bf16[256,384]{1,0:T(8,128)(2,1)S(1)}, bf16[256,384]{1,0:T(8,128)(2,1)S(1)}, u32[]{:S(2)}, u32[]{:S(2)}) collective-permute-start(bf16[256,384]{1,0:T(8,128)(2,1)S(1)} %get-tuple-element.43), channel_id=1, source_target_pairs={{0,0},{1,1},{2,2},{3,3},{4,4},{5,5},{6,6},{7,7},{8,8},{9,9},{10,10... | collective-permute-start | bytes 589832 | tf_op jit(solution)/shard_map/ppermute | solution.py:61
  116.2 3.3 %collective-permute-start.19 = (bf16[256,384]{1,0:T(8,128)(2,1)S(1)}, bf16[256,384]{1,0:T(8,128)(2,1)S(1)}, u32[]{:S(2)}, u32[]{:S(2)}) collective-permute-start(bf16[256,384]{1,0:T(8,128)(2,1)S(1)} %get-tuple-element.44), channel_id=1, source_target_pairs={{0,9},{1,8},{2,11},{3,10},{4,13},{5,12},{6,15},{7,14},{8,0},{9,1},... | collective-permute-start | bytes 589832 | tf_op jit(solution)/shard_map/ppermute | solution.py:61
  119.5 0.8 collective-permute-start.20
  120.3 0.3 collective-permute-start.21
  120.5 0.8 collective-permute-done.18.refs_0_
  121.3 2.8 %collective-permute-done.19.refs_1_ = bf16[256,384]{1,0:T(8,128)(2,1)S(1)} collective-permute-done((bf16[256,384]{1,0:T(8,128)(2,1)S(1)}, bf16[256,384]{1,0:T(8,128)(2,1)S(1)}, u32[]{:S(2)}, u32[]{:S(2)}) %collective-permute-start.19) | collective-permute-done | bytes 196640 | tf_op jit(solution)/shard_map/ppermute | solution.py:61
  124.1 2.9 %collective-permute-done.20.refs_2_ = bf16[256,384]{1,0:T(8,128)(2,1)S(1)} collective-permute-done((bf16[256,384]{1,0:T(8,128)(2,1)S(1)}, bf16[256,384]{1,0:T(8,128)(2,1)S(1)}, u32[]{:S(2)}, u32[]{:S(2)}) %collective-permute-start.20) | collective-permute-done | bytes 196640 | tf_op jit(solution)/shard_map/ppermute | solution.py:61
  127.0 2.1 %collective-permute-done.21.refs_3_ = bf16[256,384]{1,0:T(8,128)(2,1)S(1)} collective-permute-done((bf16[256,384]{1,0:T(8,128)(2,1)S(1)}, bf16[256,384]{1,0:T(8,128)(2,1)S(1)}, u32[]{:S(2)}, u32[]{:S(2)}) %collective-permute-start.21) | collective-permute-done | bytes 196640 | tf_op jit(solution)/shard_map/ppermute | solution.py:61
  129.1 0.0 slice-done
  129.1 0.0 slice-done.1
  129.1 0.0 slice-done.2
  129.1 2.1 %away.1 = f32[256,1536]{1,0:T(8,128)S(1)} custom-call(s32[4]{0:T(128)S(1)} %copy-done, bf16[256,384]{1,0:T(8,128)(2,1)S(1)} %collective-permute-done.18.refs_0_, bf16[256,384]{1,0:T(8,128)(2,1)S(1)} %collective-permute-done.19.refs_1_, bf16[256,384]{1,0:T(8,128)(2,1)S(1)} %collective-permute-done.20.refs_2_, ...), custom_call_target="tpu_custom_call" | custom-call | flops 1207959552 | bytes 1048576 | tf_op jit(solution)/shard_map/away/pallas_call | solution.py:351
  131.2 0.1 collective-permute-start.22
  131.3 0.0 copy-done.1
  131.4 2.1 %home.1.here = f32[256,1536]{1,0:T(8,128)S(1)} custom-call(s32[4]{0:T(128)S(1)} %copy-done, bf16[256,384]{1,0:T(8,128)(2,1)S(1)} %collective-permute-done.18.refs_0_, bf16[256,384]{1,0:T(8,128)(2,1)S(1)} %collective-permute-done.19.refs_1_, bf16[256,384]{1,0:T(8,128)(2,1)S(1)} %collective-permute-done.20.refs_2_, ...), custom_call_target="tpu_custom_call" | custom-call | flops 1207959552 | bytes 1048576 | tf_op jit(solution)/shard_map/home/pallas_call | solution.py:351
  133.5 1.3 collective-permute-done.22.arrived
  134.7 1.6 %shard_map.59 = bf16[256,1536]{1,0:T(8,128)(2,1)} custom-call(s32[4]{0:T(128)S(1)} %copy-done, f32[256,1536]{1,0:T(8,128)S(1)} %home.1.here, f32[256,1536]{1,0:T(8,128)S(1)} %collective-permute-done.22.arrived, bf16[1,1536]{1,0:T(2,128)(2,1)S(1)} %reshape.18.gate), custom_call_target="tpu_custom_call" | custom-call | bytes 3935232 | tf_op jit(solution)/shard_map/pallas_call | solution.py:108
  (4 shorter events, 0.0 us)
Async XLA Ops:
  0.6 28.0 %copy-start = (s32[4]{0:T(128)S(1)}, s32[4]{0:T(128)}, u32[]{:S(2)}) copy-start(s32[4]{0:T(128)} %pad_add_fusion.place) | copy-start | bytes 52
  4.8 10.4 %collective-permute-start = (bf16[3,2,256,128]{3,2,1,0:T(8,128)(2,1)}, bf16[3,2,256,128]{3,2,1,0:T(8,128)(2,1)S(1)}, u32[]{:S(2)}, u32[]{:S(2)}) collective-permute-start(bf16[3,2,256,128]{3,2,1,0:T(8,128)(2,1)} %get-tuple-element.26), channel_id=1, source_target_pairs={{0,0},{1,1},{2,2},{3,3},{4,4},{5,5},{6,6},{7,7},{8,8},{9,9},{10,10... | collective-permute-start | bytes 1179656 | tf_op jit(solution)/shard_map/ppermute | solution.py:61
  8.5 13.4 %collective-permute-start.1 = (bf16[3,2,256,128]{3,2,1,0:T(8,128)(2,1)}, bf16[3,2,256,128]{3,2,1,0:T(8,128)(2,1)S(1)}, u32[]{:S(2)}, u32[]{:S(2)}) collective-permute-start(bf16[3,2,256,128]{3,2,1,0:T(8,128)(2,1)} %get-tuple-element.27), channel_id=1, source_target_pairs={{0,8},{1,9},{2,10},{3,11},{4,12},{5,13},{6,14},{7,15},{8,1},{9,0},... | collective-permute-start | bytes 1179656 | tf_op jit(solution)/shard_map/ppermute | solution.py:61
  10.0 16.1 %collective-permute-start.2 = (bf16[3,2,256,128]{3,2,1,0:T(8,128)(2,1)}, bf16[3,2,256,128]{3,2,1,0:T(8,128)(2,1)S(1)}, u32[]{:S(2)}, u32[]{:S(2)}) collective-permute-start(bf16[3,2,256,128]{3,2,1,0:T(8,128)(2,1)} %get-tuple-element.28), channel_id=1, source_target_pairs={{0,1},{1,0},{2,3},{3,2},{4,5},{5,4},{6,7},{7,6},{8,9},{9,8},{10,11... | collective-permute-start | bytes 1179656 | tf_op jit(solution)/shard_map/ppermute | solution.py:61
  14.7 13.9 %collective-permute-start.3 = (bf16[3,2,256,128]{3,2,1,0:T(8,128)(2,1)}, bf16[3,2,256,128]{3,2,1,0:T(8,128)(2,1)S(1)}, u32[]{:S(2)}, u32[]{:S(2)}) collective-permute-start(bf16[3,2,256,128]{3,2,1,0:T(8,128)(2,1)} %get-tuple-element.29), channel_id=1, source_target_pairs={{0,9},{1,8},{2,11},{3,10},{4,13},{5,12},{6,15},{7,14},{8,0},{9,1},... | collective-permute-start | bytes 1179656 | tf_op jit(solution)/shard_map/ppermute | solution.py:61
  29.3 23.6 %collective-permute-start.8 = (bf16[3,2,2,256,128]{4,3,2,1,0:T(8,128)(2,1)S(1)}, bf16[3,2,2,256,128]{4,3,2,1,0:T(8,128)(2,1)S(1)}, u32[]{:S(2)}, u32[]{:S(2)}) collective-permute-start(bf16[3,2,2,256,128]{4,3,2,1,0:T(8,128)(2,1)S(1)} %get-tuple-element.31.refs_0_), channel_id=1, source_target_pairs={{0,64},{1,65},{2,66},{3,67},{4,68},{5,69},{6,70},{7,71},{8,72},{9,... | collective-permute-start | bytes 2359304 | tf_op jit(solution)/shard_map/ppermute | solution.py:61
  32.0 8.9 %collective-permute-start.10 = (bf16[3,256,128]{2,1,0:T(8,128)(2,1)}, bf16[3,256,128]{2,1,0:T(8,128)(2,1)S(1)}, u32[]{:S(2)}, u32[]{:S(2)}) collective-permute-start(bf16[3,256,128]{2,1,0:T(8,128)(2,1)} %get-tuple-element.32), channel_id=1, source_target_pairs={{0,0},{1,1},{2,2},{3,3},{4,4},{5,5},{6,6},{7,7},{8,8},{9,9},{10,10... | collective-permute-start | bytes 589832 | tf_op jit(solution)/shard_map/ppermute | solution.py:61
  33.9 10.1 %collective-permute-start.11 = (bf16[3,256,128]{2,1,0:T(8,128)(2,1)}, bf16[3,256,128]{2,1,0:T(8,128)(2,1)S(1)}, u32[]{:S(2)}, u32[]{:S(2)}) collective-permute-start(bf16[3,256,128]{2,1,0:T(8,128)(2,1)} %get-tuple-element.33), channel_id=1, source_target_pairs={{0,8},{1,9},{2,10},{3,11},{4,12},{5,13},{6,14},{7,15},{8,1},{9,0},... | collective-permute-start | bytes 589832 | tf_op jit(solution)/shard_map/ppermute | solution.py:61
  36.6 9.7 %collective-permute-start.12 = (bf16[3,256,128]{2,1,0:T(8,128)(2,1)}, bf16[3,256,128]{2,1,0:T(8,128)(2,1)S(1)}, u32[]{:S(2)}, u32[]{:S(2)}) collective-permute-start(bf16[3,256,128]{2,1,0:T(8,128)(2,1)} %get-tuple-element.34), channel_id=1, source_target_pairs={{0,1},{1,0},{2,3},{3,2},{4,5},{5,4},{6,7},{7,6},{8,9},{9,8},{10,11... | collective-permute-start | bytes 589832 | tf_op jit(solution)/shard_map/ppermute | solution.py:61
  38.2 12.8 %collective-permute-start.13 = (bf16[3,256,128]{2,1,0:T(8,128)(2,1)}, bf16[3,256,128]{2,1,0:T(8,128)(2,1)S(1)}, u32[]{:S(2)}, u32[]{:S(2)}) collective-permute-start(bf16[3,256,128]{2,1,0:T(8,128)(2,1)} %get-tuple-element.35), channel_id=1, source_target_pairs={{0,9},{1,8},{2,11},{3,10},{4,13},{5,12},{6,15},{7,14},{8,0},{9,1},... | collective-permute-start | bytes 589832 | tf_op jit(solution)/shard_map/ppermute | solution.py:61
  41.0 19.7 %collective-permute-start.14 = (bf16[3,2,2,256,128]{4,3,2,1,0:T(8,128)(2,1)S(1)}, bf16[3,2,2,256,128]{4,3,2,1,0:T(8,128)(2,1)S(1)}, u32[]{:S(2)}, u32[]{:S(2)}) collective-permute-start(bf16[3,2,2,256,128]{4,3,2,1,0:T(8,128)(2,1)S(1)} %get-tuple-element.30.refs_1_), channel_id=1, source_target_pairs={{0,2},{1,3},{2,4},{3,5},{4,6},{5,7},{8,10},{9,11},{10,12},{11,13},... | collective-permute-start | bytes 2359304 | tf_op jit(solution)/shard_map/ppermute | solution.py:61
  44.1 19.7 %collective-permute-start.16 = (bf16[3,2,2,256,128]{4,3,2,1,0:T(8,128)(2,1)S(1)}, bf16[3,2,2,256,128]{4,3,2,1,0:T(8,128)(2,1)S(1)}, u32[]{:S(2)}, u32[]{:S(2)}) collective-permute-start(bf16[3,2,2,256,128]{4,3,2,1,0:T(8,128)(2,1)S(1)} %get-tuple-element.31.refs_0_), channel_id=1, source_target_pairs={{2,0},{3,1},{4,2},{5,3},{6,4},{7,5},{10,8},{11,9},{12,10},{13,11},... | collective-permute-start | bytes 2359304 | tf_op jit(solution)/shard_map/ppermute | solution.py:61
  46.3 17.5 %collective-permute-start.4 = (bf16[3,2,2,256,128]{4,3,2,1,0:T(8,128)(2,1)S(1)}, bf16[3,2,2,256,128]{4,3,2,1,0:T(8,128)(2,1)S(1)}, u32[]{:S(2)}, u32[]{:S(2)}) collective-permute-start(bf16[3,2,2,256,128]{4,3,2,1,0:T(8,128)(2,1)S(1)} %get-tuple-element.30.refs_1_), channel_id=1, source_target_pairs={{64,112},{65,113},{66,114},{67,115},{68,116},{69,117},{70,118},{71... | collective-permute-start | bytes 2359304 | tf_op jit(solution)/shard_map/ppermute | solution.py:61
  51.0 17.8 %collective-permute-start.6 = (bf16[3,2,2,256,128]{4,3,2,1,0:T(8,128)(2,1)S(1)}, bf16[3,2,2,256,128]{4,3,2,1,0:T(8,128)(2,1)S(1)}, u32[]{:S(2)}, u32[]{:S(2)}) collective-permute-start(bf16[3,2,2,256,128]{4,3,2,1,0:T(8,128)(2,1)S(1)} %get-tuple-element.31.refs_0_), channel_id=1, source_target_pairs={{64,112},{65,113},{66,114},{67,115},{68,116},{69,117},{70,118},{71... | collective-permute-start | bytes 2359304 | tf_op jit(solution)/shard_map/ppermute | solution.py:61
  52.9 17.8 %collective-permute-start.9 = (bf16[3,2,2,256,128]{4,3,2,1,0:T(8,128)(2,1)S(1)}, bf16[3,2,2,256,128]{4,3,2,1,0:T(8,128)(2,1)S(1)}, u32[]{:S(2)}, u32[]{:S(2)}) collective-permute-start(bf16[3,2,2,256,128]{4,3,2,1,0:T(8,128)(2,1)S(1)} %get-tuple-element.30.refs_1_), channel_id=1, source_target_pairs={{0,64},{1,65},{2,66},{3,67},{4,68},{5,69},{6,70},{7,71},{8,72},{9,... | collective-permute-start | bytes 2359304 | tf_op jit(solution)/shard_map/ppermute | solution.py:61
  60.7 45.2 %collective-permute-start.15 = (bf16[3,2,2,256,128]{4,3,2,1,0:T(8,128)(2,1)S(1)}, bf16[3,2,2,256,128]{4,3,2,1,0:T(8,128)(2,1)S(1)}, u32[]{:S(2)}, u32[]{:S(2)}) collective-permute-start(bf16[3,2,2,256,128]{4,3,2,1,0:T(8,128)(2,1)S(1)} %collective-permute-done.14.refs_0_), channel_id=1, source_target_pairs={{0,64},{1,65},{2,66},{3,67},{4,68},{5,69},{6,70},{7,71},{8,72},{9,... | collective-permute-start | bytes 2359304 | tf_op jit(solution)/shard_map/ppermute | solution.py:61
  63.8 42.1 %collective-permute-start.17 = (bf16[3,2,2,256,128]{4,3,2,1,0:T(8,128)(2,1)S(1)}, bf16[3,2,2,256,128]{4,3,2,1,0:T(8,128)(2,1)S(1)}, u32[]{:S(2)}, u32[]{:S(2)}) collective-permute-start(bf16[3,2,2,256,128]{4,3,2,1,0:T(8,128)(2,1)S(1)} %collective-permute-done.16.refs_2_), channel_id=1, source_target_pairs={{0,64},{1,65},{2,66},{3,67},{4,68},{5,69},{6,70},{7,71},{8,72},{9,... | collective-permute-start | bytes 2359304 | tf_op jit(solution)/shard_map/ppermute | solution.py:61
  63.8 46.3 %collective-permute-start.5 = (bf16[3,2,2,256,128]{4,3,2,1,0:T(8,128)(2,1)S(1)}, bf16[3,2,2,256,128]{4,3,2,1,0:T(8,128)(2,1)S(1)}, u32[]{:S(2)}, u32[]{:S(2)}) collective-permute-start(bf16[3,2,2,256,128]{4,3,2,1,0:T(8,128)(2,1)S(1)} %collective-permute-done.4.refs_1_), channel_id=1, source_target_pairs={{0,2},{1,3},{2,4},{3,5},{4,6},{5,7},{8,10},{9,11},{10,12},{11,13},... | collective-permute-start | bytes 2359304 | tf_op jit(solution)/shard_map/ppermute | solution.py:61
  68.8 41.4 %collective-permute-start.7 = (bf16[3,2,2,256,128]{4,3,2,1,0:T(8,128)(2,1)S(1)}, bf16[3,2,2,256,128]{4,3,2,1,0:T(8,128)(2,1)S(1)}, u32[]{:S(2)}, u32[]{:S(2)}) collective-permute-start(bf16[3,2,2,256,128]{4,3,2,1,0:T(8,128)(2,1)S(1)} %collective-permute-done.6.refs_0_), channel_id=1, source_target_pairs={{2,0},{3,1},{4,2},{5,3},{6,4},{7,5},{10,8},{11,9},{12,10},{13,11},... | collective-permute-start | bytes 2359304 | tf_op jit(solution)/shard_map/ppermute | solution.py:61
  101.5 27.6 %slice-start = ((s8[9437184]{0:T(1024)(128)(4,1)}), s8[4194304]{0:T(1024)(128)(4,1)S(1)}, s32[]{:S(2)}) async-start(s8[9437184]{0:T(1024)(128)(4,1)} %bitcast.8), calls=%async_computation | async-start | bytes 8388608
  101.5 27.6 %slice-start.1 = ((s8[9437184]{0:T(1024)(128)(4,1)}), s8[4194304]{0:T(1024)(128)(4,1)S(1)}, s32[]{:S(2)}) async-start(s8[9437184]{0:T(1024)(128)(4,1)} %bitcast.8), calls=%async_computation.1 | async-start | bytes 8388608
  105.9 23.2 %slice-start.2 = ((s8[9437184]{0:T(1024)(128)(4,1)}), s8[1048576]{0:T(1024)(128)(4,1)S(1)}, s32[]{:S(2)}) async-start(s8[9437184]{0:T(1024)(128)(4,1)} %bitcast.8), calls=%async_computation.2 | async-start | bytes 2097152
  114.3 7.0 %collective-permute-start.18 = (bf16[256,384]{1,0:T(8,128)(2,1)S(1)}, bf16[256,384]{1,0:T(8,128)(2,1)S(1)}, u32[]{:S(2)}, u32[]{:S(2)}) collective-permute-start(bf16[256,384]{1,0:T(8,128)(2,1)S(1)} %get-tuple-element.43), channel_id=1, source_target_pairs={{0,0},{1,1},{2,2},{3,3},{4,4},{5,5},{6,6},{7,7},{8,8},{9,9},{10,10... | collective-permute-start | bytes 589832 | tf_op jit(solution)/shard_map/ppermute | solution.py:61
  116.2 7.9 %collective-permute-start.19 = (bf16[256,384]{1,0:T(8,128)(2,1)S(1)}, bf16[256,384]{1,0:T(8,128)(2,1)S(1)}, u32[]{:S(2)}, u32[]{:S(2)}) collective-permute-start(bf16[256,384]{1,0:T(8,128)(2,1)S(1)} %get-tuple-element.44), channel_id=1, source_target_pairs={{0,9},{1,8},{2,11},{3,10},{4,13},{5,12},{6,15},{7,14},{8,0},{9,1},... | collective-permute-start | bytes 589832 | tf_op jit(solution)/shard_map/ppermute | solution.py:61
  119.5 7.5 %collective-permute-start.20 = (bf16[256,384]{1,0:T(8,128)(2,1)S(1)}, bf16[256,384]{1,0:T(8,128)(2,1)S(1)}, u32[]{:S(2)}, u32[]{:S(2)}) collective-permute-start(bf16[256,384]{1,0:T(8,128)(2,1)S(1)} %get-tuple-element.45), channel_id=1, source_target_pairs={{0,1},{1,0},{2,3},{3,2},{4,5},{5,4},{6,7},{7,6},{8,9},{9,8},{10,11... | collective-permute-start | bytes 589832 | tf_op jit(solution)/shard_map/ppermute | solution.py:61
  120.3 11.1 %copy-start.1 = (bf16[1536]{0:T(1024)(128)(2,1)S(1)}, bf16[1536]{0:T(1024)(128)(2,1)}, u32[]{:S(2)}) copy-start(bf16[1536]{0:T(1024)(128)(2,1)} %param.9) | copy-start | bytes 9220
  120.3 8.9 %collective-permute-start.21 = (bf16[256,384]{1,0:T(8,128)(2,1)S(1)}, bf16[256,384]{1,0:T(8,128)(2,1)S(1)}, u32[]{:S(2)}, u32[]{:S(2)}) collective-permute-start(bf16[256,384]{1,0:T(8,128)(2,1)S(1)} %get-tuple-element.46), channel_id=1, source_target_pairs={{0,8},{1,9},{2,10},{3,11},{4,12},{5,13},{6,14},{7,15},{8,1},{9,0},... | collective-permute-start | bytes 589832 | tf_op jit(solution)/shard_map/ppermute | solution.py:61
  131.2 3.5 %collective-permute-start.22 = (f32[256,1536]{1,0:T(8,128)S(1)}, f32[256,1536]{1,0:T(8,128)S(1)}, u32[]{:S(2)}, u32[]{:S(2)}) collective-permute-start(f32[256,1536]{1,0:T(8,128)S(1)} %away.1), channel_id=1, source_target_pairs={{0,64},{1,65},{2,66},{3,67},{4,68},{5,69},{6,70},{7,71},{8,72},{9,... | collective-permute-start | bytes 4718600 | tf_op jit(solution)/shard_map/ppermute | solution.py:61

commit v3 on v2

v3 whole, which is shorter than its diff:
```python
import math

import jax
import jax.numpy as jnp
from jax import lax
from jax.experimental import pallas as pl
from jax.experimental.pallas import tpu as pltpu
from jax.sharding import PartitionSpec as P


HD = 128
TILE = 256
AXES = ("grp", "ta", "ha", "wa")
FLIP = (0, 1, 1, 0)
HEADS = 3
ROWS = 144
LIMIT = 2.0**100
SCALE = HD**-0.5 * math.log2(math.e)
F32 = jnp.float32
BF16 = jnp.bfloat16


def flat(core, y, z, x):
    return ((core * 4 + y) * 2 + z % 2) * 8 + x * 2 + z // 2


def pairs(move):
    found = []
    for core in range(2):
        for y in range(4):
            for z in range(4):
                for x in range(4):
                    there = move(core, y, z, x)
                    if there is not None:
                        found.append((flat(core, y, z, x), flat(*there)))
    return sorted(found)


def out_to_heads(step):
    def move(core, y, z, x):
        half = y // 2
        return FLIP[y], (core if half == 0 else 3 - core), (z + step) % 4, x

    return pairs(move)


def back_to_tiles(step):
    return sorted((b, a) for a, b in out_to_heads(step))


def to_partner(core, y, z, x):
    return 1 - core, y, z, x


def to_outer(core, y, z, x):
    return (core, 3 - y, z, x) if core == 1 else None


def send(x, perm):
    return lax.ppermute(x, AXES, perm)


def turned(block):
    across = block.T
    return across[:, :HD], across[:, HD:]


def slot_cols(place, step, head):
    at = ((place[0] + step) % 4) * HEADS + head
    return pl.ds(pl.multiple_of(at * HD, HD), HD)


def pack_body(place, k_in, v_in, *outs):
    for step in range(4):
        for head in range(HEADS):
            cols = slot_cols(place, step, head)
            outs[step][head, 0] = k_in[:, cols]
            outs[step][head, 1, :HD], outs[step][head, 1, HD:] = turned(v_in[:, cols])


def pack_q_body(place, q_in, *outs):
    for step in range(4):
        for head in range(HEADS):
            outs[step][head, :HD], outs[step][head, HD:] = turned(
                q_in[:, slot_cols(place, step, head)]
            )


VMEM = pl.BlockSpec(memory_space=pltpu.MemorySpace.VMEM)
SMEM = pl.BlockSpec(memory_space=pltpu.MemorySpace.SMEM)


def local_call(body, place, operands, shapes, flops=0, limit=24, aliases=None):
    single = not isinstance(shapes, (list, tuple))
    listed = [shapes] if single else list(shapes)
    moved = sum(math.prod(a.shape) * a.dtype.itemsize for a in list(operands) + listed)
    return pl.pallas_call(
        body,
        in_specs=[SMEM] + [VMEM] * len(operands),
        out_specs=VMEM if single else [VMEM] * len(listed),
        out_shape=shapes,
        cost_estimate=pl.CostEstimate(flops=flops, bytes_accessed=moved, transcendentals=0),
        compiler_params=pltpu.CompilerParams(vmem_limit_bytes=limit * 1024 * 1024),
        input_output_aliases=aliases or {},
    )(place, *operands)


def gather_body(place, *refs):
    chunks, halves, whole = refs[:4], refs[4:6], refs[6]
    for step in range(4):
        z_from = (place[0] - step + 4) % 4
        whole[z_from // 2, :, z_from % 2] = chunks[step][...]
        for high in range(2):

            @pl.when(z_from // 2 == high)
            def _():
                halves[high][:, z_from % 2] = chunks[step][...]


MIXED = jax.ShapeDtypeStruct((HEADS, 2, ROWS, 2 * TILE), F32)
PEAK = jax.ShapeDtypeStruct((HEADS, 2, 1, 2 * TILE), F32)
TURNED = jax.ShapeDtypeStruct((HEADS, 4, 2 * HD, TILE), BF16)


def spread(place, q_in, turned_q):
    for step in range(4):
        z_from = (place[0] - step + 4) % 4
        for head in range(HEADS):
            both = jnp.concatenate([q_in[step][head, :HD], q_in[step][head, HD:]], axis=1)
            scaled = both.astype(F32) * SCALE
            high = scaled.astype(BF16)
            turned_q[head, z_from, :HD] = high
            turned_q[head, z_from, HD:] = (scaled - high.astype(F32)).astype(BF16)


def loaded(tiles):
    keys = jnp.concatenate([ref[head, low, 0] for ref, head, low in tiles], axis=0)
    values = jnp.concatenate(
        [
            ref[head, low, 1, half * HD : (half + 1) * HD]
            for ref, head, low in tiles
            for half in range(2)
        ],
        axis=1,
    )
    return keys, jnp.concatenate([values, jnp.ones((ROWS - HD, values.shape[1]), BF16)], axis=0)


def queries_of(turned_q, head, side):
    return jnp.concatenate([turned_q[head, 2 * side], turned_q[head, 2 * side + 1]], axis=1)


def scored(keys, queries):
    return jnp.dot(jnp.concatenate([keys, keys], axis=1), queries, preferred_element_type=F32)


def quick(queries, tiles, level, bias=None):
    keys, values = loaded(tiles)
    scores = scored(keys, queries) - (level if bias is None else level - bias)
    return jnp.dot(values, jnp.exp2(scores).astype(BF16), preferred_element_type=F32)


def careful(turned_q, mixed, peak, head, side, ref, bias=0.0):
    def one(low, carry):
        keys, values = loaded([(ref, head, low)])
        scores = scored(keys, queries_of(turned_q, head, side)) + bias
        before = peak[head, side]
        top = jnp.maximum(before, jnp.max(scores, axis=0, keepdims=True))
        probs = jnp.exp2(scores - top).astype(BF16)
        fresh = jnp.dot(values, probs, preferred_element_type=F32)
        mixed[head, side] = mixed[head, side] * jnp.exp2(before - top) + fresh
        peak[head, side] = top
        return carry

    lax.fori_loop(0, 2, one, 0)


def both_lows(head, *refs):
    return [(ref, head, low) for ref in refs for low in range(2)]


def within(sums):
    return jnp.max(sums) < LIMIT


def redo(turned_q, mixed, peak, shares, biases=(0.0, 0.0)):
    def one(head, carry):
        for side in range(2):
            for ref in shares[side]:
                careful(turned_q, mixed, peak, head, side, ref, biases[side])
        return carry

    lax.fori_loop(0, HEADS, one, 0)


def redo_alike(turned_q, mixed, peak, refs):
    def one(at, carry):
        for ref in refs:
            careful(turned_q, mixed, peak, at // 2, at % 2, ref)
        return carry

    lax.fori_loop(0, 2 * HEADS, one, 0)


def copied(source, target):
    def one(head, carry):
        target[head] = source[head]
        return carry

    lax.fori_loop(0, HEADS, one, 0)


def larger(one, two):
    return two if one is None else jnp.maximum(one, two)


def first_body(place, *refs):
    own, inner, q_in, (turned_q, mixed, peak) = refs[:2], refs[2], refs[3:7], refs[7:]
    inner = (inner.at[0], inner.at[1])
    spread(place, q_in, turned_q)

    def one(head, worst):
        for side in range(2):
            queries = queries_of(turned_q, head, side)
            level = jnp.max(scored(own[0][head, 0, 0, :HD], queries), axis=0, keepdims=True)
            peak[head, side] = level
            fresh = quick(queries, both_lows(head, *own), level) + quick(
                queries, both_lows(head, *inner), level
            )
            mixed[head, side] = fresh
            worst = jnp.maximum(worst, fresh[HD : HD + 8])
        return worst

    worst = lax.fori_loop(0, HEADS, one, jnp.zeros((8, 2 * TILE), F32))

    @pl.when(jnp.logical_not(within(worst)))
    def _():
        mixed[...] = jnp.zeros_like(mixed)
        redo_alike(turned_q, mixed, peak, (*own, *inner))


def more(turned_q, mixed_in, mixed, peak, shares, biases=(None, None)):
    worst = None
    for head in range(HEADS):
        for side in range(2):
            queries = queries_of(turned_q, head, side)
            fresh = mixed_in[head, side] + quick(
                queries, both_lows(head, *shares[side]), peak[head, side], biases[side]
            )
            mixed[head, side] = fresh
            worst = larger(worst, fresh[HD : HD + 8])
    return within(worst)


def edge_biases(place):
    return [jnp.where(place[2] == end, -1e30, 0.0).astype(F32) for end in (0, 3)]


def second_body(place, *refs):
    outer, (turned_q, mixed_in, _, mixed, peak) = refs[:2], refs[2:]

    @pl.when(place[1] == 0)
    def _():
        copied(mixed_in, mixed)

    @pl.when(place[1] == 1)
    def _():
        good = more(turned_q, mixed_in, mixed, peak, (outer, outer))

        @pl.when(jnp.logical_not(good))
        def _():
            copied(mixed_in, mixed)
            redo_alike(turned_q, mixed, peak, outer)


def third_body(place, *refs):
    left, right, turned_q, mixed_in, _, mixed, peak = refs
    biases = edge_biases(place)
    good = more(turned_q, mixed_in, mixed, peak, ((left,), (right,)), biases)

    @pl.when(jnp.logical_not(good))
    def _():
        copied(mixed_in, mixed)
        redo(turned_q, mixed, peak, ((left,), (right,)), biases)


def last_body(place, *refs):
    left, right, turned_q, mixed_in = refs[:2], refs[2:4], refs[4], refs[5]
    outs, (peak, mixed, done) = refs[7:11], refs[11:]
    biases = edge_biases(place)

    def passes(shares):
        good = more(turned_q, mixed_in, mixed, peak, shares, biases)

        @pl.when(jnp.logical_not(good))
        def _():
            copied(mixed_in, mixed)
            redo(turned_q, mixed, peak, shares, biases)

    @pl.when(place[1] == 1)
    def _():
        passes((left, right))

    @pl.when(place[1] == 0)
    def _():
        passes((left[:1], right[:1]))

    for head in range(HEADS):
        for side in range(2):
            inverse = 1.0 / mixed[head, side, HD : HD + 1]
            result = (mixed[head, side, :HD] * inverse).astype(BF16).T
            for low in range(2):
                done[2 * side + low, head] = result[low * TILE : (low + 1) * TILE]

    for step in range(4):
        z_from = (place[0] - step + 4) % 4
        for head in range(HEADS):
            outs[step][:, head * HD : (head + 1) * HD] = done[z_from, head]


def last(place, operands, flops):
    out = jax.ShapeDtypeStruct((TILE, HEADS * HD), BF16)
    return pl.pallas_call(
        last_body,
        in_specs=[SMEM] + [VMEM] * len(operands),
        out_specs=[VMEM] * 5,
        out_shape=[out] * 4 + [PEAK],
        scratch_shapes=[pltpu.VMEM(MIXED.shape, F32), pltpu.VMEM((4, HEADS, TILE, HD), BF16)],
        input_output_aliases={7: 4},
        cost_estimate=pl.CostEstimate(flops=flops, bytes_accessed=1 << 20, transcendentals=0),
        compiler_params=pltpu.CompilerParams(vmem_limit_bytes=24 * 1024 * 1024),
        name="last",
    )(place, *operands)[:4]


def join_body(place, *refs):
    chunks, joined = refs[:4], refs[4]
    for step in range(4):
        for head in range(HEADS):
            joined[:, slot_cols(place, step, head)] = chunks[step][:, head * HD : (head + 1) * HD]


def own_cols(core, width):
    return pl.ds(pl.multiple_of(core * width, width), width)


def home_body(place, joined, weight, out):
    cols = own_cols(place[1], out.shape[1])
    out[...] = jnp.dot(joined[...], weight[:, cols], preferred_element_type=F32)


def cut_body(place, weight, out):
    out[...] = weight[:, own_cols(1 - place[1], out.shape[1])]


def close_body(place, here, joined, weight, gate, out):
    there = jnp.dot(joined[...], weight[...], preferred_element_type=F32)
    out[...] = (gate[...].astype(F32) * (here[...] + there)).astype(BF16)


def shards(query_tiles, key_tiles, value_tiles, out_weight, gate):
    features = query_tiles.shape[4]
    q, k, v = (a.reshape(TILE, features) for a in (query_tiles, key_tiles, value_tiles))
    core, y = lax.axis_index("grp"), lax.axis_index("ta")
    wide = lax.axis_index("wa")
    z, x = (wide % 2) * 2 + lax.axis_index("ha"), wide // 2
    place = jnp.stack([z, core, x, y]).astype(jnp.int32)
    partner, outer_pairs = pairs(to_partner), pairs(to_outer)
    to_right = pairs(lambda core, y, z, x: (core, y, z, x + 1) if x < 3 else None)
    to_left = pairs(lambda core, y, z, x: (core, y, z, x - 1) if x > 0 else None)
    upper = flat(1, 0, 0, 0)
    right_upper, left_upper = ([p for p in perm if p[0] >= upper] for perm in (to_right, to_left))
    flops_of = lambda tiles: HEADS * 4 * TILE * tiles * TILE * 6 * HD

    kv_shape = jax.ShapeDtypeStruct((HEADS, 2, TILE, HD), BF16)
    kv_sent = local_call(pack_body, place, [k, v], [kv_shape] * 4)
    kv = [send(kv_sent[s], out_to_heads(s)) for s in range(4)]
    q_shape = jax.ShapeDtypeStruct((HEADS, TILE, HD), BF16)
    q_sent = local_call(pack_q_body, place, [q], [q_shape] * 4)
    queries = [send(q_sent[s], out_to_heads(s)) for s in range(4)]
    weight_away = local_call(
        cut_body, place, [out_weight], jax.ShapeDtypeStruct((features, features), BF16)
    )
    weight_other = send(weight_away, partner)
    half = (HEADS, 2, 2, TILE, HD)
    *own, whole = local_call(
        gather_body, place, kv,
        [jax.ShapeDtypeStruct(half, BF16)] * 2 + [jax.ShapeDtypeStruct((2, *half), BF16)],
    )
    outer = [send(own[i], outer_pairs) for i in range(2)]
    inner = send(whole, partner)
    right, left = send(own[0], to_left), send(own[1], to_right)
    state = local_call(
        first_body, place, [*own, inner, *queries], [TURNED, MIXED, PEAK], flops_of(8)
    )
    turned_q, mixed, peak = state
    right_outer = send(outer[0], left_upper)
    left_outer = send(outer[1], right_upper)
    mixed, peak = local_call(
        second_body, place, [*outer, turned_q, mixed, peak], [MIXED, PEAK],
        flops_of(4), aliases={5: 1},
    )
    right_inner, left_inner = send(right, partner), send(left, partner)
    mixed, peak = local_call(
        third_body, place, [left, right, turned_q, mixed, peak],
        [MIXED, PEAK], flops_of(2), aliases={5: 1},
    )
    outs = last(
        place, [left_inner, left_outer, right_inner, right_outer, turned_q, mixed, peak], flops_of(4)
    )
    chunks = [send(outs[s], back_to_tiles(s)) for s in range(4)]
    joined = local_call(join_body, place, chunks, jax.ShapeDtypeStruct((TILE, features), BF16))
    arrived = send(joined, partner)
    flops = 2 * TILE * features * features
    here = local_call(
        home_body, place, [joined, out_weight], jax.ShapeDtypeStruct((TILE, features), F32), flops
    )
    branch = local_call(
        close_body, place, [here, arrived, weight_other, gate.reshape(1, -1)],
        jax.ShapeDtypeStruct((TILE, features), BF16), flops,
    )
    return branch.reshape(1, 1, 1, TILE, features)


def solution(mesh):
    spec = P("ta", "ha", "wa", None, "grp")

    return jax.shard_map(
        shards,
        mesh=mesh,
        in_specs=(spec, spec, spec, P("grp", None), P("grp")),
        out_specs=spec,
        check_vma=False,
    )
```

time: 137 us -> 146 us (1.066)
  the two profiles are of different devices: /device:TPU:3 before, /device:TPU:1 now
where the time goes in v3:
time: 146 us; the launch traced here: 145 us
  Pallas kernels  49.9 us (34%)
  starting transfers between devices  48.5 us (33%)
  waiting for transfers between devices  42.8 us (29%)
  local copies, waits for them, and re-layouts  3.73 us (3%)
    ppermute x23, starting transfers between devices, send(): return lax.ppermute(x, AXES, perm)  48.5 us
    pallas_call x10, Pallas kernels, local_call(): pl.pallas_call(body, in_specs=[SMEM] + [VMEM] * len(operands), out_specs=...  46 us
    ppermute x23, waiting for transfers between devices, send(): return lax.ppermute(x, AXES, perm)  42.8 us
    pallas_call x1, Pallas kernels, last(): pl.pallas_call(last_body, in_specs=[SMEM] + [VMEM] * len(operands), out_s...  3.94 us
    unnamed x16, local copies, waits for them, and re-layouts  3.72 us
  transfers between devices with their start and end apart: 23, of which 14 were waited for; matrix products, arithmetic and copies ran while one was open for 0% of the time, Pallas kernels for 32%

profile of v3, /device:TPU:1, one launch (start us, length us, event | category | flops | bytes accessed | tf_op | source)
XLA Modules:
  0.0 145.5 jit_solution(11834934752234814692)
XLA Ops:
  0.0 0.1 pad_add_fusion.place
  0.1 3.7 %copy-done = bf16[1536,3072]{1,0:T(8,128)(2,1)S(1)} copy-done((bf16[1536,3072]{1,0:T(8,128)(2,1)S(1)}, bf16[1536,3072]{1,0:T(8,128)(2,1)}, u32[]{:S(2)}) %copy-start) | copy-done | bytes 9437208
  3.8 0.9 shard_map.63
  4.6 0.0 copy-start.3
  4.7 1.5 %collective-permute-start.22 = (bf16[1536,1536]{1,0:T(8,128)(2,1)S(1)}, bf16[1536,1536]{1,0:T(8,128)(2,1)S(1)}, u32[]{:S(2)}, u32[]{:S(2)}) collective-permute-start(bf16[1536,1536]{1,0:T(8,128)(2,1)S(1)} %shard_map.63), channel_id=1, source_target_pairs={{0,64},{1,65},{2,66},{3,67},{4,68},{5,69},{6,70},{7,71},{8,72},{9,... | collective-permute-start | bytes 14155784 | tf_op jit(solution)/shard_map/ppermute | solution.py:60
  6.1 0.8 shard_map.55
  7.0 3.6 %collective-permute-start = (bf16[3,2,256,128]{3,2,1,0:T(8,128)(2,1)S(1)}, bf16[3,2,256,128]{3,2,1,0:T(8,128)(2,1)S(1)}, u32[]{:S(2)}, u32[]{:S(2)}) collective-permute-start(bf16[3,2,256,128]{3,2,1,0:T(8,128)(2,1)S(1)} %get-tuple-element.27), channel_id=1, source_target_pairs={{0,0},{1,1},{2,2},{3,3},{4,4},{5,5},{6,6},{7,7},{8,8},{9,9},{10,10... | collective-permute-start | bytes 1179656 | tf_op jit(solution)/shard_map/ppermute | solution.py:60
  10.6 1.6 %collective-permute-start.1 = (bf16[3,2,256,128]{3,2,1,0:T(8,128)(2,1)S(1)}, bf16[3,2,256,128]{3,2,1,0:T(8,128)(2,1)S(1)}, u32[]{:S(2)}, u32[]{:S(2)}) collective-permute-start(bf16[3,2,256,128]{3,2,1,0:T(8,128)(2,1)S(1)} %get-tuple-element.28), channel_id=1, source_target_pairs={{0,8},{1,9},{2,10},{3,11},{4,12},{5,13},{6,14},{7,15},{8,1},{9,0},... | collective-permute-start | bytes 1179656 | tf_op jit(solution)/shard_map/ppermute | solution.py:60
  12.2 4.6 %collective-permute-start.2 = (bf16[3,2,256,128]{3,2,1,0:T(8,128)(2,1)S(1)}, bf16[3,2,256,128]{3,2,1,0:T(8,128)(2,1)S(1)}, u32[]{:S(2)}, u32[]{:S(2)}) collective-permute-start(bf16[3,2,256,128]{3,2,1,0:T(8,128)(2,1)S(1)} %get-tuple-element.29), channel_id=1, source_target_pairs={{0,1},{1,0},{2,3},{3,2},{4,5},{5,4},{6,7},{7,6},{8,9},{9,8},{10,11... | collective-permute-start | bytes 1179656 | tf_op jit(solution)/shard_map/ppermute | solution.py:60
  16.8 0.6 collective-permute-start.3
  17.4 0.0 collective-permute-done.refs_0_
  17.4 6.8 %collective-permute-done.1.refs_1_ = bf16[3,2,256,128]{3,2,1,0:T(8,128)(2,1)S(1)} collective-permute-done((bf16[3,2,256,128]{3,2,1,0:T(8,128)(2,1)S(1)}, bf16[3,2,256,128]{3,2,1,0:T(8,128)(2,1)S(1)}, u32[]{:S(2)}, u32[]{:S(2)}) %collective-permute-start.1) | collective-permute-done | bytes 393248 | tf_op jit(solution)/shard_map/ppermute | solution.py:60
  24.2 3.9 %collective-permute-done.2.refs_2_ = bf16[3,2,256,128]{3,2,1,0:T(8,128)(2,1)S(1)} collective-permute-done((bf16[3,2,256,128]{3,2,1,0:T(8,128)(2,1)S(1)}, bf16[3,2,256,128]{3,2,1,0:T(8,128)(2,1)S(1)}, u32[]{:S(2)}, u32[]{:S(2)}) %collective-permute-start.2) | collective-permute-done | bytes 393248 | tf_op jit(solution)/shard_map/ppermute | solution.py:60
  28.1 2.5 %collective-permute-done.3.refs_3_ = bf16[3,2,256,128]{3,2,1,0:T(8,128)(2,1)S(1)} collective-permute-done((bf16[3,2,256,128]{3,2,1,0:T(8,128)(2,1)S(1)}, bf16[3,2,256,128]{3,2,1,0:T(8,128)(2,1)S(1)}, u32[]{:S(2)}, u32[]{:S(2)}) %collective-permute-start.3) | collective-permute-done | bytes 393248 | tf_op jit(solution)/shard_map/ppermute | solution.py:60
  30.6 0.8 shard_map.56
  31.4 4.6 %collective-permute-start.10 = (bf16[3,2,2,256,128]{4,3,2,1,0:T(8,128)(2,1)S(1)}, bf16[3,2,2,256,128]{4,3,2,1,0:T(8,128)(2,1)S(1)}, u32[]{:S(2)}, u32[]{:S(2)}) collective-permute-start(bf16[3,2,2,256,128]{4,3,2,1,0:T(8,128)(2,1)S(1)} %get-tuple-element.32.refs_0_), channel_id=1, source_target_pairs={{64,112},{65,113},{66,114},{67,115},{68,116},{69,117},{70,118},{71... | collective-permute-start | bytes 2359304 | tf_op jit(solution)/shard_map/ppermute | solution.py:60
  36.1 0.1 collective-permute-start.12
  36.2 0.8 shard_map.57
  37.0 2.2 %collective-permute-start.13 = (bf16[3,256,128]{2,1,0:T(8,128)(2,1)S(1)}, bf16[3,256,128]{2,1,0:T(8,128)(2,1)S(1)}, u32[]{:S(2)}, u32[]{:S(2)}) collective-permute-start(bf16[3,256,128]{2,1,0:T(8,128)(2,1)S(1)} %get-tuple-element.34), channel_id=1, source_target_pairs={{0,0},{1,1},{2,2},{3,3},{4,4},{5,5},{6,6},{7,7},{8,8},{9,9},{10,10... | collective-permute-start | bytes 589832 | tf_op jit(solution)/shard_map/ppermute | solution.py:60
  39.2 3.6 %collective-permute-start.14 = (bf16[3,256,128]{2,1,0:T(8,128)(2,1)S(1)}, bf16[3,256,128]{2,1,0:T(8,128)(2,1)S(1)}, u32[]{:S(2)}, u32[]{:S(2)}) collective-permute-start(bf16[3,256,128]{2,1,0:T(8,128)(2,1)S(1)} %get-tuple-element.35), channel_id=1, source_target_pairs={{0,8},{1,9},{2,10},{3,11},{4,12},{5,13},{6,14},{7,15},{8,1},{9,0},... | collective-permute-start | bytes 589832 | tf_op jit(solution)/shard_map/ppermute | solution.py:60
  42.8 1.4 collective-permute-done.13.refs_3_
  44.3 2.5 %collective-permute-start.15 = (bf16[3,256,128]{2,1,0:T(8,128)(2,1)S(1)}, bf16[3,256,128]{2,1,0:T(8,128)(2,1)S(1)}, u32[]{:S(2)}, u32[]{:S(2)}) collective-permute-start(bf16[3,256,128]{2,1,0:T(8,128)(2,1)S(1)} %get-tuple-element.36), channel_id=1, source_target_pairs={{0,1},{1,0},{2,3},{3,2},{4,5},{5,4},{6,7},{7,6},{8,9},{9,8},{10,11... | collective-permute-start | bytes 589832 | tf_op jit(solution)/shard_map/ppermute | solution.py:60
  46.8 2.4 %collective-permute-done.14.refs_4_ = bf16[3,256,128]{2,1,0:T(8,128)(2,1)S(1)} collective-permute-done((bf16[3,256,128]{2,1,0:T(8,128)(2,1)S(1)}, bf16[3,256,128]{2,1,0:T(8,128)(2,1)S(1)}, u32[]{:S(2)}, u32[]{:S(2)}) %collective-permute-start.14) | collective-permute-done | bytes 196640 | tf_op jit(solution)/shard_map/ppermute | solution.py:60
  49.2 1.0 collective-permute-start.16
  50.2 1.5 %collective-permute-done.15.refs_5_ = bf16[3,256,128]{2,1,0:T(8,128)(2,1)S(1)} collective-permute-done((bf16[3,256,128]{2,1,0:T(8,128)(2,1)S(1)}, bf16[3,256,128]{2,1,0:T(8,128)(2,1)S(1)}, u32[]{:S(2)}, u32[]{:S(2)}) %collective-permute-start.15) | collective-permute-done | bytes 196640 | tf_op jit(solution)/shard_map/ppermute | solution.py:60
  51.8 2.3 %collective-permute-start.6 = (bf16[3,2,2,256,128]{4,3,2,1,0:T(8,128)(2,1)S(1)}, bf16[3,2,2,256,128]{4,3,2,1,0:T(8,128)(2,1)S(1)}, u32[]{:S(2)}, u32[]{:S(2)}) collective-permute-start(bf16[3,2,2,256,128]{4,3,2,1,0:T(8,128)(2,1)S(1)} %get-tuple-element.31.refs_1_), channel_id=1, source_target_pairs={{64,112},{65,113},{66,114},{67,115},{68,116},{69,117},{70,118},{71... | collective-permute-start | bytes 2359304 | tf_op jit(solution)/shard_map/ppermute | solution.py:60
  54.1 1.2 collective-permute-done.16.refs_6_
  55.3 3.2 %collective-permute-start.4 = (bf16[3,2,2,256,128]{4,3,2,1,0:T(8,128)(2,1)S(1)}, bf16[3,2,2,256,128]{4,3,2,1,0:T(8,128)(2,1)S(1)}, u32[]{:S(2)}, u32[]{:S(2)}) collective-permute-start(bf16[3,2,2,256,128]{4,3,2,1,0:T(8,128)(2,1)S(1)} %get-tuple-element.31.refs_1_), channel_id=1, source_target_pairs={{0,2},{1,3},{2,4},{3,5},{4,6},{5,7},{8,10},{9,11},{10,12},{11,13},... | collective-permute-start | bytes 2359304 | tf_op jit(solution)/shard_map/ppermute | solution.py:60
  58.5 0.0 collective-permute-done.10.refs_0_
  58.5 1.3 collective-permute-start.8
  59.8 5.9 %collective-permute-done.6.refs_1_ = bf16[3,2,2,256,128]{4,3,2,1,0:T(8,128)(2,1)S(1)} collective-permute-done((bf16[3,2,2,256,128]{4,3,2,1,0:T(8,128)(2,1)S(1)}, bf16[3,2,2,256,128]{4,3,2,1,0:T(8,128)(2,1)S(1)}, u32[]{:S(2)}, u32[]{:S(2)}) %collective-permute-start.6) | collective-permute-done | bytes 786464 | tf_op jit(solution)/shard_map/ppermute | solution.py:60
  65.7 1.3 collective-permute-start.11
  67.0 7.2 %collective-permute-done.4.refs_0_ = bf16[3,2,2,256,128]{4,3,2,1,0:T(8,128)(2,1)S(1)} collective-permute-done((bf16[3,2,2,256,128]{4,3,2,1,0:T(8,128)(2,1)S(1)}, bf16[3,2,2,256,128]{4,3,2,1,0:T(8,128)(2,1)S(1)}, u32[]{:S(2)}, u32[]{:S(2)}) %collective-permute-start.4) | collective-permute-done | bytes 786464 | tf_op jit(solution)/shard_map/ppermute | solution.py:60
  74.2 1.9 %collective-permute-start.5 = (bf16[3,2,2,256,128]{4,3,2,1,0:T(8,128)(2,1)S(1)}, bf16[3,2,2,256,128]{4,3,2,1,0:T(8,128)(2,1)S(1)}, u32[]{:S(2)}, u32[]{:S(2)}) collective-permute-start(bf16[3,2,2,256,128]{4,3,2,1,0:T(8,128)(2,1)S(1)} %collective-permute-done.4.refs_0_), channel_id=1, source_target_pairs={{0,64},{1,65},{2,66},{3,67},{4,68},{5,69},{6,70},{7,71},{8,72},{9,... | collective-permute-start | bytes 2359304 | tf_op jit(solution)/shard_map/ppermute | solution.py:60
  76.2 2.0 %collective-permute-done.8.refs_1_ = bf16[3,2,2,256,128]{4,3,2,1,0:T(8,128)(2,1)S(1)} collective-permute-done((bf16[3,2,2,256,128]{4,3,2,1,0:T(8,128)(2,1)S(1)}, bf16[3,2,2,256,128]{4,3,2,1,0:T(8,128)(2,1)S(1)}, u32[]{:S(2)}, u32[]{:S(2)}) %collective-permute-start.8) | collective-permute-done | bytes 786464 | tf_op jit(solution)/shard_map/ppermute | solution.py:60
  78.1 3.1 %collective-permute-start.7 = (bf16[3,2,2,256,128]{4,3,2,1,0:T(8,128)(2,1)S(1)}, bf16[3,2,2,256,128]{4,3,2,1,0:T(8,128)(2,1)S(1)}, u32[]{:S(2)}, u32[]{:S(2)}) collective-permute-start(bf16[3,2,2,256,128]{4,3,2,1,0:T(8,128)(2,1)S(1)} %collective-permute-done.6.refs_1_), channel_id=1, source_target_pairs={{64,66},{65,67},{66,68},{67,69},{68,70},{69,71},{72,74},{73,75},{7... | collective-permute-start | bytes 2359304 | tf_op jit(solution)/shard_map/ppermute | solution.py:60
  81.3 0.0 collective-permute-done.12.refs_2_
  81.3 1.7 %collective-permute-start.9 = (bf16[3,2,2,256,128]{4,3,2,1,0:T(8,128)(2,1)S(1)}, bf16[3,2,2,256,128]{4,3,2,1,0:T(8,128)(2,1)S(1)}, u32[]{:S(2)}, u32[]{:S(2)}) collective-permute-start(bf16[3,2,2,256,128]{4,3,2,1,0:T(8,128)(2,1)S(1)} %collective-permute-done.8.refs_1_), channel_id=1, source_target_pairs={{0,64},{1,65},{2,66},{3,67},{4,68},{5,69},{6,70},{7,71},{8,72},{9,... | collective-permute-start | bytes 2359304 | tf_op jit(solution)/shard_map/ppermute | solution.py:60
  82.9 30.7 %shard_map.58 = (bf16[3,4,256,256]{3,2,1,0:T(8,128)(2,1)S(1)}, f32[3,2,144,512]{3,2,1,0:T(8,128)S(1)}, f32[3,2,1,512]{3,2,1,0:T(1,128)S(1)}) custom-call(s32[4]{0:T(128)S(1)} %pad_add_fusion.place, bf16[3,2,2,256,128]{4,3,2,1,0:T(8,128)(2,1)S(1)} %get-tuple-element.32.refs_0_, bf16[3,2,2,256,128]{4,3,2,1,0:T(8,128)(2,1)S(1)} %get-tuple-element.31.refs_1_, ...), custom_call_target="tpu_custom_call" | custom-call | flops 4831838208 | bytes 7286784 | tf_op jit(solution)/shard_map/pallas_call | solution.py:97
  113.6 0.0 slice-start
  113.6 0.0 slice-start.1
  113.6 3.7 %shard_map.59 = (f32[3,2,144,512]{3,2,1,0:T(8,128)S(1)}, f32[3,2,1,512]{3,2,1,0:T(1,128)S(1)}) custom-call(s32[4]{0:T(128)S(1)} %pad_add_fusion.place, bf16[3,2,2,256,128]{4,3,2,1,0:T(8,128)(2,1)S(1)} %collective-permute-done.10.refs_0_, bf16[3,2,2,256,128]{4,3,2,1,0:T(8,128)(2,1)S(1)} %collective-permute-done.6.refs_1_, ...), custom_call_target="tpu_custom_call", output_to_operand_aliasing={{1}: (5, {})} | custom-call | flops 2415919104 | bytes 6709248 | tf_op jit(solution)/shard_map/pallas_call | solution.py:97
  117.4 2.8 %shard_map.60 = (f32[3,2,144,512]{3,2,1,0:T(8,128)S(1)}, f32[3,2,1,512]{3,2,1,0:T(1,128)S(1)}) custom-call(s32[4]{0:T(128)S(1)} %pad_add_fusion.place, bf16[3,2,2,256,128]{4,3,2,1,0:T(8,128)(2,1)S(1)} %collective-permute-done.4.refs_0_, bf16[3,2,2,256,128]{4,3,2,1,0:T(8,128)(2,1)S(1)} %collective-permute-done.8.refs_1_, ...), custom_call_target="tpu_custom_call", output_to_operand_aliasing={{1}: (5, {})} | custom-call | flops 1207959552 | bytes 6709248 | tf_op jit(solution)/shard_map/pallas_call | solution.py:97
  120.2 0.0 collective-permute-done.11.refs_3_
  120.2 0.0 collective-permute-done.5.refs_0_
  120.2 0.0 collective-permute-done.7.refs_1_
  120.2 0.0 collective-permute-done.9.refs_2_
  120.3 0.0 copy-start.4
  120.3 0.0 slice-start.2
  120.3 3.9 %last.1 = (bf16[256,384]{1,0:T(8,128)(2,1)S(1)}, bf16[256,384]{1,0:T(8,128)(2,1)S(1)}, bf16[256,384]{1,0:T(8,128)(2,1)S(1)}, bf16[256,384]{1,0:T(8,128)(2,1)S(1)}, f32[3,2,1,512]{3,2,1,0:T(1,128)S(1)}) custom-call(s32[4]{0:T(128)S(1)} %pad_add_fusion.place, ...), custom_call_target="tpu_custom_call", output_to_operand_aliasing={{4}: (7, {})} | custom-call | flops 2415919104 | bytes 1048576 | tf_op jit(solution)/shard_map/last/pallas_call | solution.py:323
  124.2 1.9 %collective-permute-start.17 = (bf16[256,384]{1,0:T(8,128)(2,1)S(1)}, bf16[256,384]{1,0:T(8,128)(2,1)S(1)}, u32[]{:S(2)}, u32[]{:S(2)}) collective-permute-start(bf16[256,384]{1,0:T(8,128)(2,1)S(1)} %get-tuple-element.45), channel_id=1, source_target_pairs={{0,0},{1,1},{2,2},{3,3},{4,4},{5,5},{6,6},{7,7},{8,8},{9,9},{10,10... | collective-permute-start | bytes 589832 | tf_op jit(solution)/shard_map/ppermute | solution.py:60
  126.2 1.9 %collective-permute-start.18 = (bf16[256,384]{1,0:T(8,128)(2,1)S(1)}, bf16[256,384]{1,0:T(8,128)(2,1)S(1)}, u32[]{:S(2)}, u32[]{:S(2)}) collective-permute-start(bf16[256,384]{1,0:T(8,128)(2,1)S(1)} %get-tuple-element.46), channel_id=1, source_target_pairs={{0,9},{1,8},{2,11},{3,10},{4,13},{5,12},{6,15},{7,14},{8,0},{9,1},... | collective-permute-start | bytes 589832 | tf_op jit(solution)/shard_map/ppermute | solution.py:60
  128.0 3.1 %collective-permute-start.19 = (bf16[256,384]{1,0:T(8,128)(2,1)S(1)}, bf16[256,384]{1,0:T(8,128)(2,1)S(1)}, u32[]{:S(2)}, u32[]{:S(2)}) collective-permute-start(bf16[256,384]{1,0:T(8,128)(2,1)S(1)} %get-tuple-element.47), channel_id=1, source_target_pairs={{0,1},{1,0},{2,3},{3,2},{4,5},{5,4},{6,7},{7,6},{8,9},{9,8},{10,11... | collective-permute-start | bytes 589832 | tf_op jit(solution)/shard_map/ppermute | solution.py:60
  131.1 1.0 collective-permute-start.20
  132.1 0.0 collective-permute-done.17.refs_0_
  132.1 2.9 %collective-permute-done.18.refs_1_ = bf16[256,384]{1,0:T(8,128)(2,1)S(1)} collective-permute-done((bf16[256,384]{1,0:T(8,128)(2,1)S(1)}, bf16[256,384]{1,0:T(8,128)(2,1)S(1)}, u32[]{:S(2)}, u32[]{:S(2)}) %collective-permute-start.18) | collective-permute-done | bytes 196640 | tf_op jit(solution)/shard_map/ppermute | solution.py:60
  135.0 3.8 %collective-permute-done.19.refs_2_ = bf16[256,384]{1,0:T(8,128)(2,1)S(1)} collective-permute-done((bf16[256,384]{1,0:T(8,128)(2,1)S(1)}, bf16[256,384]{1,0:T(8,128)(2,1)S(1)}, u32[]{:S(2)}, u32[]{:S(2)}) %collective-permute-start.19) | collective-permute-done | bytes 196640 | tf_op jit(solution)/shard_map/ppermute | solution.py:60
  138.7 0.9 collective-permute-done.20.refs_3_
  139.6 0.7 shard_map.61.joined
  140.3 0.1 collective-permute-start.21
  140.4 1.9 %shard_map.62.here = f32[256,1536]{1,0:T(8,128)S(1)} custom-call(s32[4]{0:T(128)S(1)} %pad_add_fusion.place, bf16[256,1536]{1,0:T(8,128)(2,1)S(1)} %shard_map.61.joined, bf16[1536,3072]{1,0:T(8,128)(2,1)S(1)} %bitcast.9), custom_call_target="tpu_custom_call" | custom-call | flops 1207959552 | bytes 11796480 | tf_op jit(solution)/shard_map/pallas_call | solution.py:97
  142.4 0.3 collective-permute-done.21.joined
  142.7 0.0 collective-permute-done.22.weight
  142.7 2.8 %shard_map.64 = bf16[256,1536]{1,0:T(8,128)(2,1)} custom-call(s32[4]{0:T(128)S(1)} %pad_add_fusion.place, f32[256,1536]{1,0:T(8,128)S(1)} %shard_map.62.here, bf16[256,1536]{1,0:T(8,128)(2,1)S(1)} %collective-permute-done.21.joined, bf16[1536,1536]{1,0:T(8,128)(2,1)S(1)} %collective-permute-done.22.weight, bf16[1,1536]{1,0:T(2,128)(2,1)S(1)} %reshape.18.gate), custom_call_target="tpu_custom_call" | custom-call | flops 1207959552 | bytes 7867392 | tf_op jit(solution)/shard_map/pallas_call | solution.py:97
  (12 shorter events, 0.0 us)
Async XLA Ops:
  0.1 3.7 %copy-start = (bf16[1536,3072]{1,0:T(8,128)(2,1)S(1)}, bf16[1536,3072]{1,0:T(8,128)(2,1)}, u32[]{:S(2)}) copy-start(bf16[1536,3072]{1,0:T(8,128)(2,1)} %weight.3) | copy-start | bytes 28311556
  3.8 2.4 %copy-start.1 = (bf16[1,1,1,256,1536]{4,3,2,1,0:T(8,128)(2,1)S(1)}, bf16[1,1,1,256,1536]{4,3,2,1,0:T(8,128)(2,1)}, u32[]{:S(2)}) copy-start(bf16[1,1,1,256,1536]{4,3,2,1,0:T(8,128)(2,1)} %param.6) | copy-start | bytes 2359300
  3.8 2.4 %copy-start.2 = (bf16[1,1,1,256,1536]{4,3,2,1,0:T(8,128)(2,1)S(1)}, bf16[1,1,1,256,1536]{4,3,2,1,0:T(8,128)(2,1)}, u32[]{:S(2)}) copy-start(bf16[1,1,1,256,1536]{4,3,2,1,0:T(8,128)(2,1)} %param.7) | copy-start | bytes 2359300
  4.6 31.5 %copy-start.3 = (bf16[1,1,1,256,1536]{4,3,2,1,0:T(8,128)(2,1)S(1)}, bf16[1,1,1,256,1536]{4,3,2,1,0:T(8,128)(2,1)}, u32[]{:S(2)}) copy-start(bf16[1,1,1,256,1536]{4,3,2,1,0:T(8,128)(2,1)} %param.5) | copy-start | bytes 2359300
  4.7 138.0 %collective-permute-start.22 = (bf16[1536,1536]{1,0:T(8,128)(2,1)S(1)}, bf16[1536,1536]{1,0:T(8,128)(2,1)S(1)}, u32[]{:S(2)}, u32[]{:S(2)}) collective-permute-start(bf16[1536,1536]{1,0:T(8,128)(2,1)S(1)} %shard_map.63), channel_id=1, source_target_pairs={{0,64},{1,65},{2,66},{3,67},{4,68},{5,69},{6,70},{7,71},{8,72},{9,... | collective-permute-start | bytes 14155784 | tf_op jit(solution)/shard_map/ppermute | solution.py:60
  7.0 10.4 %collective-permute-start = (bf16[3,2,256,128]{3,2,1,0:T(8,128)(2,1)S(1)}, bf16[3,2,256,128]{3,2,1,0:T(8,128)(2,1)S(1)}, u32[]{:S(2)}, u32[]{:S(2)}) collective-permute-start(bf16[3,2,256,128]{3,2,1,0:T(8,128)(2,1)S(1)} %get-tuple-element.27), channel_id=1, source_target_pairs={{0,0},{1,1},{2,2},{3,3},{4,4},{5,5},{6,6},{7,7},{8,8},{9,9},{10,10... | collective-permute-start | bytes 1179656 | tf_op jit(solution)/shard_map/ppermute | solution.py:60
  10.6 13.6 %collective-permute-start.1 = (bf16[3,2,256,128]{3,2,1,0:T(8,128)(2,1)S(1)}, bf16[3,2,256,128]{3,2,1,0:T(8,128)(2,1)S(1)}, u32[]{:S(2)}, u32[]{:S(2)}) collective-permute-start(bf16[3,2,256,128]{3,2,1,0:T(8,128)(2,1)S(1)} %get-tuple-element.28), channel_id=1, source_target_pairs={{0,8},{1,9},{2,10},{3,11},{4,12},{5,13},{6,14},{7,15},{8,1},{9,0},... | collective-permute-start | bytes 1179656 | tf_op jit(solution)/shard_map/ppermute | solution.py:60
  12.2 15.9 %collective-permute-start.2 = (bf16[3,2,256,128]{3,2,1,0:T(8,128)(2,1)S(1)}, bf16[3,2,256,128]{3,2,1,0:T(8,128)(2,1)S(1)}, u32[]{:S(2)}, u32[]{:S(2)}) collective-permute-start(bf16[3,2,256,128]{3,2,1,0:T(8,128)(2,1)S(1)} %get-tuple-element.29), channel_id=1, source_target_pairs={{0,1},{1,0},{2,3},{3,2},{4,5},{5,4},{6,7},{7,6},{8,9},{9,8},{10,11... | collective-permute-start | bytes 1179656 | tf_op jit(solution)/shard_map/ppermute | solution.py:60
  16.8 13.8 %collective-permute-start.3 = (bf16[3,2,256,128]{3,2,1,0:T(8,128)(2,1)S(1)}, bf16[3,2,256,128]{3,2,1,0:T(8,128)(2,1)S(1)}, u32[]{:S(2)}, u32[]{:S(2)}) collective-permute-start(bf16[3,2,256,128]{3,2,1,0:T(8,128)(2,1)S(1)} %get-tuple-element.30), channel_id=1, source_target_pairs={{0,9},{1,8},{2,11},{3,10},{4,13},{5,12},{6,15},{7,14},{8,0},{9,1},... | collective-permute-start | bytes 1179656 | tf_op jit(solution)/shard_map/ppermute | solution.py:60
  31.4 27.0 %collective-permute-start.10 = (bf16[3,2,2,256,128]{4,3,2,1,0:T(8,128)(2,1)S(1)}, bf16[3,2,2,256,128]{4,3,2,1,0:T(8,128)(2,1)S(1)}, u32[]{:S(2)}, u32[]{:S(2)}) collective-permute-start(bf16[3,2,2,256,128]{4,3,2,1,0:T(8,128)(2,1)S(1)} %get-tuple-element.32.refs_0_), channel_id=1, source_target_pairs={{64,112},{65,113},{66,114},{67,115},{68,116},{69,117},{70,118},{71... | collective-permute-start | bytes 2359304 | tf_op jit(solution)/shard_map/ppermute | solution.py:60
  36.1 45.2 %collective-permute-start.12 = (bf16[2,3,2,2,256,128]{5,4,3,2,1,0:T(8,128)(2,1)S(1)}, bf16[2,3,2,2,256,128]{5,4,3,2,1,0:T(8,128)(2,1)S(1)}, u32[]{:S(2)}, u32[]{:S(2)}) collective-permute-start(bf16[2,3,2,2,256,128]{5,4,3,2,1,0:T(8,128)(2,1)S(1)} %get-tuple-element.33), channel_id=1, source_target_pairs={{0,64},{1,65},{2,66},{3,67},{4,68},{5,69},{6,70},{7,71},{8,72},{9,... | collective-permute-start | bytes 4718600 | tf_op jit(solution)/shard_map/ppermute | solution.py:60
  37.0 7.3 %collective-permute-start.13 = (bf16[3,256,128]{2,1,0:T(8,128)(2,1)S(1)}, bf16[3,256,128]{2,1,0:T(8,128)(2,1)S(1)}, u32[]{:S(2)}, u32[]{:S(2)}) collective-permute-start(bf16[3,256,128]{2,1,0:T(8,128)(2,1)S(1)} %get-tuple-element.34), channel_id=1, source_target_pairs={{0,0},{1,1},{2,2},{3,3},{4,4},{5,5},{6,6},{7,7},{8,8},{9,9},{10,10... | collective-permute-start | bytes 589832 | tf_op jit(solution)/shard_map/ppermute | solution.py:60
  39.2 10.0 %collective-permute-start.14 = (bf16[3,256,128]{2,1,0:T(8,128)(2,1)S(1)}, bf16[3,256,128]{2,1,0:T(8,128)(2,1)S(1)}, u32[]{:S(2)}, u32[]{:S(2)}) collective-permute-start(bf16[3,256,128]{2,1,0:T(8,128)(2,1)S(1)} %get-tuple-element.35), channel_id=1, source_target_pairs={{0,8},{1,9},{2,10},{3,11},{4,12},{5,13},{6,14},{7,15},{8,1},{9,0},... | collective-permute-start | bytes 589832 | tf_op jit(solution)/shard_map/ppermute | solution.py:60
  44.3 7.5 %collective-permute-start.15 = (bf16[3,256,128]{2,1,0:T(8,128)(2,1)S(1)}, bf16[3,256,128]{2,1,0:T(8,128)(2,1)S(1)}, u32[]{:S(2)}, u32[]{:S(2)}) collective-permute-start(bf16[3,256,128]{2,1,0:T(8,128)(2,1)S(1)} %get-tuple-element.36), channel_id=1, source_target_pairs={{0,1},{1,0},{2,3},{3,2},{4,5},{5,4},{6,7},{7,6},{8,9},{9,8},{10,11... | collective-permute-start | bytes 589832 | tf_op jit(solution)/shard_map/ppermute | solution.py:60
  49.2 6.1 %collective-permute-start.16 = (bf16[3,256,128]{2,1,0:T(8,128)(2,1)S(1)}, bf16[3,256,128]{2,1,0:T(8,128)(2,1)S(1)}, u32[]{:S(2)}, u32[]{:S(2)}) collective-permute-start(bf16[3,256,128]{2,1,0:T(8,128)(2,1)S(1)} %get-tuple-element.37), channel_id=1, source_target_pairs={{0,9},{1,8},{2,11},{3,10},{4,13},{5,12},{6,15},{7,14},{8,0},{9,1},... | collective-permute-start | bytes 589832 | tf_op jit(solution)/shard_map/ppermute | solution.py:60
  51.8 13.9 %collective-permute-start.6 = (bf16[3,2,2,256,128]{4,3,2,1,0:T(8,128)(2,1)S(1)}, bf16[3,2,2,256,128]{4,3,2,1,0:T(8,128)(2,1)S(1)}, u32[]{:S(2)}, u32[]{:S(2)}) collective-permute-start(bf16[3,2,2,256,128]{4,3,2,1,0:T(8,128)(2,1)S(1)} %get-tuple-element.31.refs_1_), channel_id=1, source_target_pairs={{64,112},{65,113},{66,114},{67,115},{68,116},{69,117},{70,118},{71... | collective-permute-start | bytes 2359304 | tf_op jit(solution)/shard_map/ppermute | solution.py:60
  55.3 18.9 %collective-permute-start.4 = (bf16[3,2,2,256,128]{4,3,2,1,0:T(8,128)(2,1)S(1)}, bf16[3,2,2,256,128]{4,3,2,1,0:T(8,128)(2,1)S(1)}, u32[]{:S(2)}, u32[]{:S(2)}) collective-permute-start(bf16[3,2,2,256,128]{4,3,2,1,0:T(8,128)(2,1)S(1)} %get-tuple-element.31.refs_1_), channel_id=1, source_target_pairs={{0,2},{1,3},{2,4},{3,5},{4,6},{5,7},{8,10},{9,11},{10,12},{11,13},... | collective-permute-start | bytes 2359304 | tf_op jit(solution)/shard_map/ppermute | solution.py:60
  58.5 19.7 %collective-permute-start.8 = (bf16[3,2,2,256,128]{4,3,2,1,0:T(8,128)(2,1)S(1)}, bf16[3,2,2,256,128]{4,3,2,1,0:T(8,128)(2,1)S(1)}, u32[]{:S(2)}, u32[]{:S(2)}) collective-permute-start(bf16[3,2,2,256,128]{4,3,2,1,0:T(8,128)(2,1)S(1)} %get-tuple-element.32.refs_0_), channel_id=1, source_target_pairs={{2,0},{3,1},{4,2},{5,3},{6,4},{7,5},{10,8},{11,9},{12,10},{13,11},... | collective-permute-start | bytes 2359304 | tf_op jit(solution)/shard_map/ppermute | solution.py:60
  65.7 54.5 %collective-permute-start.11 = (bf16[3,2,2,256,128]{4,3,2,1,0:T(8,128)(2,1)S(1)}, bf16[3,2,2,256,128]{4,3,2,1,0:T(8,128)(2,1)S(1)}, u32[]{:S(2)}, u32[]{:S(2)}) collective-permute-start(bf16[3,2,2,256,128]{4,3,2,1,0:T(8,128)(2,1)S(1)} %collective-permute-done.10.refs_0_), channel_id=1, source_target_pairs={{66,64},{67,65},{68,66},{69,67},{70,68},{71,69},{74,72},{75,73},{7... | collective-permute-start | bytes 2359304 | tf_op jit(solution)/shard_map/ppermute | solution.py:60
  74.2 46.0 %collective-permute-start.5 = (bf16[3,2,2,256,128]{4,3,2,1,0:T(8,128)(2,1)S(1)}, bf16[3,2,2,256,128]{4,3,2,1,0:T(8,128)(2,1)S(1)}, u32[]{:S(2)}, u32[]{:S(2)}) collective-permute-start(bf16[3,2,2,256,128]{4,3,2,1,0:T(8,128)(2,1)S(1)} %collective-permute-done.4.refs_0_), channel_id=1, source_target_pairs={{0,64},{1,65},{2,66},{3,67},{4,68},{5,69},{6,70},{7,71},{8,72},{9,... | collective-permute-start | bytes 2359304 | tf_op jit(solution)/shard_map/ppermute | solution.py:60
  78.1 42.1 %collective-permute-start.7 = (bf16[3,2,2,256,128]{4,3,2,1,0:T(8,128)(2,1)S(1)}, bf16[3,2,2,256,128]{4,3,2,1,0:T(8,128)(2,1)S(1)}, u32[]{:S(2)}, u32[]{:S(2)}) collective-permute-start(bf16[3,2,2,256,128]{4,3,2,1,0:T(8,128)(2,1)S(1)} %collective-permute-done.6.refs_1_), channel_id=1, source_target_pairs={{64,66},{65,67},{66,68},{67,69},{68,70},{69,71},{72,74},{73,75},{7... | collective-permute-start | bytes 2359304 | tf_op jit(solution)/shard_map/ppermute | solution.py:60
  81.3 39.0 %collective-permute-start.9 = (bf16[3,2,2,256,128]{4,3,2,1,0:T(8,128)(2,1)S(1)}, bf16[3,2,2,256,128]{4,3,2,1,0:T(8,128)(2,1)S(1)}, u32[]{:S(2)}, u32[]{:S(2)}) collective-permute-start(bf16[3,2,2,256,128]{4,3,2,1,0:T(8,128)(2,1)S(1)} %collective-permute-done.8.refs_1_), channel_id=1, source_target_pairs={{0,64},{1,65},{2,66},{3,67},{4,68},{5,69},{6,70},{7,71},{8,72},{9,... | collective-permute-start | bytes 2359304 | tf_op jit(solution)/shard_map/ppermute | solution.py:60
  113.6 26.8 %slice-start = ((s8[9437184]{0:T(1024)(128)(4,1)}), s8[4194304]{0:T(1024)(128)(4,1)S(1)}, s32[]{:S(2)}) async-start(s8[9437184]{0:T(1024)(128)(4,1)} %bitcast.8), calls=%async_computation | async-start | bytes 8388608
  113.6 26.8 %slice-start.1 = ((s8[9437184]{0:T(1024)(128)(4,1)}), s8[4194304]{0:T(1024)(128)(4,1)S(1)}, s32[]{:S(2)}) async-start(s8[9437184]{0:T(1024)(128)(4,1)} %bitcast.8), calls=%async_computation.1 | async-start | bytes 8388608
  120.3 20.1 %copy-start.4 = (bf16[1536]{0:T(1024)(128)(2,1)S(1)}, bf16[1536]{0:T(1024)(128)(2,1)}, u32[]{:S(2)}) copy-start(bf16[1536]{0:T(1024)(128)(2,1)} %param.9) | copy-start | bytes 9220
  120.3 20.2 %slice-start.2 = ((s8[9437184]{0:T(1024)(128)(4,1)}), s8[1048576]{0:T(1024)(128)(4,1)S(1)}, s32[]{:S(2)}) async-start(s8[9437184]{0:T(1024)(128)(4,1)} %bitcast.8), calls=%async_computation.2 | async-start | bytes 2097152
  124.2 7.8 %collective-permute-start.17 = (bf16[256,384]{1,0:T(8,128)(2,1)S(1)}, bf16[256,384]{1,0:T(8,128)(2,1)S(1)}, u32[]{:S(2)}, u32[]{:S(2)}) collective-permute-start(bf16[256,384]{1,0:T(8,128)(2,1)S(1)} %get-tuple-element.45), channel_id=1, source_target_pairs={{0,0},{1,1},{2,2},{3,3},{4,4},{5,5},{6,6},{7,7},{8,8},{9,9},{10,10... | collective-permute-start | bytes 589832 | tf_op jit(solution)/shard_map/ppermute | solution.py:60
  126.2 8.8 %collective-permute-start.18 = (bf16[256,384]{1,0:T(8,128)(2,1)S(1)}, bf16[256,384]{1,0:T(8,128)(2,1)S(1)}, u32[]{:S(2)}, u32[]{:S(2)}) collective-permute-start(bf16[256,384]{1,0:T(8,128)(2,1)S(1)} %get-tuple-element.46), channel_id=1, source_target_pairs={{0,9},{1,8},{2,11},{3,10},{4,13},{5,12},{6,15},{7,14},{8,0},{9,1},... | collective-permute-start | bytes 589832 | tf_op jit(solution)/shard_map/ppermute | solution.py:60
  128.0 10.7 %collective-permute-start.19 = (bf16[256,384]{1,0:T(8,128)(2,1)S(1)}, bf16[256,384]{1,0:T(8,128)(2,1)S(1)}, u32[]{:S(2)}, u32[]{:S(2)}) collective-permute-start(bf16[256,384]{1,0:T(8,128)(2,1)S(1)} %get-tuple-element.47), channel_id=1, source_target_pairs={{0,1},{1,0},{2,3},{3,2},{4,5},{5,4},{6,7},{7,6},{8,9},{9,8},{10,11... | collective-permute-start | bytes 589832 | tf_op jit(solution)/shard_map/ppermute | solution.py:60
  131.1 8.5 %collective-permute-start.20 = (bf16[256,384]{1,0:T(8,128)(2,1)S(1)}, bf16[256,384]{1,0:T(8,128)(2,1)S(1)}, u32[]{:S(2)}, u32[]{:S(2)}) collective-permute-start(bf16[256,384]{1,0:T(8,128)(2,1)S(1)} %get-tuple-element.48), channel_id=1, source_target_pairs={{0,8},{1,9},{2,10},{3,11},{4,12},{5,13},{6,14},{7,15},{8,1},{9,0},... | collective-permute-start | bytes 589832 | tf_op jit(solution)/shard_map/ppermute | solution.py:60
  140.3 2.4 %collective-permute-start.21 = (bf16[256,1536]{1,0:T(8,128)(2,1)S(1)}, bf16[256,1536]{1,0:T(8,128)(2,1)S(1)}, u32[]{:S(2)}, u32[]{:S(2)}) collective-permute-start(bf16[256,1536]{1,0:T(8,128)(2,1)S(1)} %shard_map.61.joined), channel_id=1, source_target_pairs={{0,64},{1,65},{2,66},{3,67},{4,68},{5,69},{6,70},{7,71},{8,72},{9,... | collective-permute-start | bytes 2359304 | tf_op jit(solution)/shard_map/ppermute | solution.py:60

commit v4 on v3

--- a/solution.py
+++ b/solution.py
@@ -1,3 +1,4 @@
+import functools
 import math
 
 import jax
@@ -56,6 +57,14 @@
     return (core, 3 - y, z, x) if core == 1 else None
 
 
+def to_near(core, y, z, x):
+    return core, y, z, x ^ 1
+
+
+def to_far(core, y, z, x):
+    return (core, y, z, 3 - x) if x in (1, 2) else None
+
+
 def send(x, perm):
     return lax.ppermute(x, AXES, perm)
 
@@ -86,23 +95,31 @@
             )
 
 
+def placed():
+    wide = lax.axis_index("wa")
+    return (wide & 1) * 2 + lax.axis_index("ha"), lax.axis_index("grp"), wide >> 1, lax.axis_index("ta")
+
+
+def here_body(body, *refs):
+    body(placed(), *refs)
+
+
 VMEM = pl.BlockSpec(memory_space=pltpu.MemorySpace.VMEM)
-SMEM = pl.BlockSpec(memory_space=pltpu.MemorySpace.SMEM)
-
-
-def local_call(body, place, operands, shapes, flops=0, limit=24, aliases=None):
+
+
+def local_call(body, operands, shapes, flops=0, limit=24, aliases=None):
     single = not isinstance(shapes, (list, tuple))
     listed = [shapes] if single else list(shapes)
     moved = sum(math.prod(a.shape) * a.dtype.itemsize for a in list(operands) + listed)
     return pl.pallas_call(
-        body,
-        in_specs=[SMEM] + [VMEM] * len(operands),
+        functools.partial(here_body, body),
+        in_specs=[VMEM] * len(operands),
         out_specs=VMEM if single else [VMEM] * len(listed),
         out_shape=shapes,
         cost_estimate=pl.CostEstimate(flops=flops, bytes_accessed=moved, transcendentals=0),
         compiler_params=pltpu.CompilerParams(vmem_limit_bytes=limit * 1024 * 1024),
         input_output_aliases=aliases or {},
-    )(place, *operands)
+    )(*operands)
 
 
 def gather_body(place, *refs):
@@ -110,11 +127,12 @@
     for step in range(4):
         z_from = (place[0] - step + 4) % 4
         whole[z_from // 2, :, z_from % 2] = chunks[step][...]
-        for high in range(2):
-
-            @pl.when(z_from // 2 == high)
+        beside_far = z_from // 2 == place[2] % 2
+        for which, chosen in ((0, jnp.logical_not(beside_far)), (1, beside_far)):
+
+            @pl.when(chosen)
             def _():
-                halves[high][:, z_from % 2] = chunks[step][...]
+                halves[which][:, z_from % 2] = chunks[step][...]
 
 
 MIXED = jax.ShapeDtypeStruct((HEADS, 2, ROWS, 2 * TILE), F32)
@@ -183,11 +201,11 @@
     return jnp.max(sums) < LIMIT
 
 
-def redo(turned_q, mixed, peak, shares, biases=(0.0, 0.0)):
+def redo(turned_q, mixed, peak, shares, sides, biases):
     def one(head, carry):
-        for side in range(2):
-            for ref in shares[side]:
-                careful(turned_q, mixed, peak, head, side, ref, biases[side])
+        for part in range(2):
+            for ref in shares[part]:
+                careful(turned_q, mixed, peak, head, sides[part], ref, 0.0 if part == 0 else biases[1])
         return carry
 
     lax.fori_loop(0, HEADS, one, 0)
@@ -231,7 +249,9 @@
             worst = jnp.maximum(worst, fresh[HD : HD + 8])
         return worst
 
-    worst = lax.fori_loop(0, HEADS, one, jnp.zeros((8, 2 * TILE), F32))
+    worst = jnp.zeros((8, 2 * TILE), F32)
+    for head in range(HEADS):
+        worst = one(head, worst)
 
     @pl.when(jnp.logical_not(within(worst)))
     def _():
@@ -239,21 +259,26 @@
         redo_alike(turned_q, mixed, peak, (*own, *inner))
 
 
-def more(turned_q, mixed_in, mixed, peak, shares, biases=(None, None)):
+def more(turned_q, mixed_in, mixed, peak, shares, sides=(0, 1), biases=(None, None)):
     worst = None
     for head in range(HEADS):
-        for side in range(2):
-            queries = queries_of(turned_q, head, side)
+        for part in range(2):
+            side = sides[part]
             fresh = mixed_in[head, side] + quick(
-                queries, both_lows(head, *shares[side]), peak[head, side], biases[side]
+                queries_of(turned_q, head, side),
+                both_lows(head, *shares[part]),
+                peak[head, side],
+                biases[part],
             )
             mixed[head, side] = fresh
             worst = larger(worst, fresh[HD : HD + 8])
     return within(worst)
 
 
-def edge_biases(place):
-    return [jnp.where(place[2] == end, -1e30, 0.0).astype(F32) for end in (0, 3)]
+def edge_sides(place):
+    far_side = place[2] % 2
+    missing = jnp.logical_or(place[2] == 0, place[2] == 3)
+    return (1 - far_side, far_side), (None, jnp.where(missing, -1e30, 0.0).astype(F32))
 
 
 def second_body(place, *refs):
@@ -274,36 +299,37 @@
 
 
 def third_body(place, *refs):
-    left, right, turned_q, mixed_in, _, mixed, peak = refs
-    biases = edge_biases(place)
-    good = more(turned_q, mixed_in, mixed, peak, ((left,), (right,)), biases)
+    near, far, turned_q, mixed_in, _, mixed, peak = refs
+    sides, biases = edge_sides(place)
+    shares = (near,), (far,)
+    good = more(turned_q, mixed_in, mixed, peak, shares, sides, biases)
 
     @pl.when(jnp.logical_not(good))
     def _():
         copied(mixed_in, mixed)
-        redo(turned_q, mixed, peak, ((left,), (right,)), biases)
+        redo(turned_q, mixed, peak, shares, sides, biases)
 
 
 def last_body(place, *refs):
-    left, right, turned_q, mixed_in = refs[:2], refs[2:4], refs[4], refs[5]
+    near, far, turned_q, mixed_in = refs[:2], refs[2:4], refs[4], refs[5]
     outs, (peak, mixed, done) = refs[7:11], refs[11:]
-    biases = edge_biases(place)
+    sides, biases = edge_sides(place)
 
     def passes(shares):
-        good = more(turned_q, mixed_in, mixed, peak, shares, biases)
+        good = more(turned_q, mixed_in, mixed, peak, shares, sides, biases)
 
         @pl.when(jnp.logical_not(good))
         def _():
             copied(mixed_in, mixed)
-            redo(turned_q, mixed, peak, shares, biases)
+            redo(turned_q, mixed, peak, shares, sides, biases)
 
     @pl.when(place[1] == 1)
     def _():
-        passes((left, right))
+        passes((near, far))
 
     @pl.when(place[1] == 0)
     def _():
-        passes((left[:1], right[:1]))
+        passes((near[:1], far[:1]))
 
     for head in range(HEADS):
         for side in range(2):
@@ -318,19 +344,19 @@
             outs[step][:, head * HD : (head + 1) * HD] = done[z_from, head]
 
 
-def last(place, operands, flops):
+def last(operands, flops):
     out = jax.ShapeDtypeStruct((TILE, HEADS * HD), BF16)
     return pl.pallas_call(
-        last_body,
-        in_specs=[SMEM] + [VMEM] * len(operands),
+        functools.partial(here_body, last_body),
+        in_specs=[VMEM] * len(operands),
         out_specs=[VMEM] * 5,
         out_shape=[out] * 4 + [PEAK],
         scratch_shapes=[pltpu.VMEM(MIXED.shape, F32), pltpu.VMEM((4, HEADS, TILE, HD), BF16)],
-        input_output_aliases={7: 4},
+        input_output_aliases={6: 4},
         cost_estimate=pl.CostEstimate(flops=flops, bytes_accessed=1 << 20, transcendentals=0),
         compiler_params=pltpu.CompilerParams(vmem_limit_bytes=24 * 1024 * 1024),
         name="last",
-    )(place, *operands)[:4]
+    )(*operands)[:4]
 
 
 def join_body(place, *refs):
@@ -361,62 +387,55 @@
 def shards(query_tiles, key_tiles, value_tiles, out_weight, gate):
     features = query_tiles.shape[4]
     q, k, v = (a.reshape(TILE, features) for a in (query_tiles, key_tiles, value_tiles))
-    core, y = lax.axis_index("grp"), lax.axis_index("ta")
-    wide = lax.axis_index("wa")
-    z, x = (wide % 2) * 2 + lax.axis_index("ha"), wide // 2
-    place = jnp.stack([z, core, x, y]).astype(jnp.int32)
     partner, outer_pairs = pairs(to_partner), pairs(to_outer)
-    to_right = pairs(lambda core, y, z, x: (core, y, z, x + 1) if x < 3 else None)
-    to_left = pairs(lambda core, y, z, x: (core, y, z, x - 1) if x > 0 else None)
+    near_pairs, far_pairs = pairs(to_near), pairs(to_far)
     upper = flat(1, 0, 0, 0)
-    right_upper, left_upper = ([p for p in perm if p[0] >= upper] for perm in (to_right, to_left))
+    near_upper, far_upper = ([p for p in perm if p[0] >= upper] for perm in (near_pairs, far_pairs))
     flops_of = lambda tiles: HEADS * 4 * TILE * tiles * TILE * 6 * HD
 
     kv_shape = jax.ShapeDtypeStruct((HEADS, 2, TILE, HD), BF16)
-    kv_sent = local_call(pack_body, place, [k, v], [kv_shape] * 4)
+    kv_sent = local_call(pack_body, [k, v], [kv_shape] * 4)
     kv = [send(kv_sent[s], out_to_heads(s)) for s in range(4)]
     q_shape = jax.ShapeDtypeStruct((HEADS, TILE, HD), BF16)
-    q_sent = local_call(pack_q_body, place, [q], [q_shape] * 4)
+    q_sent = local_call(pack_q_body, [q], [q_shape] * 4)
     queries = [send(q_sent[s], out_to_heads(s)) for s in range(4)]
     weight_away = local_call(
-        cut_body, place, [out_weight], jax.ShapeDtypeStruct((features, features), BF16)
+        cut_body, [out_weight], jax.ShapeDtypeStruct((features, features), BF16)
     )
     weight_other = send(weight_away, partner)
     half = (HEADS, 2, 2, TILE, HD)
     *own, whole = local_call(
-        gather_body, place, kv,
+        gather_body, kv,
         [jax.ShapeDtypeStruct(half, BF16)] * 2 + [jax.ShapeDtypeStruct((2, *half), BF16)],
     )
     outer = [send(own[i], outer_pairs) for i in range(2)]
     inner = send(whole, partner)
-    right, left = send(own[0], to_left), send(own[1], to_right)
-    state = local_call(
-        first_body, place, [*own, inner, *queries], [TURNED, MIXED, PEAK], flops_of(8)
-    )
+    near, far = send(own[0], near_pairs), send(own[1], far_pairs)
+    state = local_call(first_body, [*own, inner, *queries], [TURNED, MIXED, PEAK], flops_of(8))
     turned_q, mixed, peak = state
-    right_outer = send(outer[0], left_upper)
-    left_outer = send(outer[1], right_upper)
+    near_outer = send(outer[0], near_upper)
+    far_outer = send(outer[1], far_upper)
     mixed, peak = local_call(
-        second_body, place, [*outer, turned_q, mixed, peak], [MIXED, PEAK],
-        flops_of(4), aliases={5: 1},
-    )
-    right_inner, left_inner = send(right, partner), send(left, partner)
+        second_body, [*outer, turned_q, mixed, peak], [MIXED, PEAK],
+        flops_of(4), aliases={4: 1},
+    )
+    near_inner, far_inner = send(near, partner), send(far, partner)
     mixed, peak = local_call(
-        third_body, place, [left, right, turned_q, mixed, peak],
-        [MIXED, PEAK], flops_of(2), aliases={5: 1},
+        third_body, [near, far, turned_q, mixed, peak],
+        [MIXED, PEAK], flops_of(2), aliases={4: 1},
     )
     outs = last(
-        place, [left_inner, left_outer, right_inner, right_outer, turned_q, mixed, peak], flops_of(4)
+        [near_inner, near_outer, far_inner, far_outer, turned_q, mixed, peak], flops_of(4)
     )
     chunks = [send(outs[s], back_to_tiles(s)) for s in range(4)]
-    joined = local_call(join_body, place, chunks, jax.ShapeDtypeStruct((TILE, features), BF16))
+    joined = local_call(join_body, chunks, jax.ShapeDtypeStruct((TILE, features), BF16))
     arrived = send(joined, partner)
     flops = 2 * TILE * features * features
     here = local_call(
-        home_body, place, [joined, out_weight], jax.ShapeDtypeStruct((TILE, features), F32), flops
+        home_body, [joined, out_weight], jax.ShapeDtypeStruct((TILE, features), F32), flops
     )
     branch = local_call(
-        close_body, place, [here, arrived, weight_other, gate.reshape(1, -1)],
+        close_body, [here, arrived, weight_other, gate.reshape(1, -1)],
         jax.ShapeDtypeStruct((TILE, features), BF16), flops,
     )
     return branch.reshape(1, 1, 1, TILE, features)

time: 146 us -> 138 us (0.945)
  Pallas kernels: 49.9 us -> 43.8 us
  starting transfers between devices: 48.5 us -> 46.6 us
    pallas_call x11, Pallas kernels: 49.9 us -> 43.8 us  [the longest x10 40.2 us: local_call(): pl.pallas_call(functools.partial(here_body, body), in_specs=[VMEM] * len(...]
    ppermute x23, starting transfers between devices: 48.5 us -> 46.6 us  [send(): return lax.ppermute(x, AXES, perm)]
  transfers between devices with their start and end apart: 23 -> 23, of which waited for: 14 -> 13; matrix products, arithmetic and copies ran while one was open for 0% -> 0% of each run, Pallas kernels for 32% -> 30%
where the time goes in v4:
time: 138 us
  starting transfers between devices  46.6 us (34%)
  Pallas kernels  43.8 us (32%)
  waiting for transfers between devices  43.5 us (32%)
  local copies, waits for them, and re-layouts  3.73 us (3%)
    ppermute x23, starting transfers between devices, send(): return lax.ppermute(x, AXES, perm)  46.6 us
    ppermute x23, waiting for transfers between devices, send(): return lax.ppermute(x, AXES, perm)  43.5 us
    pallas_call x10, Pallas kernels, local_call(): pl.pallas_call(functools.partial(here_body, body), in_specs=[VMEM] * len(...  40.2 us
    unnamed x16, local copies, waits for them, and re-layouts  3.72 us
    pallas_call x1, Pallas kernels, last(): pl.pallas_call(functools.partial(here_body, last_body), in_specs=[VMEM] *...  3.6 us
  transfers between devices with their start and end apart: 23, of which 13 were waited for; matrix products, arithmetic and copies ran while one was open for 0% of the time, Pallas kernels for 30%

profile of v4, /device:TPU:1, one launch (start us, length us, event | category | flops | bytes accessed | tf_op | source)
XLA Modules:
  0.0 137.9 jit_solution(3337111532871333349)
XLA Ops:
  0.0 3.7 %copy-done = bf16[1536,3072]{1,0:T(8,128)(2,1)S(1)} copy-done((bf16[1536,3072]{1,0:T(8,128)(2,1)S(1)}, bf16[1536,3072]{1,0:T(8,128)(2,1)}, u32[]{:S(2)}) %copy-start) | copy-done | bytes 9437208
  3.7 0.3 shard_map.63
  4.0 0.0 copy-start.3
  4.0 1.5 %collective-permute-start.22 = (bf16[1536,1536]{1,0:T(8,128)(2,1)S(1)}, bf16[1536,1536]{1,0:T(8,128)(2,1)S(1)}, u32[]{:S(2)}, u32[]{:S(2)}) collective-permute-start(bf16[1536,1536]{1,0:T(8,128)(2,1)S(1)} %shard_map.63), channel_id=1, source_target_pairs={{0,64},{1,65},{2,66},{3,67},{4,68},{5,69},{6,70},{7,71},{8,72},{9,... | collective-permute-start | bytes 14155784 | tf_op jit(solution)/shard_map/ppermute | solution.py:69
  5.5 0.0 copy-done.1
  5.5 0.3 shard_map.55
  5.8 4.1 %collective-permute-start = (bf16[3,2,256,128]{3,2,1,0:T(8,128)(2,1)S(1)}, bf16[3,2,256,128]{3,2,1,0:T(8,128)(2,1)S(1)}, u32[]{:S(2)}, u32[]{:S(2)}) collective-permute-start(bf16[3,2,256,128]{3,2,1,0:T(8,128)(2,1)S(1)} %get-tuple-element.27), channel_id=1, source_target_pairs={{0,0},{1,1},{2,2},{3,3},{4,4},{5,5},{6,6},{7,7},{8,8},{9,9},{10,10... | collective-permute-start | bytes 1179656 | tf_op jit(solution)/shard_map/ppermute | solution.py:69
  9.9 1.4 %collective-permute-start.1 = (bf16[3,2,256,128]{3,2,1,0:T(8,128)(2,1)S(1)}, bf16[3,2,256,128]{3,2,1,0:T(8,128)(2,1)S(1)}, u32[]{:S(2)}, u32[]{:S(2)}) collective-permute-start(bf16[3,2,256,128]{3,2,1,0:T(8,128)(2,1)S(1)} %get-tuple-element.28), channel_id=1, source_target_pairs={{0,8},{1,9},{2,10},{3,11},{4,12},{5,13},{6,14},{7,15},{8,1},{9,0},... | collective-permute-start | bytes 1179656 | tf_op jit(solution)/shard_map/ppermute | solution.py:69
  11.4 4.8 %collective-permute-start.2 = (bf16[3,2,256,128]{3,2,1,0:T(8,128)(2,1)S(1)}, bf16[3,2,256,128]{3,2,1,0:T(8,128)(2,1)S(1)}, u32[]{:S(2)}, u32[]{:S(2)}) collective-permute-start(bf16[3,2,256,128]{3,2,1,0:T(8,128)(2,1)S(1)} %get-tuple-element.29), channel_id=1, source_target_pairs={{0,1},{1,0},{2,3},{3,2},{4,5},{5,4},{6,7},{7,6},{8,9},{9,8},{10,11... | collective-permute-start | bytes 1179656 | tf_op jit(solution)/shard_map/ppermute | solution.py:69
  16.1 0.5 collective-permute-start.3
  16.6 0.0 collective-permute-done.refs_0_
  16.6 6.8 %collective-permute-done.1.refs_1_ = bf16[3,2,256,128]{3,2,1,0:T(8,128)(2,1)S(1)} collective-permute-done((bf16[3,2,256,128]{3,2,1,0:T(8,128)(2,1)S(1)}, bf16[3,2,256,128]{3,2,1,0:T(8,128)(2,1)S(1)}, u32[]{:S(2)}, u32[]{:S(2)}) %collective-permute-start.1) | collective-permute-done | bytes 393248 | tf_op jit(solution)/shard_map/ppermute | solution.py:69
  23.4 3.9 %collective-permute-done.2.refs_2_ = bf16[3,2,256,128]{3,2,1,0:T(8,128)(2,1)S(1)} collective-permute-done((bf16[3,2,256,128]{3,2,1,0:T(8,128)(2,1)S(1)}, bf16[3,2,256,128]{3,2,1,0:T(8,128)(2,1)S(1)}, u32[]{:S(2)}, u32[]{:S(2)}) %collective-permute-start.2) | collective-permute-done | bytes 393248 | tf_op jit(solution)/shard_map/ppermute | solution.py:69
  27.3 2.5 %collective-permute-done.3.refs_3_ = bf16[3,2,256,128]{3,2,1,0:T(8,128)(2,1)S(1)} collective-permute-done((bf16[3,2,256,128]{3,2,1,0:T(8,128)(2,1)S(1)}, bf16[3,2,256,128]{3,2,1,0:T(8,128)(2,1)S(1)}, u32[]{:S(2)}, u32[]{:S(2)}) %collective-permute-start.3) | collective-permute-done | bytes 393248 | tf_op jit(solution)/shard_map/ppermute | solution.py:69
  29.8 0.3 shard_map.56
  30.1 4.5 %collective-permute-start.10 = (bf16[3,2,2,256,128]{4,3,2,1,0:T(8,128)(2,1)S(1)}, bf16[3,2,2,256,128]{4,3,2,1,0:T(8,128)(2,1)S(1)}, u32[]{:S(2)}, u32[]{:S(2)}) collective-permute-start(bf16[3,2,2,256,128]{4,3,2,1,0:T(8,128)(2,1)S(1)} %get-tuple-element.32.refs_1_), channel_id=1, source_target_pairs={{64,112},{65,113},{66,114},{67,115},{68,116},{69,117},{70,118},{71... | collective-permute-start | bytes 2359304 | tf_op jit(solution)/shard_map/ppermute | solution.py:69
  34.6 0.1 collective-permute-start.12
  34.7 0.3 shard_map.57
  35.0 2.2 %collective-permute-start.13 = (bf16[3,256,128]{2,1,0:T(8,128)(2,1)S(1)}, bf16[3,256,128]{2,1,0:T(8,128)(2,1)S(1)}, u32[]{:S(2)}, u32[]{:S(2)}) collective-permute-start(bf16[3,256,128]{2,1,0:T(8,128)(2,1)S(1)} %get-tuple-element.34), channel_id=1, source_target_pairs={{0,0},{1,1},{2,2},{3,3},{4,4},{5,5},{6,6},{7,7},{8,8},{9,9},{10,10... | collective-permute-start | bytes 589832 | tf_op jit(solution)/shard_map/ppermute | solution.py:69
  37.2 3.6 %collective-permute-start.14 = (bf16[3,256,128]{2,1,0:T(8,128)(2,1)S(1)}, bf16[3,256,128]{2,1,0:T(8,128)(2,1)S(1)}, u32[]{:S(2)}, u32[]{:S(2)}) collective-permute-start(bf16[3,256,128]{2,1,0:T(8,128)(2,1)S(1)} %get-tuple-element.35), channel_id=1, source_target_pairs={{0,8},{1,9},{2,10},{3,11},{4,12},{5,13},{6,14},{7,15},{8,1},{9,0},... | collective-permute-start | bytes 589832 | tf_op jit(solution)/shard_map/ppermute | solution.py:69
  40.8 1.5 %collective-permute-done.13.refs_3_ = bf16[3,256,128]{2,1,0:T(8,128)(2,1)S(1)} collective-permute-done((bf16[3,256,128]{2,1,0:T(8,128)(2,1)S(1)}, bf16[3,256,128]{2,1,0:T(8,128)(2,1)S(1)}, u32[]{:S(2)}, u32[]{:S(2)}) %collective-permute-start.13) | collective-permute-done | bytes 196640 | tf_op jit(solution)/shard_map/ppermute | solution.py:69
  42.3 2.5 %collective-permute-start.15 = (bf16[3,256,128]{2,1,0:T(8,128)(2,1)S(1)}, bf16[3,256,128]{2,1,0:T(8,128)(2,1)S(1)}, u32[]{:S(2)}, u32[]{:S(2)}) collective-permute-start(bf16[3,256,128]{2,1,0:T(8,128)(2,1)S(1)} %get-tuple-element.36), channel_id=1, source_target_pairs={{0,1},{1,0},{2,3},{3,2},{4,5},{5,4},{6,7},{7,6},{8,9},{9,8},{10,11... | collective-permute-start | bytes 589832 | tf_op jit(solution)/shard_map/ppermute | solution.py:69
  44.8 2.4 %collective-permute-done.14.refs_4_ = bf16[3,256,128]{2,1,0:T(8,128)(2,1)S(1)} collective-permute-done((bf16[3,256,128]{2,1,0:T(8,128)(2,1)S(1)}, bf16[3,256,128]{2,1,0:T(8,128)(2,1)S(1)}, u32[]{:S(2)}, u32[]{:S(2)}) %collective-permute-start.14) | collective-permute-done | bytes 196640 | tf_op jit(solution)/shard_map/ppermute | solution.py:69
  47.2 1.0 collective-permute-start.16
  48.3 1.5 %collective-permute-done.15.refs_5_ = bf16[3,256,128]{2,1,0:T(8,128)(2,1)S(1)} collective-permute-done((bf16[3,256,128]{2,1,0:T(8,128)(2,1)S(1)}, bf16[3,256,128]{2,1,0:T(8,128)(2,1)S(1)}, u32[]{:S(2)}, u32[]{:S(2)}) %collective-permute-start.15) | collective-permute-done | bytes 196640 | tf_op jit(solution)/shard_map/ppermute | solution.py:69
  49.8 2.5 %collective-permute-start.6 = (bf16[3,2,2,256,128]{4,3,2,1,0:T(8,128)(2,1)S(1)}, bf16[3,2,2,256,128]{4,3,2,1,0:T(8,128)(2,1)S(1)}, u32[]{:S(2)}, u32[]{:S(2)}) collective-permute-start(bf16[3,2,2,256,128]{4,3,2,1,0:T(8,128)(2,1)S(1)} %get-tuple-element.31.refs_0_), channel_id=1, source_target_pairs={{64,112},{65,113},{66,114},{67,115},{68,116},{69,117},{70,118},{71... | collective-permute-start | bytes 2359304 | tf_op jit(solution)/shard_map/ppermute | solution.py:69
  52.3 1.0 collective-permute-done.16.refs_6_
  53.3 1.2 collective-permute-start.4
  54.5 0.0 collective-permute-done.10.refs_1_
  54.5 0.7 collective-permute-start.8
  55.2 8.5 %collective-permute-done.6.refs_0_ = bf16[3,2,2,256,128]{4,3,2,1,0:T(8,128)(2,1)S(1)} collective-permute-done((bf16[3,2,2,256,128]{4,3,2,1,0:T(8,128)(2,1)S(1)}, bf16[3,2,2,256,128]{4,3,2,1,0:T(8,128)(2,1)S(1)}, u32[]{:S(2)}, u32[]{:S(2)}) %collective-permute-start.6) | collective-permute-done | bytes 786464 | tf_op jit(solution)/shard_map/ppermute | solution.py:69
  63.7 0.7 collective-permute-start.11
  64.4 6.9 %collective-permute-done.4.refs_0_ = bf16[3,2,2,256,128]{4,3,2,1,0:T(8,128)(2,1)S(1)} collective-permute-done((bf16[3,2,2,256,128]{4,3,2,1,0:T(8,128)(2,1)S(1)}, bf16[3,2,2,256,128]{4,3,2,1,0:T(8,128)(2,1)S(1)}, u32[]{:S(2)}, u32[]{:S(2)}) %collective-permute-start.4) | collective-permute-done | bytes 786464 | tf_op jit(solution)/shard_map/ppermute | solution.py:69
  71.4 1.9 %collective-permute-start.5 = (bf16[3,2,2,256,128]{4,3,2,1,0:T(8,128)(2,1)S(1)}, bf16[3,2,2,256,128]{4,3,2,1,0:T(8,128)(2,1)S(1)}, u32[]{:S(2)}, u32[]{:S(2)}) collective-permute-start(bf16[3,2,2,256,128]{4,3,2,1,0:T(8,128)(2,1)S(1)} %collective-permute-done.4.refs_0_), channel_id=1, source_target_pairs={{0,64},{1,65},{2,66},{3,67},{4,68},{5,69},{6,70},{7,71},{8,72},{9,... | collective-permute-start | bytes 2359304 | tf_op jit(solution)/shard_map/ppermute | solution.py:69
  73.3 0.0 collective-permute-done.8.refs_1_
  73.3 3.7 %collective-permute-start.7 = (bf16[3,2,2,256,128]{4,3,2,1,0:T(8,128)(2,1)S(1)}, bf16[3,2,2,256,128]{4,3,2,1,0:T(8,128)(2,1)S(1)}, u32[]{:S(2)}, u32[]{:S(2)}) collective-permute-start(bf16[3,2,2,256,128]{4,3,2,1,0:T(8,128)(2,1)S(1)} %collective-permute-done.6.refs_0_), channel_id=1, source_target_pairs={{64,66},{65,67},{66,64},{67,65},{68,70},{69,71},{70,68},{71,69},{7... | collective-permute-start | bytes 2359304 | tf_op jit(solution)/shard_map/ppermute | solution.py:69
  77.0 0.0 collective-permute-done.12.refs_2_
  77.0 0.1 collective-permute-start.9
  77.1 30.0 %shard_map.58 = (bf16[3,4,256,256]{3,2,1,0:T(8,128)(2,1)S(1)}, f32[3,2,144,512]{3,2,1,0:T(8,128)S(1)}, f32[3,2,1,512]{3,2,1,0:T(1,128)S(1)}) custom-call(bf16[3,2,2,256,128]{4,3,2,1,0:T(8,128)(2,1)S(1)} %get-tuple-element.31.refs_0_, bf16[3,2,2,256,128]{4,3,2,1,0:T(8,128)(2,1)S(1)} %get-tuple-element.32.refs_1_, ...), custom_call_target="tpu_custom_call" | custom-call | flops 4831838208 | bytes 7286784 | tf_op jit(solution)/shard_map/pallas_call | solution.py:114
  107.1 0.0 slice-start
  107.1 0.0 slice-start.1
  107.1 3.0 %shard_map.59 = (f32[3,2,144,512]{3,2,1,0:T(8,128)S(1)}, f32[3,2,1,512]{3,2,1,0:T(1,128)S(1)}) custom-call(bf16[3,2,2,256,128]{4,3,2,1,0:T(8,128)(2,1)S(1)} %collective-permute-done.6.refs_0_, bf16[3,2,2,256,128]{4,3,2,1,0:T(8,128)(2,1)S(1)} %collective-permute-done.10.refs_1_, ...), custom_call_target="tpu_custom_call", output_to_operand_aliasing={{1}: (4, {})} | custom-call | flops 2415919104 | bytes 6709248 | tf_op jit(solution)/shard_map/pallas_call | solution.py:114
  110.1 2.3 %shard_map.60 = (f32[3,2,144,512]{3,2,1,0:T(8,128)S(1)}, f32[3,2,1,512]{3,2,1,0:T(1,128)S(1)}) custom-call(bf16[3,2,2,256,128]{4,3,2,1,0:T(8,128)(2,1)S(1)} %collective-permute-done.4.refs_0_, bf16[3,2,2,256,128]{4,3,2,1,0:T(8,128)(2,1)S(1)} %collective-permute-done.8.refs_1_, ...), custom_call_target="tpu_custom_call", output_to_operand_aliasing={{1}: (4, {})} | custom-call | flops 1207959552 | bytes 6709248 | tf_op jit(solution)/shard_map/pallas_call | solution.py:114
  112.4 0.0 collective-permute-done.11.refs_3_
  112.5 0.0 collective-permute-done.5.refs_0_
  112.5 0.0 collective-permute-done.7.refs_1_
  112.5 0.0 collective-permute-done.9.refs_2_
  112.5 0.0 copy-start.4
  112.5 0.0 slice-start.2
  112.5 3.6 %last.1 = (bf16[256,384]{1,0:T(8,128)(2,1)S(1)}, bf16[256,384]{1,0:T(8,128)(2,1)S(1)}, bf16[256,384]{1,0:T(8,128)(2,1)S(1)}, bf16[256,384]{1,0:T(8,128)(2,1)S(1)}, f32[3,2,1,512]{3,2,1,0:T(1,128)S(1)}) custom-call(bf16[3,2,2,256,128]{4,3,2,1,0:T(8,128)(2,1)S(1)} %collective-permute-done.5.refs_0_, ...), custom_call_target="tpu_custom_call", output_to_operand_aliasing={{4}: (6, {})} | custom-call | flops 2415919104 | bytes 1048576 | tf_op jit(solution)/shard_map/last/pallas_call | solution.py:349
  116.1 1.9 %collective-permute-start.17 = (bf16[256,384]{1,0:T(8,128)(2,1)S(1)}, bf16[256,384]{1,0:T(8,128)(2,1)S(1)}, u32[]{:S(2)}, u32[]{:S(2)}) collective-permute-start(bf16[256,384]{1,0:T(8,128)(2,1)S(1)} %get-tuple-element.45), channel_id=1, source_target_pairs={{0,0},{1,1},{2,2},{3,3},{4,4},{5,5},{6,6},{7,7},{8,8},{9,9},{10,10... | collective-permute-start | bytes 589832 | tf_op jit(solution)/shard_map/ppermute | solution.py:69
  118.0 2.8 %collective-permute-start.18 = (bf16[256,384]{1,0:T(8,128)(2,1)S(1)}, bf16[256,384]{1,0:T(8,128)(2,1)S(1)}, u32[]{:S(2)}, u32[]{:S(2)}) collective-permute-start(bf16[256,384]{1,0:T(8,128)(2,1)S(1)} %get-tuple-element.46), channel_id=1, source_target_pairs={{0,9},{1,8},{2,11},{3,10},{4,13},{5,12},{6,15},{7,14},{8,0},{9,1},... | collective-permute-start | bytes 589832 | tf_op jit(solution)/shard_map/ppermute | solution.py:69
  120.9 3.8 %collective-permute-start.19 = (bf16[256,384]{1,0:T(8,128)(2,1)S(1)}, bf16[256,384]{1,0:T(8,128)(2,1)S(1)}, u32[]{:S(2)}, u32[]{:S(2)}) collective-permute-start(bf16[256,384]{1,0:T(8,128)(2,1)S(1)} %get-tuple-element.47), channel_id=1, source_target_pairs={{0,1},{1,0},{2,3},{3,2},{4,5},{5,4},{6,7},{7,6},{8,9},{9,8},{10,11... | collective-permute-start | bytes 589832 | tf_op jit(solution)/shard_map/ppermute | solution.py:69
  124.7 0.8 collective-permute-start.20
  125.5 0.0 collective-permute-done.17.refs_0_
  125.5 3.0 %collective-permute-done.18.refs_1_ = bf16[256,384]{1,0:T(8,128)(2,1)S(1)} collective-permute-done((bf16[256,384]{1,0:T(8,128)(2,1)S(1)}, bf16[256,384]{1,0:T(8,128)(2,1)S(1)}, u32[]{:S(2)}, u32[]{:S(2)}) %collective-permute-start.18) | collective-permute-done | bytes 196640 | tf_op jit(solution)/shard_map/ppermute | solution.py:69
  128.5 3.7 %collective-permute-done.19.refs_2_ = bf16[256,384]{1,0:T(8,128)(2,1)S(1)} collective-permute-done((bf16[256,384]{1,0:T(8,128)(2,1)S(1)}, bf16[256,384]{1,0:T(8,128)(2,1)S(1)}, u32[]{:S(2)}, u32[]{:S(2)}) %collective-permute-start.19) | collective-permute-done | bytes 196640 | tf_op jit(solution)/shard_map/ppermute | solution.py:69
  132.2 0.9 collective-permute-done.20.refs_3_
  133.1 0.1 shard_map.61.refs_0_
  133.3 0.1 collective-permute-start.21
  133.5 1.4 %shard_map.62.refs_0_ = f32[256,1536]{1,0:T(8,128)S(1)} custom-call(bf16[256,1536]{1,0:T(8,128)(2,1)S(1)} %shard_map.61.refs_0_, bf16[1536,3072]{1,0:T(8,128)(2,1)S(1)} %bitcast.5), custom_call_target="tpu_custom_call" | custom-call | flops 1207959552 | bytes 11796480 | tf_op jit(solution)/shard_map/pallas_call | solution.py:114
  134.9 0.8 collective-permute-done.21.refs_1_
  135.7 0.0 collective-permute-done.22.refs_2_
  135.7 2.3 %shard_map.64 = bf16[256,1536]{1,0:T(8,128)(2,1)} custom-call(f32[256,1536]{1,0:T(8,128)S(1)} %shard_map.62.refs_0_, bf16[256,1536]{1,0:T(8,128)(2,1)S(1)} %collective-permute-done.21.refs_1_, bf16[1536,1536]{1,0:T(8,128)(2,1)S(1)} %collective-permute-done.22.refs_2_, bf16[1,1536]{1,0:T(2,128)(2,1)S(1)} %reshape.18.refs_3_), custom_call_target="tpu_custom_call" | custom-call | flops 1207959552 | bytes 7867392 | tf_op jit(solution)/shard_map/pallas_call | solution.py:114
  (11 shorter events, 0.0 us)
Async XLA Ops:
  0.0 3.7 %copy-start = (bf16[1536,3072]{1,0:T(8,128)(2,1)S(1)}, bf16[1536,3072]{1,0:T(8,128)(2,1)}, u32[]{:S(2)}) copy-start(bf16[1536,3072]{1,0:T(8,128)(2,1)} %refs_0_.1) | copy-start | bytes 28311556
  3.7 1.8 %copy-start.1 = (bf16[1,1,1,256,1536]{4,3,2,1,0:T(8,128)(2,1)S(1)}, bf16[1,1,1,256,1536]{4,3,2,1,0:T(8,128)(2,1)}, u32[]{:S(2)}) copy-start(bf16[1,1,1,256,1536]{4,3,2,1,0:T(8,128)(2,1)} %param.6) | copy-start | bytes 2359300
  3.7 1.8 %copy-start.2 = (bf16[1,1,1,256,1536]{4,3,2,1,0:T(8,128)(2,1)S(1)}, bf16[1,1,1,256,1536]{4,3,2,1,0:T(8,128)(2,1)}, u32[]{:S(2)}) copy-start(bf16[1,1,1,256,1536]{4,3,2,1,0:T(8,128)(2,1)} %param.7) | copy-start | bytes 2359300
  4.0 30.7 %copy-start.3 = (bf16[1,1,1,256,1536]{4,3,2,1,0:T(8,128)(2,1)S(1)}, bf16[1,1,1,256,1536]{4,3,2,1,0:T(8,128)(2,1)}, u32[]{:S(2)}) copy-start(bf16[1,1,1,256,1536]{4,3,2,1,0:T(8,128)(2,1)} %param.5) | copy-start | bytes 2359300
  4.0 131.6 %collective-permute-start.22 = (bf16[1536,1536]{1,0:T(8,128)(2,1)S(1)}, bf16[1536,1536]{1,0:T(8,128)(2,1)S(1)}, u32[]{:S(2)}, u32[]{:S(2)}) collective-permute-start(bf16[1536,1536]{1,0:T(8,128)(2,1)S(1)} %shard_map.63), channel_id=1, source_target_pairs={{0,64},{1,65},{2,66},{3,67},{4,68},{5,69},{6,70},{7,71},{8,72},{9,... | collective-permute-start | bytes 14155784 | tf_op jit(solution)/shard_map/ppermute | solution.py:69
  5.8 10.8 %collective-permute-start = (bf16[3,2,256,128]{3,2,1,0:T(8,128)(2,1)S(1)}, bf16[3,2,256,128]{3,2,1,0:T(8,128)(2,1)S(1)}, u32[]{:S(2)}, u32[]{:S(2)}) collective-permute-start(bf16[3,2,256,128]{3,2,1,0:T(8,128)(2,1)S(1)} %get-tuple-element.27), channel_id=1, source_target_pairs={{0,0},{1,1},{2,2},{3,3},{4,4},{5,5},{6,6},{7,7},{8,8},{9,9},{10,10... | collective-permute-start | bytes 1179656 | tf_op jit(solution)/shard_map/ppermute | solution.py:69
  9.9 13.4 %collective-permute-start.1 = (bf16[3,2,256,128]{3,2,1,0:T(8,128)(2,1)S(1)}, bf16[3,2,256,128]{3,2,1,0:T(8,128)(2,1)S(1)}, u32[]{:S(2)}, u32[]{:S(2)}) collective-permute-start(bf16[3,2,256,128]{3,2,1,0:T(8,128)(2,1)S(1)} %get-tuple-element.28), channel_id=1, source_target_pairs={{0,8},{1,9},{2,10},{3,11},{4,12},{5,13},{6,14},{7,15},{8,1},{9,0},... | collective-permute-start | bytes 1179656 | tf_op jit(solution)/shard_map/ppermute | solution.py:69
  11.4 15.9 %collective-permute-start.2 = (bf16[3,2,256,128]{3,2,1,0:T(8,128)(2,1)S(1)}, bf16[3,2,256,128]{3,2,1,0:T(8,128)(2,1)S(1)}, u32[]{:S(2)}, u32[]{:S(2)}) collective-permute-start(bf16[3,2,256,128]{3,2,1,0:T(8,128)(2,1)S(1)} %get-tuple-element.29), channel_id=1, source_target_pairs={{0,1},{1,0},{2,3},{3,2},{4,5},{5,4},{6,7},{7,6},{8,9},{9,8},{10,11... | collective-permute-start | bytes 1179656 | tf_op jit(solution)/shard_map/ppermute | solution.py:69
  16.1 13.7 %collective-permute-start.3 = (bf16[3,2,256,128]{3,2,1,0:T(8,128)(2,1)S(1)}, bf16[3,2,256,128]{3,2,1,0:T(8,128)(2,1)S(1)}, u32[]{:S(2)}, u32[]{:S(2)}) collective-permute-start(bf16[3,2,256,128]{3,2,1,0:T(8,128)(2,1)S(1)} %get-tuple-element.30), channel_id=1, source_target_pairs={{0,9},{1,8},{2,11},{3,10},{4,13},{5,12},{6,15},{7,14},{8,0},{9,1},... | collective-permute-start | bytes 1179656 | tf_op jit(solution)/shard_map/ppermute | solution.py:69
  30.1 24.4 %collective-permute-start.10 = (bf16[3,2,2,256,128]{4,3,2,1,0:T(8,128)(2,1)S(1)}, bf16[3,2,2,256,128]{4,3,2,1,0:T(8,128)(2,1)S(1)}, u32[]{:S(2)}, u32[]{:S(2)}) collective-permute-start(bf16[3,2,2,256,128]{4,3,2,1,0:T(8,128)(2,1)S(1)} %get-tuple-element.32.refs_1_), channel_id=1, source_target_pairs={{64,112},{65,113},{66,114},{67,115},{68,116},{69,117},{70,118},{71... | collective-permute-start | bytes 2359304 | tf_op jit(solution)/shard_map/ppermute | solution.py:69
  34.6 42.4 %collective-permute-start.12 = (bf16[2,3,2,2,256,128]{5,4,3,2,1,0:T(8,128)(2,1)S(1)}, bf16[2,3,2,2,256,128]{5,4,3,2,1,0:T(8,128)(2,1)S(1)}, u32[]{:S(2)}, u32[]{:S(2)}) collective-permute-start(bf16[2,3,2,2,256,128]{5,4,3,2,1,0:T(8,128)(2,1)S(1)} %get-tuple-element.33), channel_id=1, source_target_pairs={{0,64},{1,65},{2,66},{3,67},{4,68},{5,69},{6,70},{7,71},{8,72},{9,... | collective-permute-start | bytes 4718600 | tf_op jit(solution)/shard_map/ppermute | solution.py:69
  35.0 7.3 %collective-permute-start.13 = (bf16[3,256,128]{2,1,0:T(8,128)(2,1)S(1)}, bf16[3,256,128]{2,1,0:T(8,128)(2,1)S(1)}, u32[]{:S(2)}, u32[]{:S(2)}) collective-permute-start(bf16[3,256,128]{2,1,0:T(8,128)(2,1)S(1)} %get-tuple-element.34), channel_id=1, source_target_pairs={{0,0},{1,1},{2,2},{3,3},{4,4},{5,5},{6,6},{7,7},{8,8},{9,9},{10,10... | collective-permute-start | bytes 589832 | tf_op jit(solution)/shard_map/ppermute | solution.py:69
  37.2 10.0 %collective-permute-start.14 = (bf16[3,256,128]{2,1,0:T(8,128)(2,1)S(1)}, bf16[3,256,128]{2,1,0:T(8,128)(2,1)S(1)}, u32[]{:S(2)}, u32[]{:S(2)}) collective-permute-start(bf16[3,256,128]{2,1,0:T(8,128)(2,1)S(1)} %get-tuple-element.35), channel_id=1, source_target_pairs={{0,8},{1,9},{2,10},{3,11},{4,12},{5,13},{6,14},{7,15},{8,1},{9,0},... | collective-permute-start | bytes 589832 | tf_op jit(solution)/shard_map/ppermute | solution.py:69
  42.3 7.5 %collective-permute-start.15 = (bf16[3,256,128]{2,1,0:T(8,128)(2,1)S(1)}, bf16[3,256,128]{2,1,0:T(8,128)(2,1)S(1)}, u32[]{:S(2)}, u32[]{:S(2)}) collective-permute-start(bf16[3,256,128]{2,1,0:T(8,128)(2,1)S(1)} %get-tuple-element.36), channel_id=1, source_target_pairs={{0,1},{1,0},{2,3},{3,2},{4,5},{5,4},{6,7},{7,6},{8,9},{9,8},{10,11... | collective-permute-start | bytes 589832 | tf_op jit(solution)/shard_map/ppermute | solution.py:69
  47.2 6.1 %collective-permute-start.16 = (bf16[3,256,128]{2,1,0:T(8,128)(2,1)S(1)}, bf16[3,256,128]{2,1,0:T(8,128)(2,1)S(1)}, u32[]{:S(2)}, u32[]{:S(2)}) collective-permute-start(bf16[3,256,128]{2,1,0:T(8,128)(2,1)S(1)} %get-tuple-element.37), channel_id=1, source_target_pairs={{0,9},{1,8},{2,11},{3,10},{4,13},{5,12},{6,15},{7,14},{8,0},{9,1},... | collective-permute-start | bytes 589832 | tf_op jit(solution)/shard_map/ppermute | solution.py:69
  49.8 13.9 %collective-permute-start.6 = (bf16[3,2,2,256,128]{4,3,2,1,0:T(8,128)(2,1)S(1)}, bf16[3,2,2,256,128]{4,3,2,1,0:T(8,128)(2,1)S(1)}, u32[]{:S(2)}, u32[]{:S(2)}) collective-permute-start(bf16[3,2,2,256,128]{4,3,2,1,0:T(8,128)(2,1)S(1)} %get-tuple-element.31.refs_0_), channel_id=1, source_target_pairs={{64,112},{65,113},{66,114},{67,115},{68,116},{69,117},{70,118},{71... | collective-permute-start | bytes 2359304 | tf_op jit(solution)/shard_map/ppermute | solution.py:69
  53.3 18.0 %collective-permute-start.4 = (bf16[3,2,2,256,128]{4,3,2,1,0:T(8,128)(2,1)S(1)}, bf16[3,2,2,256,128]{4,3,2,1,0:T(8,128)(2,1)S(1)}, u32[]{:S(2)}, u32[]{:S(2)}) collective-permute-start(bf16[3,2,2,256,128]{4,3,2,1,0:T(8,128)(2,1)S(1)} %get-tuple-element.31.refs_0_), channel_id=1, source_target_pairs={{0,2},{1,3},{2,0},{3,1},{4,6},{5,7},{6,4},{7,5},{8,10},{9,11},{10,... | collective-permute-start | bytes 2359304 | tf_op jit(solution)/shard_map/ppermute | solution.py:69
  54.5 18.7 %collective-permute-start.8 = (bf16[3,2,2,256,128]{4,3,2,1,0:T(8,128)(2,1)S(1)}, bf16[3,2,2,256,128]{4,3,2,1,0:T(8,128)(2,1)S(1)}, u32[]{:S(2)}, u32[]{:S(2)}) collective-permute-start(bf16[3,2,2,256,128]{4,3,2,1,0:T(8,128)(2,1)S(1)} %get-tuple-element.32.refs_1_), channel_id=1, source_target_pairs={{2,4},{3,5},{4,2},{5,3},{10,12},{11,13},{12,10},{13,11},{18,20},{1... | collective-permute-start | bytes 2359304 | tf_op jit(solution)/shard_map/ppermute | solution.py:69
  63.7 48.7 %collective-permute-start.11 = (bf16[3,2,2,256,128]{4,3,2,1,0:T(8,128)(2,1)S(1)}, bf16[3,2,2,256,128]{4,3,2,1,0:T(8,128)(2,1)S(1)}, u32[]{:S(2)}, u32[]{:S(2)}) collective-permute-start(bf16[3,2,2,256,128]{4,3,2,1,0:T(8,128)(2,1)S(1)} %collective-permute-done.10.refs_1_), channel_id=1, source_target_pairs={{66,68},{67,69},{68,66},{69,67},{74,76},{75,77},{76,74},{77,75},{8... | collective-permute-start | bytes 2359304 | tf_op jit(solution)/shard_map/ppermute | solution.py:69
  71.4 41.1 %collective-permute-start.5 = (bf16[3,2,2,256,128]{4,3,2,1,0:T(8,128)(2,1)S(1)}, bf16[3,2,2,256,128]{4,3,2,1,0:T(8,128)(2,1)S(1)}, u32[]{:S(2)}, u32[]{:S(2)}) collective-permute-start(bf16[3,2,2,256,128]{4,3,2,1,0:T(8,128)(2,1)S(1)} %collective-permute-done.4.refs_0_), channel_id=1, source_target_pairs={{0,64},{1,65},{2,66},{3,67},{4,68},{5,69},{6,70},{7,71},{8,72},{9,... | collective-permute-start | bytes 2359304 | tf_op jit(solution)/shard_map/ppermute | solution.py:69
  73.3 39.2 %collective-permute-start.7 = (bf16[3,2,2,256,128]{4,3,2,1,0:T(8,128)(2,1)S(1)}, bf16[3,2,2,256,128]{4,3,2,1,0:T(8,128)(2,1)S(1)}, u32[]{:S(2)}, u32[]{:S(2)}) collective-permute-start(bf16[3,2,2,256,128]{4,3,2,1,0:T(8,128)(2,1)S(1)} %collective-permute-done.6.refs_0_), channel_id=1, source_target_pairs={{64,66},{65,67},{66,64},{67,65},{68,70},{69,71},{70,68},{71,69},{7... | collective-permute-start | bytes 2359304 | tf_op jit(solution)/shard_map/ppermute | solution.py:69
  77.0 35.4 %collective-permute-start.9 = (bf16[3,2,2,256,128]{4,3,2,1,0:T(8,128)(2,1)S(1)}, bf16[3,2,2,256,128]{4,3,2,1,0:T(8,128)(2,1)S(1)}, u32[]{:S(2)}, u32[]{:S(2)}) collective-permute-start(bf16[3,2,2,256,128]{4,3,2,1,0:T(8,128)(2,1)S(1)} %collective-permute-done.8.refs_1_), channel_id=1, source_target_pairs={{0,64},{1,65},{2,66},{3,67},{4,68},{5,69},{6,70},{7,71},{8,72},{9,... | collective-permute-start | bytes 2359304 | tf_op jit(solution)/shard_map/ppermute | solution.py:69
  107.1 26.3 %slice-start = ((s8[9437184]{0:T(1024)(128)(4,1)}), s8[4194304]{0:T(1024)(128)(4,1)S(1)}, s32[]{:S(2)}) async-start(s8[9437184]{0:T(1024)(128)(4,1)} %bitcast.4), calls=%async_computation | async-start | bytes 8388608
  107.1 26.3 %slice-start.1 = ((s8[9437184]{0:T(1024)(128)(4,1)}), s8[4194304]{0:T(1024)(128)(4,1)S(1)}, s32[]{:S(2)}) async-start(s8[9437184]{0:T(1024)(128)(4,1)} %bitcast.4), calls=%async_computation.1 | async-start | bytes 8388608
  112.5 20.9 %copy-start.4 = (bf16[1536]{0:T(1024)(128)(2,1)S(1)}, bf16[1536]{0:T(1024)(128)(2,1)}, u32[]{:S(2)}) copy-start(bf16[1536]{0:T(1024)(128)(2,1)} %param.9) | copy-start | bytes 9220
  112.5 20.9 %slice-start.2 = ((s8[9437184]{0:T(1024)(128)(4,1)}), s8[1048576]{0:T(1024)(128)(4,1)S(1)}, s32[]{:S(2)}) async-start(s8[9437184]{0:T(1024)(128)(4,1)} %bitcast.4), calls=%async_computation.2 | async-start | bytes 2097152
  116.1 9.4 %collective-permute-start.17 = (bf16[256,384]{1,0:T(8,128)(2,1)S(1)}, bf16[256,384]{1,0:T(8,128)(2,1)S(1)}, u32[]{:S(2)}, u32[]{:S(2)}) collective-permute-start(bf16[256,384]{1,0:T(8,128)(2,1)S(1)} %get-tuple-element.45), channel_id=1, source_target_pairs={{0,0},{1,1},{2,2},{3,3},{4,4},{5,5},{6,6},{7,7},{8,8},{9,9},{10,10... | collective-permute-start | bytes 589832 | tf_op jit(solution)/shard_map/ppermute | solution.py:69
  118.0 10.5 %collective-permute-start.18 = (bf16[256,384]{1,0:T(8,128)(2,1)S(1)}, bf16[256,384]{1,0:T(8,128)(2,1)S(1)}, u32[]{:S(2)}, u32[]{:S(2)}) collective-permute-start(bf16[256,384]{1,0:T(8,128)(2,1)S(1)} %get-tuple-element.46), channel_id=1, source_target_pairs={{0,9},{1,8},{2,11},{3,10},{4,13},{5,12},{6,15},{7,14},{8,0},{9,1},... | collective-permute-start | bytes 589832 | tf_op jit(solution)/shard_map/ppermute | solution.py:69
  120.9 11.3 %collective-permute-start.19 = (bf16[256,384]{1,0:T(8,128)(2,1)S(1)}, bf16[256,384]{1,0:T(8,128)(2,1)S(1)}, u32[]{:S(2)}, u32[]{:S(2)}) collective-permute-start(bf16[256,384]{1,0:T(8,128)(2,1)S(1)} %get-tuple-element.47), channel_id=1, source_target_pairs={{0,1},{1,0},{2,3},{3,2},{4,5},{5,4},{6,7},{7,6},{8,9},{9,8},{10,11... | collective-permute-start | bytes 589832 | tf_op jit(solution)/shard_map/ppermute | solution.py:69
  124.7 8.5 %collective-permute-start.20 = (bf16[256,384]{1,0:T(8,128)(2,1)S(1)}, bf16[256,384]{1,0:T(8,128)(2,1)S(1)}, u32[]{:S(2)}, u32[]{:S(2)}) collective-permute-start(bf16[256,384]{1,0:T(8,128)(2,1)S(1)} %get-tuple-element.48), channel_id=1, source_target_pairs={{0,8},{1,9},{2,10},{3,11},{4,12},{5,13},{6,14},{7,15},{8,1},{9,0},... | collective-permute-start | bytes 589832 | tf_op jit(solution)/shard_map/ppermute | solution.py:69
  133.3 2.4 %collective-permute-start.21 = (bf16[256,1536]{1,0:T(8,128)(2,1)S(1)}, bf16[256,1536]{1,0:T(8,128)(2,1)S(1)}, u32[]{:S(2)}, u32[]{:S(2)}) collective-permute-start(bf16[256,1536]{1,0:T(8,128)(2,1)S(1)} %shard_map.61.refs_0_), channel_id=1, source_target_pairs={{0,64},{1,65},{2,66},{3,67},{4,68},{5,69},{6,70},{7,71},{8,72},{9,... | collective-permute-start | bytes 2359304 | tf_op jit(solution)/shard_map/ppermute | solution.py:69

commit v5 on v4

--- a/solution.py
+++ b/solution.py
@@ -311,25 +311,15 @@
 
 
 def last_body(place, *refs):
-    near, far, turned_q, mixed_in = refs[:2], refs[2:4], refs[4], refs[5]
-    outs, (peak, mixed, done) = refs[7:11], refs[11:]
-    sides, biases = edge_sides(place)
-
-    def passes(shares):
-        good = more(turned_q, mixed_in, mixed, peak, shares, sides, biases)
-
-        @pl.when(jnp.logical_not(good))
-        def _():
-            copied(mixed_in, mixed)
-            redo(turned_q, mixed, peak, shares, sides, biases)
+    outs, (peak, mixed, done) = refs[5:9], refs[9:]
 
     @pl.when(place[1] == 1)
     def _():
-        passes((near, far))
+        third_body(place, *refs[:5], mixed, peak)
 
     @pl.when(place[1] == 0)
     def _():
-        passes((near[:1], far[:1]))
+        copied(refs[3], mixed)
 
     for head in range(HEADS):
         for side in range(2):
@@ -352,7 +342,7 @@
         out_specs=[VMEM] * 5,
         out_shape=[out] * 4 + [PEAK],
         scratch_shapes=[pltpu.VMEM(MIXED.shape, F32), pltpu.VMEM((4, HEADS, TILE, HD), BF16)],
-        input_output_aliases={6: 4},
+        input_output_aliases={4: 4},
         cost_estimate=pl.CostEstimate(flops=flops, bytes_accessed=1 << 20, transcendentals=0),
         compiler_params=pltpu.CompilerParams(vmem_limit_bytes=24 * 1024 * 1024),
         name="last",
@@ -424,9 +414,11 @@
         third_body, [near, far, turned_q, mixed, peak],
         [MIXED, PEAK], flops_of(2), aliases={4: 1},
     )
-    outs = last(
-        [near_inner, near_outer, far_inner, far_outer, turned_q, mixed, peak], flops_of(4)
-    )
+    mixed, peak = local_call(
+        third_body, [near_inner, far_inner, turned_q, mixed, peak],
+        [MIXED, PEAK], flops_of(2), aliases={4: 1},
+    )
+    outs = last([near_outer, far_outer, turned_q, mixed, peak], flops_of(2))
     chunks = [send(outs[s], back_to_tiles(s)) for s in range(4)]
     joined = local_call(join_body, chunks, jax.ShapeDtypeStruct((TILE, features), BF16))
     arrived = send(joined, partner)

time: 138 us -> 139 us (level)
  the two profiles are of different devices: /device:TPU:1 before, /device:TPU:3 now
where the time goes in v5:
time: 139 us
  starting transfers between devices  48.9 us (35%)
  Pallas kernels  45.2 us (33%)
  waiting for transfers between devices  40.1 us (29%)
  local copies, waits for them, and re-layouts  3.99 us (3%)
    ppermute x23, starting transfers between devices, send(): return lax.ppermute(x, AXES, perm)  48.9 us
    pallas_call x11, Pallas kernels, local_call(): pl.pallas_call(functools.partial(here_body, body), in_specs=[VMEM] * len(...  42.5 us
    ppermute x23, waiting for transfers between devices, send(): return lax.ppermute(x, AXES, perm)  40.1 us
    unnamed x16, local copies, waits for them, and re-layouts  3.98 us
  transfers between devices with their start and end apart: 23, of which 13 were waited for; matrix products, arithmetic and copies ran while one was open for 0% of the time, Pallas kernels for 31%

profile of v5, /device:TPU:3, one launch (start us, length us, event | category | flops | bytes accessed | tf_op | source)
XLA Modules:
  0.0 138.5 jit_solution(8664936761478807218)
XLA Ops:
  0.0 3.7 %copy-done = bf16[1536,3072]{1,0:T(8,128)(2,1)S(1)} copy-done((bf16[1536,3072]{1,0:T(8,128)(2,1)S(1)}, bf16[1536,3072]{1,0:T(8,128)(2,1)}, u32[]{:S(2)}) %copy-start) | copy-done | bytes 9437208
  3.7 0.3 shard_map.64
  4.0 0.0 copy-start.3
  4.0 0.8 collective-permute-start.22
  4.8 0.0 copy-done.1
  4.8 0.2 copy-done.2
  5.1 0.3 shard_map.55
  5.4 3.8 %collective-permute-start = (bf16[3,2,256,128]{3,2,1,0:T(8,128)(2,1)S(1)}, bf16[3,2,256,128]{3,2,1,0:T(8,128)(2,1)S(1)}, u32[]{:S(2)}, u32[]{:S(2)}) collective-permute-start(bf16[3,2,256,128]{3,2,1,0:T(8,128)(2,1)S(1)} %get-tuple-element.29), channel_id=1, source_target_pairs={{0,0},{1,1},{2,2},{3,3},{4,4},{5,5},{6,6},{7,7},{8,8},{9,9},{10,10... | collective-permute-start | bytes 1179656 | tf_op jit(solution)/shard_map/ppermute | solution.py:69
  9.1 1.4 %collective-permute-start.1 = (bf16[3,2,256,128]{3,2,1,0:T(8,128)(2,1)S(1)}, bf16[3,2,256,128]{3,2,1,0:T(8,128)(2,1)S(1)}, u32[]{:S(2)}, u32[]{:S(2)}) collective-permute-start(bf16[3,2,256,128]{3,2,1,0:T(8,128)(2,1)S(1)} %get-tuple-element.30), channel_id=1, source_target_pairs={{0,8},{1,9},{2,10},{3,11},{4,12},{5,13},{6,14},{7,15},{8,1},{9,0},... | collective-permute-start | bytes 1179656 | tf_op jit(solution)/shard_map/ppermute | solution.py:69
  10.6 4.8 %collective-permute-start.2 = (bf16[3,2,256,128]{3,2,1,0:T(8,128)(2,1)S(1)}, bf16[3,2,256,128]{3,2,1,0:T(8,128)(2,1)S(1)}, u32[]{:S(2)}, u32[]{:S(2)}) collective-permute-start(bf16[3,2,256,128]{3,2,1,0:T(8,128)(2,1)S(1)} %get-tuple-element.31), channel_id=1, source_target_pairs={{0,1},{1,0},{2,3},{3,2},{4,5},{5,4},{6,7},{7,6},{8,9},{9,8},{10,11... | collective-permute-start | bytes 1179656 | tf_op jit(solution)/shard_map/ppermute | solution.py:69
  15.3 0.5 collective-permute-start.3
  15.8 0.0 collective-permute-done.refs_0_
  15.8 6.8 %collective-permute-done.1.refs_1_ = bf16[3,2,256,128]{3,2,1,0:T(8,128)(2,1)S(1)} collective-permute-done((bf16[3,2,256,128]{3,2,1,0:T(8,128)(2,1)S(1)}, bf16[3,2,256,128]{3,2,1,0:T(8,128)(2,1)S(1)}, u32[]{:S(2)}, u32[]{:S(2)}) %collective-permute-start.1) | collective-permute-done | bytes 393248 | tf_op jit(solution)/shard_map/ppermute | solution.py:69
  22.6 3.9 %collective-permute-done.2.refs_2_ = bf16[3,2,256,128]{3,2,1,0:T(8,128)(2,1)S(1)} collective-permute-done((bf16[3,2,256,128]{3,2,1,0:T(8,128)(2,1)S(1)}, bf16[3,2,256,128]{3,2,1,0:T(8,128)(2,1)S(1)}, u32[]{:S(2)}, u32[]{:S(2)}) %collective-permute-start.2) | collective-permute-done | bytes 393248 | tf_op jit(solution)/shard_map/ppermute | solution.py:69
  26.5 2.5 %collective-permute-done.3.refs_3_ = bf16[3,2,256,128]{3,2,1,0:T(8,128)(2,1)S(1)} collective-permute-done((bf16[3,2,256,128]{3,2,1,0:T(8,128)(2,1)S(1)}, bf16[3,2,256,128]{3,2,1,0:T(8,128)(2,1)S(1)}, u32[]{:S(2)}, u32[]{:S(2)}) %collective-permute-start.3) | collective-permute-done | bytes 393248 | tf_op jit(solution)/shard_map/ppermute | solution.py:69
  29.0 0.3 shard_map.56
  29.3 4.5 %collective-permute-start.4 = (bf16[3,2,2,256,128]{4,3,2,1,0:T(8,128)(2,1)S(1)}, bf16[3,2,2,256,128]{4,3,2,1,0:T(8,128)(2,1)S(1)}, u32[]{:S(2)}, u32[]{:S(2)}) collective-permute-start(bf16[3,2,2,256,128]{4,3,2,1,0:T(8,128)(2,1)S(1)} %get-tuple-element.33.refs_0_), channel_id=1, source_target_pairs={{64,112},{65,113},{66,114},{67,115},{68,116},{69,117},{70,118},{71... | collective-permute-start | bytes 2359304 | tf_op jit(solution)/shard_map/ppermute | solution.py:69
  33.8 0.1 collective-permute-start.8
  33.9 0.3 shard_map.57
  34.2 0.1 collective-permute-start.10
  34.3 4.4 %collective-permute-start.11 = (bf16[3,256,128]{2,1,0:T(8,128)(2,1)S(1)}, bf16[3,256,128]{2,1,0:T(8,128)(2,1)S(1)}, u32[]{:S(2)}, u32[]{:S(2)}) collective-permute-start(bf16[3,256,128]{2,1,0:T(8,128)(2,1)S(1)} %get-tuple-element.38), channel_id=1, source_target_pairs={{0,1},{1,0},{2,3},{3,2},{4,5},{5,4},{6,7},{7,6},{8,9},{9,8},{10,11... | collective-permute-start | bytes 589832 | tf_op jit(solution)/shard_map/ppermute | solution.py:69
  38.7 2.9 %collective-permute-done.10.refs_4_ = bf16[3,256,128]{2,1,0:T(8,128)(2,1)S(1)} collective-permute-done((bf16[3,256,128]{2,1,0:T(8,128)(2,1)S(1)}, bf16[3,256,128]{2,1,0:T(8,128)(2,1)S(1)}, u32[]{:S(2)}, u32[]{:S(2)}) %collective-permute-start.10) | collective-permute-done | bytes 196640 | tf_op jit(solution)/shard_map/ppermute | solution.py:69
  41.6 0.7 collective-permute-start.12
  42.2 2.0 %collective-permute-done.11.refs_5_ = bf16[3,256,128]{2,1,0:T(8,128)(2,1)S(1)} collective-permute-done((bf16[3,256,128]{2,1,0:T(8,128)(2,1)S(1)}, bf16[3,256,128]{2,1,0:T(8,128)(2,1)S(1)}, u32[]{:S(2)}, u32[]{:S(2)}) %collective-permute-start.11) | collective-permute-done | bytes 196640 | tf_op jit(solution)/shard_map/ppermute | solution.py:69
  44.3 3.2 %collective-permute-start.9 = (bf16[3,256,128]{2,1,0:T(8,128)(2,1)S(1)}, bf16[3,256,128]{2,1,0:T(8,128)(2,1)S(1)}, u32[]{:S(2)}, u32[]{:S(2)}) collective-permute-start(bf16[3,256,128]{2,1,0:T(8,128)(2,1)S(1)} %get-tuple-element.36), channel_id=1, source_target_pairs={{0,0},{1,1},{2,2},{3,3},{4,4},{5,5},{6,6},{7,7},{8,8},{9,9},{10,10... | collective-permute-start | bytes 589832 | tf_op jit(solution)/shard_map/ppermute | solution.py:69
  47.5 0.3 collective-permute-done.12.refs_6_
  47.9 0.3 collective-permute-start.13
  48.1 3.1 %collective-permute-done.9.refs_3_ = bf16[3,256,128]{2,1,0:T(8,128)(2,1)S(1)} collective-permute-done((bf16[3,256,128]{2,1,0:T(8,128)(2,1)S(1)}, bf16[3,256,128]{2,1,0:T(8,128)(2,1)S(1)}, u32[]{:S(2)}, u32[]{:S(2)}) %collective-permute-start.9) | collective-permute-done | bytes 196640 | tf_op jit(solution)/shard_map/ppermute | solution.py:69
  51.2 3.1 %collective-permute-start.15 = (bf16[3,2,2,256,128]{4,3,2,1,0:T(8,128)(2,1)S(1)}, bf16[3,2,2,256,128]{4,3,2,1,0:T(8,128)(2,1)S(1)}, u32[]{:S(2)}, u32[]{:S(2)}) collective-permute-start(bf16[3,2,2,256,128]{4,3,2,1,0:T(8,128)(2,1)S(1)} %get-tuple-element.34.refs_1_), channel_id=1, source_target_pairs={{2,4},{3,5},{4,2},{5,3},{10,12},{11,13},{12,10},{13,11},{18,20},{1... | collective-permute-start | bytes 2359304 | tf_op jit(solution)/shard_map/ppermute | solution.py:69
  54.4 0.0 collective-permute-done.4.refs_0_
  54.4 2.3 %collective-permute-start.6 = (bf16[3,2,2,256,128]{4,3,2,1,0:T(8,128)(2,1)S(1)}, bf16[3,2,2,256,128]{4,3,2,1,0:T(8,128)(2,1)S(1)}, u32[]{:S(2)}, u32[]{:S(2)}) collective-permute-start(bf16[3,2,2,256,128]{4,3,2,1,0:T(8,128)(2,1)S(1)} %get-tuple-element.34.refs_1_), channel_id=1, source_target_pairs={{64,112},{65,113},{66,114},{67,115},{68,116},{69,117},{70,118},{71... | collective-permute-start | bytes 2359304 | tf_op jit(solution)/shard_map/ppermute | solution.py:69
  56.7 6.7 %collective-permute-done.13.refs_0_ = bf16[3,2,2,256,128]{4,3,2,1,0:T(8,128)(2,1)S(1)} collective-permute-done((bf16[3,2,2,256,128]{4,3,2,1,0:T(8,128)(2,1)S(1)}, bf16[3,2,2,256,128]{4,3,2,1,0:T(8,128)(2,1)S(1)}, u32[]{:S(2)}, u32[]{:S(2)}) %collective-permute-start.13) | collective-permute-done | bytes 786464 | tf_op jit(solution)/shard_map/ppermute | solution.py:69
  63.3 4.5 %collective-permute-start.14 = (bf16[3,2,2,256,128]{4,3,2,1,0:T(8,128)(2,1)S(1)}, bf16[3,2,2,256,128]{4,3,2,1,0:T(8,128)(2,1)S(1)}, u32[]{:S(2)}, u32[]{:S(2)}) collective-permute-start(bf16[3,2,2,256,128]{4,3,2,1,0:T(8,128)(2,1)S(1)} %collective-permute-done.13.refs_0_), channel_id=1, source_target_pairs={{0,64},{1,65},{2,66},{3,67},{4,68},{5,69},{6,70},{7,71},{8,72},{9,... | collective-permute-start | bytes 2359304 | tf_op jit(solution)/shard_map/ppermute | solution.py:69
  67.8 3.5 %collective-permute-done.15.refs_1_ = bf16[3,2,2,256,128]{4,3,2,1,0:T(8,128)(2,1)S(1)} collective-permute-done((bf16[3,2,2,256,128]{4,3,2,1,0:T(8,128)(2,1)S(1)}, bf16[3,2,2,256,128]{4,3,2,1,0:T(8,128)(2,1)S(1)}, u32[]{:S(2)}, u32[]{:S(2)}) %collective-permute-start.15) | collective-permute-done | bytes 786464 | tf_op jit(solution)/shard_map/ppermute | solution.py:69
  71.3 1.8 %collective-permute-start.16 = (bf16[3,2,2,256,128]{4,3,2,1,0:T(8,128)(2,1)S(1)}, bf16[3,2,2,256,128]{4,3,2,1,0:T(8,128)(2,1)S(1)}, u32[]{:S(2)}, u32[]{:S(2)}) collective-permute-start(bf16[3,2,2,256,128]{4,3,2,1,0:T(8,128)(2,1)S(1)} %collective-permute-done.15.refs_1_), channel_id=1, source_target_pairs={{0,64},{1,65},{2,66},{3,67},{4,68},{5,69},{6,70},{7,71},{8,72},{9,... | collective-permute-start | bytes 2359304 | tf_op jit(solution)/shard_map/ppermute | solution.py:69
  73.1 0.0 collective-permute-done.6.refs_1_
  73.1 1.9 %collective-permute-start.5 = (bf16[3,2,2,256,128]{4,3,2,1,0:T(8,128)(2,1)S(1)}, bf16[3,2,2,256,128]{4,3,2,1,0:T(8,128)(2,1)S(1)}, u32[]{:S(2)}, u32[]{:S(2)}) collective-permute-start(bf16[3,2,2,256,128]{4,3,2,1,0:T(8,128)(2,1)S(1)} %collective-permute-done.4.refs_0_), channel_id=1, source_target_pairs={{64,66},{65,67},{66,64},{67,65},{68,70},{69,71},{70,68},{71,69},{7... | collective-permute-start | bytes 2359304 | tf_op jit(solution)/shard_map/ppermute | solution.py:69
  75.0 0.0 collective-permute-done.8.refs_2_
  75.0 3.1 %collective-permute-start.7 = (bf16[3,2,2,256,128]{4,3,2,1,0:T(8,128)(2,1)S(1)}, bf16[3,2,2,256,128]{4,3,2,1,0:T(8,128)(2,1)S(1)}, u32[]{:S(2)}, u32[]{:S(2)}) collective-permute-start(bf16[3,2,2,256,128]{4,3,2,1,0:T(8,128)(2,1)S(1)} %collective-permute-done.6.refs_1_), channel_id=1, source_target_pairs={{66,68},{67,69},{68,66},{69,67},{74,76},{75,77},{76,74},{77,75},{8... | collective-permute-start | bytes 2359304 | tf_op jit(solution)/shard_map/ppermute | solution.py:69
  78.1 29.9 %shard_map.58 = (bf16[3,4,256,256]{3,2,1,0:T(8,128)(2,1)S(1)}, f32[3,2,144,512]{3,2,1,0:T(8,128)S(1)}, f32[3,2,1,512]{3,2,1,0:T(1,128)S(1)}) custom-call(bf16[3,2,2,256,128]{4,3,2,1,0:T(8,128)(2,1)S(1)} %get-tuple-element.33.refs_0_, bf16[3,2,2,256,128]{4,3,2,1,0:T(8,128)(2,1)S(1)} %get-tuple-element.34.refs_1_, ...), custom_call_target="tpu_custom_call" | custom-call | flops 4831838208 | bytes 7286784 | tf_op jit(solution)/shard_map/pallas_call | solution.py:114
  108.0 0.0 slice-start
  108.0 0.0 slice-start.1
  108.0 3.0 %shard_map.59 = (f32[3,2,144,512]{3,2,1,0:T(8,128)S(1)}, f32[3,2,1,512]{3,2,1,0:T(1,128)S(1)}) custom-call(bf16[3,2,2,256,128]{4,3,2,1,0:T(8,128)(2,1)S(1)} %collective-permute-done.4.refs_0_, bf16[3,2,2,256,128]{4,3,2,1,0:T(8,128)(2,1)S(1)} %collective-permute-done.6.refs_1_, ...), custom_call_target="tpu_custom_call", output_to_operand_aliasing={{1}: (4, {})} | custom-call | flops 2415919104 | bytes 6709248 | tf_op jit(solution)/shard_map/pallas_call | solution.py:114
  111.0 2.3 %shard_map.60 = (f32[3,2,144,512]{3,2,1,0:T(8,128)S(1)}, f32[3,2,1,512]{3,2,1,0:T(1,128)S(1)}) custom-call(bf16[3,2,2,256,128]{4,3,2,1,0:T(8,128)(2,1)S(1)} %collective-permute-done.13.refs_0_, bf16[3,2,2,256,128]{4,3,2,1,0:T(8,128)(2,1)S(1)} %collective-permute-done.15.refs_1_, ...), custom_call_target="tpu_custom_call", output_to_operand_aliasing={{1}: (4, {})} | custom-call | flops 1207959552 | bytes 6709248 | tf_op jit(solution)/shard_map/pallas_call | solution.py:114
  113.4 0.0 collective-permute-done.14.refs_0_
  113.4 0.0 collective-permute-done.16.refs_1_
  113.4 0.0 slice-start.2
  113.4 2.3 %shard_map.61 = (f32[3,2,144,512]{3,2,1,0:T(8,128)S(1)}, f32[3,2,1,512]{3,2,1,0:T(1,128)S(1)}) custom-call(bf16[3,2,2,256,128]{4,3,2,1,0:T(8,128)(2,1)S(1)} %collective-permute-done.14.refs_0_, bf16[3,2,2,256,128]{4,3,2,1,0:T(8,128)(2,1)S(1)} %collective-permute-done.16.refs_1_, ...), custom_call_target="tpu_custom_call", output_to_operand_aliasing={{1}: (4, {})} | custom-call | flops 1207959552 | bytes 6709248 | tf_op jit(solution)/shard_map/pallas_call | solution.py:114
  115.7 0.0 collective-permute-done.5.refs_0_
  115.7 0.0 collective-permute-done.7.refs_1_
  115.7 0.0 copy-start.4
  115.8 2.7 %last.1 = (bf16[256,384]{1,0:T(8,128)(2,1)S(1)}, bf16[256,384]{1,0:T(8,128)(2,1)S(1)}, bf16[256,384]{1,0:T(8,128)(2,1)S(1)}, bf16[256,384]{1,0:T(8,128)(2,1)S(1)}, f32[3,2,1,512]{3,2,1,0:T(1,128)S(1)}) custom-call(bf16[3,2,2,256,128]{4,3,2,1,0:T(8,128)(2,1)S(1)} %collective-permute-done.5.refs_0_, ...), custom_call_target="tpu_custom_call", output_to_operand_aliasing={{4}: (4, {})} | custom-call | flops 1207959552 | bytes 1048576 | tf_op jit(solution)/shard_map/last/pallas_call | solution.py:339
  118.5 1.9 %collective-permute-start.17 = (bf16[256,384]{1,0:T(8,128)(2,1)S(1)}, bf16[256,384]{1,0:T(8,128)(2,1)S(1)}, u32[]{:S(2)}, u32[]{:S(2)}) collective-permute-start(bf16[256,384]{1,0:T(8,128)(2,1)S(1)} %get-tuple-element.49), channel_id=1, source_target_pairs={{0,0},{1,1},{2,2},{3,3},{4,4},{5,5},{6,6},{7,7},{8,8},{9,9},{10,10... | collective-permute-start | bytes 589832 | tf_op jit(solution)/shard_map/ppermute | solution.py:69
  120.4 3.5 %collective-permute-start.18 = (bf16[256,384]{1,0:T(8,128)(2,1)S(1)}, bf16[256,384]{1,0:T(8,128)(2,1)S(1)}, u32[]{:S(2)}, u32[]{:S(2)}) collective-permute-start(bf16[256,384]{1,0:T(8,128)(2,1)S(1)} %get-tuple-element.50), channel_id=1, source_target_pairs={{0,9},{1,8},{2,11},{3,10},{4,13},{5,12},{6,15},{7,14},{8,0},{9,1},... | collective-permute-start | bytes 589832 | tf_op jit(solution)/shard_map/ppermute | solution.py:69
  123.9 0.3 collective-permute-start.19
  124.2 1.9 %collective-permute-start.20 = (bf16[256,384]{1,0:T(8,128)(2,1)S(1)}, bf16[256,384]{1,0:T(8,128)(2,1)S(1)}, u32[]{:S(2)}, u32[]{:S(2)}) collective-permute-start(bf16[256,384]{1,0:T(8,128)(2,1)S(1)} %get-tuple-element.52), channel_id=1, source_target_pairs={{0,8},{1,9},{2,10},{3,11},{4,12},{5,13},{6,14},{7,15},{8,1},{9,0},... | collective-permute-start | bytes 589832 | tf_op jit(solution)/shard_map/ppermute | solution.py:69
  126.2 1.7 %collective-permute-done.18.refs_1_ = bf16[256,384]{1,0:T(8,128)(2,1)S(1)} collective-permute-done((bf16[256,384]{1,0:T(8,128)(2,1)S(1)}, bf16[256,384]{1,0:T(8,128)(2,1)S(1)}, u32[]{:S(2)}, u32[]{:S(2)}) %collective-permute-start.18) | collective-permute-done | bytes 196640 | tf_op jit(solution)/shard_map/ppermute | solution.py:69
  127.8 4.0 %collective-permute-done.19.refs_2_ = bf16[256,384]{1,0:T(8,128)(2,1)S(1)} collective-permute-done((bf16[256,384]{1,0:T(8,128)(2,1)S(1)}, bf16[256,384]{1,0:T(8,128)(2,1)S(1)}, u32[]{:S(2)}, u32[]{:S(2)}) %collective-permute-start.19) | collective-permute-done | bytes 196640 | tf_op jit(solution)/shard_map/ppermute | solution.py:69
  131.9 1.9 %collective-permute-done.20.refs_3_ = bf16[256,384]{1,0:T(8,128)(2,1)S(1)} collective-permute-done((bf16[256,384]{1,0:T(8,128)(2,1)S(1)}, bf16[256,384]{1,0:T(8,128)(2,1)S(1)}, u32[]{:S(2)}, u32[]{:S(2)}) %collective-permute-start.20) | collective-permute-done | bytes 196640 | tf_op jit(solution)/shard_map/ppermute | solution.py:69
  133.7 0.1 shard_map.62.refs_0_
  133.9 0.1 collective-permute-start.21
  134.0 1.4 %shard_map.63.refs_0_ = f32[256,1536]{1,0:T(8,128)S(1)} custom-call(bf16[256,1536]{1,0:T(8,128)(2,1)S(1)} %shard_map.62.refs_0_, bf16[1536,3072]{1,0:T(8,128)(2,1)S(1)} %bitcast.5), custom_call_target="tpu_custom_call" | custom-call | flops 1207959552 | bytes 11796480 | tf_op jit(solution)/shard_map/pallas_call | solution.py:114
  135.4 0.8 collective-permute-done.21.refs_1_
  136.2 2.3 %shard_map.65 = bf16[256,1536]{1,0:T(8,128)(2,1)} custom-call(f32[256,1536]{1,0:T(8,128)S(1)} %shard_map.63.refs_0_, bf16[256,1536]{1,0:T(8,128)(2,1)S(1)} %collective-permute-done.21.refs_1_, bf16[1536,1536]{1,0:T(8,128)(2,1)S(1)} %collective-permute-done.22.refs_2_, bf16[1,1536]{1,0:T(2,128)(2,1)S(1)} %reshape.18.refs_3_), custom_call_target="tpu_custom_call" | custom-call | flops 1207959552 | bytes 7867392 | tf_op jit(solution)/shard_map/pallas_call | solution.py:114
  (12 shorter events, 0.0 us)
Async XLA Ops:
  0.0 3.7 %copy-start = (bf16[1536,3072]{1,0:T(8,128)(2,1)S(1)}, bf16[1536,3072]{1,0:T(8,128)(2,1)}, u32[]{:S(2)}) copy-start(bf16[1536,3072]{1,0:T(8,128)(2,1)} %refs_0_.1) | copy-start | bytes 28311556
  3.7 1.1 copy-start.1
  3.7 1.4 copy-start.2
  4.0 29.9 %copy-start.3 = (bf16[1,1,1,256,1536]{4,3,2,1,0:T(8,128)(2,1)S(1)}, bf16[1,1,1,256,1536]{4,3,2,1,0:T(8,128)(2,1)}, u32[]{:S(2)}) copy-start(bf16[1,1,1,256,1536]{4,3,2,1,0:T(8,128)(2,1)} %param.5) | copy-start | bytes 2359300
  4.0 132.2 %collective-permute-start.22 = (bf16[1536,1536]{1,0:T(8,128)(2,1)S(1)}, bf16[1536,1536]{1,0:T(8,128)(2,1)S(1)}, u32[]{:S(2)}, u32[]{:S(2)}) collective-permute-start(bf16[1536,1536]{1,0:T(8,128)(2,1)S(1)} %shard_map.64), channel_id=1, source_target_pairs={{0,64},{1,65},{2,66},{3,67},{4,68},{5,69},{6,70},{7,71},{8,72},{9,... | collective-permute-start | bytes 14155784 | tf_op jit(solution)/shard_map/ppermute | solution.py:69
  5.4 10.4 %collective-permute-start = (bf16[3,2,256,128]{3,2,1,0:T(8,128)(2,1)S(1)}, bf16[3,2,256,128]{3,2,1,0:T(8,128)(2,1)S(1)}, u32[]{:S(2)}, u32[]{:S(2)}) collective-permute-start(bf16[3,2,256,128]{3,2,1,0:T(8,128)(2,1)S(1)} %get-tuple-element.29), channel_id=1, source_target_pairs={{0,0},{1,1},{2,2},{3,3},{4,4},{5,5},{6,6},{7,7},{8,8},{9,9},{10,10... | collective-permute-start | bytes 1179656 | tf_op jit(solution)/shard_map/ppermute | solution.py:69
  9.1 13.4 %collective-permute-start.1 = (bf16[3,2,256,128]{3,2,1,0:T(8,128)(2,1)S(1)}, bf16[3,2,256,128]{3,2,1,0:T(8,128)(2,1)S(1)}, u32[]{:S(2)}, u32[]{:S(2)}) collective-permute-start(bf16[3,2,256,128]{3,2,1,0:T(8,128)(2,1)S(1)} %get-tuple-element.30), channel_id=1, source_target_pairs={{0,8},{1,9},{2,10},{3,11},{4,12},{5,13},{6,14},{7,15},{8,1},{9,0},... | collective-permute-start | bytes 1179656 | tf_op jit(solution)/shard_map/ppermute | solution.py:69
  10.6 15.9 %collective-permute-start.2 = (bf16[3,2,256,128]{3,2,1,0:T(8,128)(2,1)S(1)}, bf16[3,2,256,128]{3,2,1,0:T(8,128)(2,1)S(1)}, u32[]{:S(2)}, u32[]{:S(2)}) collective-permute-start(bf16[3,2,256,128]{3,2,1,0:T(8,128)(2,1)S(1)} %get-tuple-element.31), channel_id=1, source_target_pairs={{0,1},{1,0},{2,3},{3,2},{4,5},{5,4},{6,7},{7,6},{8,9},{9,8},{10,11... | collective-permute-start | bytes 1179656 | tf_op jit(solution)/shard_map/ppermute | solution.py:69
  15.3 13.7 %collective-permute-start.3 = (bf16[3,2,256,128]{3,2,1,0:T(8,128)(2,1)S(1)}, bf16[3,2,256,128]{3,2,1,0:T(8,128)(2,1)S(1)}, u32[]{:S(2)}, u32[]{:S(2)}) collective-permute-start(bf16[3,2,256,128]{3,2,1,0:T(8,128)(2,1)S(1)} %get-tuple-element.32), channel_id=1, source_target_pairs={{0,9},{1,8},{2,11},{3,10},{4,13},{5,12},{6,15},{7,14},{8,0},{9,1},... | collective-permute-start | bytes 1179656 | tf_op jit(solution)/shard_map/ppermute | solution.py:69
  29.3 25.1 %collective-permute-start.4 = (bf16[3,2,2,256,128]{4,3,2,1,0:T(8,128)(2,1)S(1)}, bf16[3,2,2,256,128]{4,3,2,1,0:T(8,128)(2,1)S(1)}, u32[]{:S(2)}, u32[]{:S(2)}) collective-permute-start(bf16[3,2,2,256,128]{4,3,2,1,0:T(8,128)(2,1)S(1)} %get-tuple-element.33.refs_0_), channel_id=1, source_target_pairs={{64,112},{65,113},{66,114},{67,115},{68,116},{69,117},{70,118},{71... | collective-permute-start | bytes 2359304 | tf_op jit(solution)/shard_map/ppermute | solution.py:69
  33.8 41.2 %collective-permute-start.8 = (bf16[2,3,2,2,256,128]{5,4,3,2,1,0:T(8,128)(2,1)S(1)}, bf16[2,3,2,2,256,128]{5,4,3,2,1,0:T(8,128)(2,1)S(1)}, u32[]{:S(2)}, u32[]{:S(2)}) collective-permute-start(bf16[2,3,2,2,256,128]{5,4,3,2,1,0:T(8,128)(2,1)S(1)} %get-tuple-element.35), channel_id=1, source_target_pairs={{0,64},{1,65},{2,66},{3,67},{4,68},{5,69},{6,70},{7,71},{8,72},{9,... | collective-permute-start | bytes 4718600 | tf_op jit(solution)/shard_map/ppermute | solution.py:69
  34.2 7.4 %collective-permute-start.10 = (bf16[3,256,128]{2,1,0:T(8,128)(2,1)S(1)}, bf16[3,256,128]{2,1,0:T(8,128)(2,1)S(1)}, u32[]{:S(2)}, u32[]{:S(2)}) collective-permute-start(bf16[3,256,128]{2,1,0:T(8,128)(2,1)S(1)} %get-tuple-element.37), channel_id=1, source_target_pairs={{0,8},{1,9},{2,10},{3,11},{4,12},{5,13},{6,14},{7,15},{8,1},{9,0},... | collective-permute-start | bytes 589832 | tf_op jit(solution)/shard_map/ppermute | solution.py:69
  34.3 10.0 %collective-permute-start.11 = (bf16[3,256,128]{2,1,0:T(8,128)(2,1)S(1)}, bf16[3,256,128]{2,1,0:T(8,128)(2,1)S(1)}, u32[]{:S(2)}, u32[]{:S(2)}) collective-permute-start(bf16[3,256,128]{2,1,0:T(8,128)(2,1)S(1)} %get-tuple-element.38), channel_id=1, source_target_pairs={{0,1},{1,0},{2,3},{3,2},{4,5},{5,4},{6,7},{7,6},{8,9},{9,8},{10,11... | collective-permute-start | bytes 589832 | tf_op jit(solution)/shard_map/ppermute | solution.py:69
  41.6 6.3 %collective-permute-start.12 = (bf16[3,256,128]{2,1,0:T(8,128)(2,1)S(1)}, bf16[3,256,128]{2,1,0:T(8,128)(2,1)S(1)}, u32[]{:S(2)}, u32[]{:S(2)}) collective-permute-start(bf16[3,256,128]{2,1,0:T(8,128)(2,1)S(1)} %get-tuple-element.39), channel_id=1, source_target_pairs={{0,9},{1,8},{2,11},{3,10},{4,13},{5,12},{6,15},{7,14},{8,0},{9,1},... | collective-permute-start | bytes 589832 | tf_op jit(solution)/shard_map/ppermute | solution.py:69
  44.3 7.0 %collective-permute-start.9 = (bf16[3,256,128]{2,1,0:T(8,128)(2,1)S(1)}, bf16[3,256,128]{2,1,0:T(8,128)(2,1)S(1)}, u32[]{:S(2)}, u32[]{:S(2)}) collective-permute-start(bf16[3,256,128]{2,1,0:T(8,128)(2,1)S(1)} %get-tuple-element.36), channel_id=1, source_target_pairs={{0,0},{1,1},{2,2},{3,3},{4,4},{5,5},{6,6},{7,7},{8,8},{9,9},{10,10... | collective-permute-start | bytes 589832 | tf_op jit(solution)/shard_map/ppermute | solution.py:69
  47.9 15.5 %collective-permute-start.13 = (bf16[3,2,2,256,128]{4,3,2,1,0:T(8,128)(2,1)S(1)}, bf16[3,2,2,256,128]{4,3,2,1,0:T(8,128)(2,1)S(1)}, u32[]{:S(2)}, u32[]{:S(2)}) collective-permute-start(bf16[3,2,2,256,128]{4,3,2,1,0:T(8,128)(2,1)S(1)} %get-tuple-element.33.refs_0_), channel_id=1, source_target_pairs={{0,2},{1,3},{2,0},{3,1},{4,6},{5,7},{6,4},{7,5},{8,10},{9,11},{10,... | collective-permute-start | bytes 2359304 | tf_op jit(solution)/shard_map/ppermute | solution.py:69
  51.2 20.1 %collective-permute-start.15 = (bf16[3,2,2,256,128]{4,3,2,1,0:T(8,128)(2,1)S(1)}, bf16[3,2,2,256,128]{4,3,2,1,0:T(8,128)(2,1)S(1)}, u32[]{:S(2)}, u32[]{:S(2)}) collective-permute-start(bf16[3,2,2,256,128]{4,3,2,1,0:T(8,128)(2,1)S(1)} %get-tuple-element.34.refs_1_), channel_id=1, source_target_pairs={{2,4},{3,5},{4,2},{5,3},{10,12},{11,13},{12,10},{13,11},{18,20},{1... | collective-permute-start | bytes 2359304 | tf_op jit(solution)/shard_map/ppermute | solution.py:69
  54.4 18.7 %collective-permute-start.6 = (bf16[3,2,2,256,128]{4,3,2,1,0:T(8,128)(2,1)S(1)}, bf16[3,2,2,256,128]{4,3,2,1,0:T(8,128)(2,1)S(1)}, u32[]{:S(2)}, u32[]{:S(2)}) collective-permute-start(bf16[3,2,2,256,128]{4,3,2,1,0:T(8,128)(2,1)S(1)} %get-tuple-element.34.refs_1_), channel_id=1, source_target_pairs={{64,112},{65,113},{66,114},{67,115},{68,116},{69,117},{70,118},{71... | collective-permute-start | bytes 2359304 | tf_op jit(solution)/shard_map/ppermute | solution.py:69
  63.3 50.0 %collective-permute-start.14 = (bf16[3,2,2,256,128]{4,3,2,1,0:T(8,128)(2,1)S(1)}, bf16[3,2,2,256,128]{4,3,2,1,0:T(8,128)(2,1)S(1)}, u32[]{:S(2)}, u32[]{:S(2)}) collective-permute-start(bf16[3,2,2,256,128]{4,3,2,1,0:T(8,128)(2,1)S(1)} %collective-permute-done.13.refs_0_), channel_id=1, source_target_pairs={{0,64},{1,65},{2,66},{3,67},{4,68},{5,69},{6,70},{7,71},{8,72},{9,... | collective-permute-start | bytes 2359304 | tf_op jit(solution)/shard_map/ppermute | solution.py:69
  71.3 42.1 %collective-permute-start.16 = (bf16[3,2,2,256,128]{4,3,2,1,0:T(8,128)(2,1)S(1)}, bf16[3,2,2,256,128]{4,3,2,1,0:T(8,128)(2,1)S(1)}, u32[]{:S(2)}, u32[]{:S(2)}) collective-permute-start(bf16[3,2,2,256,128]{4,3,2,1,0:T(8,128)(2,1)S(1)} %collective-permute-done.15.refs_1_), channel_id=1, source_target_pairs={{0,64},{1,65},{2,66},{3,67},{4,68},{5,69},{6,70},{7,71},{8,72},{9,... | collective-permute-start | bytes 2359304 | tf_op jit(solution)/shard_map/ppermute | solution.py:69
  73.1 42.6 %collective-permute-start.5 = (bf16[3,2,2,256,128]{4,3,2,1,0:T(8,128)(2,1)S(1)}, bf16[3,2,2,256,128]{4,3,2,1,0:T(8,128)(2,1)S(1)}, u32[]{:S(2)}, u32[]{:S(2)}) collective-permute-start(bf16[3,2,2,256,128]{4,3,2,1,0:T(8,128)(2,1)S(1)} %collective-permute-done.4.refs_0_), channel_id=1, source_target_pairs={{64,66},{65,67},{66,64},{67,65},{68,70},{69,71},{70,68},{71,69},{7... | collective-permute-start | bytes 2359304 | tf_op jit(solution)/shard_map/ppermute | solution.py:69
  75.0 40.7 %collective-permute-start.7 = (bf16[3,2,2,256,128]{4,3,2,1,0:T(8,128)(2,1)S(1)}, bf16[3,2,2,256,128]{4,3,2,1,0:T(8,128)(2,1)S(1)}, u32[]{:S(2)}, u32[]{:S(2)}) collective-permute-start(bf16[3,2,2,256,128]{4,3,2,1,0:T(8,128)(2,1)S(1)} %collective-permute-done.6.refs_1_), channel_id=1, source_target_pairs={{66,68},{67,69},{68,66},{69,67},{74,76},{75,77},{76,74},{77,75},{8... | collective-permute-start | bytes 2359304 | tf_op jit(solution)/shard_map/ppermute | solution.py:69
  108.0 26.0 %slice-start = ((s8[9437184]{0:T(1024)(128)(4,1)}), s8[4194304]{0:T(1024)(128)(4,1)S(1)}, s32[]{:S(2)}) async-start(s8[9437184]{0:T(1024)(128)(4,1)} %bitcast.4), calls=%async_computation | async-start | bytes 8388608
  108.0 26.0 %slice-start.1 = ((s8[9437184]{0:T(1024)(128)(4,1)}), s8[4194304]{0:T(1024)(128)(4,1)S(1)}, s32[]{:S(2)}) async-start(s8[9437184]{0:T(1024)(128)(4,1)} %bitcast.4), calls=%async_computation.1 | async-start | bytes 8388608
  113.4 20.6 %slice-start.2 = ((s8[9437184]{0:T(1024)(128)(4,1)}), s8[1048576]{0:T(1024)(128)(4,1)S(1)}, s32[]{:S(2)}) async-start(s8[9437184]{0:T(1024)(128)(4,1)} %bitcast.4), calls=%async_computation.2 | async-start | bytes 2097152
  115.7 18.2 %copy-start.4 = (bf16[1536]{0:T(1024)(128)(2,1)S(1)}, bf16[1536]{0:T(1024)(128)(2,1)}, u32[]{:S(2)}) copy-start(bf16[1536]{0:T(1024)(128)(2,1)} %param.9) | copy-start | bytes 9220
  118.5 7.7 %collective-permute-start.17 = (bf16[256,384]{1,0:T(8,128)(2,1)S(1)}, bf16[256,384]{1,0:T(8,128)(2,1)S(1)}, u32[]{:S(2)}, u32[]{:S(2)}) collective-permute-start(bf16[256,384]{1,0:T(8,128)(2,1)S(1)} %get-tuple-element.49), channel_id=1, source_target_pairs={{0,0},{1,1},{2,2},{3,3},{4,4},{5,5},{6,6},{7,7},{8,8},{9,9},{10,10... | collective-permute-start | bytes 589832 | tf_op jit(solution)/shard_map/ppermute | solution.py:69
  120.4 7.4 %collective-permute-start.18 = (bf16[256,384]{1,0:T(8,128)(2,1)S(1)}, bf16[256,384]{1,0:T(8,128)(2,1)S(1)}, u32[]{:S(2)}, u32[]{:S(2)}) collective-permute-start(bf16[256,384]{1,0:T(8,128)(2,1)S(1)} %get-tuple-element.50), channel_id=1, source_target_pairs={{0,9},{1,8},{2,11},{3,10},{4,13},{5,12},{6,15},{7,14},{8,0},{9,1},... | collective-permute-start | bytes 589832 | tf_op jit(solution)/shard_map/ppermute | solution.py:69
  123.9 8.0 %collective-permute-start.19 = (bf16[256,384]{1,0:T(8,128)(2,1)S(1)}, bf16[256,384]{1,0:T(8,128)(2,1)S(1)}, u32[]{:S(2)}, u32[]{:S(2)}) collective-permute-start(bf16[256,384]{1,0:T(8,128)(2,1)S(1)} %get-tuple-element.51), channel_id=1, source_target_pairs={{0,1},{1,0},{2,3},{3,2},{4,5},{5,4},{6,7},{7,6},{8,9},{9,8},{10,11... | collective-permute-start | bytes 589832 | tf_op jit(solution)/shard_map/ppermute | solution.py:69
  124.2 9.5 %collective-permute-start.20 = (bf16[256,384]{1,0:T(8,128)(2,1)S(1)}, bf16[256,384]{1,0:T(8,128)(2,1)S(1)}, u32[]{:S(2)}, u32[]{:S(2)}) collective-permute-start(bf16[256,384]{1,0:T(8,128)(2,1)S(1)} %get-tuple-element.52), channel_id=1, source_target_pairs={{0,8},{1,9},{2,10},{3,11},{4,12},{5,13},{6,14},{7,15},{8,1},{9,0},... | collective-permute-start | bytes 589832 | tf_op jit(solution)/shard_map/ppermute | solution.py:69
  133.9 2.4 %collective-permute-start.21 = (bf16[256,1536]{1,0:T(8,128)(2,1)S(1)}, bf16[256,1536]{1,0:T(8,128)(2,1)S(1)}, u32[]{:S(2)}, u32[]{:S(2)}) collective-permute-start(bf16[256,1536]{1,0:T(8,128)(2,1)S(1)} %shard_map.62.refs_0_), channel_id=1, source_target_pairs={{0,64},{1,65},{2,66},{3,67},{4,68},{5,69},{6,70},{7,71},{8,72},{9,... | collective-permute-start | bytes 2359304 | tf_op jit(solution)/shard_map/ppermute | solution.py:69

commit v6 on v5

--- a/solution.py
+++ b/solution.py
@@ -369,9 +369,37 @@
     out[...] = weight[:, own_cols(1 - place[1], out.shape[1])]
 
 
-def close_body(place, here, joined, weight, gate, out):
-    there = jnp.dot(joined[...], weight[...], preferred_element_type=F32)
-    out[...] = (gate[...].astype(F32) * (here[...] + there)).astype(BF16)
+def close_body(here, joined, weight, gate, out, held, sent):
+    cols = held.shape[1] // 3
+    copies = []
+    for part in range(3):
+        block = slice(part * cols, (part + 1) * cols)
+        there = jnp.dot(joined[...], weight[:, block], preferred_element_type=F32)
+        total = here[:, block] + there
+        held[:, block] = (gate[:, block].astype(F32) * total).astype(BF16)
+        copy = pltpu.make_async_copy(
+            held.at[:, pl.ds(part * cols, cols)], out.at[:, pl.ds(part * cols, cols)], sent.at[part]
+        )
+        copy.start()
+        copies.append(copy)
+    for copy in copies:
+        copy.wait()
+
+
+def close(here, joined, weight, gate):
+    features = weight.shape[0]
+    return pl.pallas_call(
+        close_body,
+        in_specs=[VMEM] * 4,
+        out_specs=pl.BlockSpec(memory_space=pltpu.MemorySpace.HBM),
+        out_shape=jax.ShapeDtypeStruct((TILE, features), BF16),
+        scratch_shapes=[pltpu.VMEM((TILE, features), BF16), pltpu.SemaphoreType.DMA((3,))],
+        cost_estimate=pl.CostEstimate(
+            flops=2 * TILE * features * features, bytes_accessed=1 << 20, transcendentals=0
+        ),
+        compiler_params=pltpu.CompilerParams(vmem_limit_bytes=24 * 1024 * 1024),
+        name="close",
+    )(here, joined, weight, gate)
 
 
 def shards(query_tiles, key_tiles, value_tiles, out_weight, gate):
@@ -426,10 +454,7 @@
     here = local_call(
         home_body, [joined, out_weight], jax.ShapeDtypeStruct((TILE, features), F32), flops
     )
-    branch = local_call(
-        close_body, [here, arrived, weight_other, gate.reshape(1, -1)],
-        jax.ShapeDtypeStruct((TILE, features), BF16), flops,
-    )
+    branch = close(here, arrived, weight_other, gate.reshape(1, -1))
     return branch.reshape(1, 1, 1, TILE, features)
 
 

time: 139 us -> 139 us (level)
    pallas_call x11 -> x10, Pallas kernels: 42.5 us -> 40.2 us  [local_call(): pl.pallas_call(functools.partial(here_body, body), in_specs=[VMEM] * len(...]
    pallas_call x0 -> x1, Pallas kernels: none -> 2.11 us  [close(): pl.pallas_call(close_body, in_specs=[VMEM] * 4, out_specs=pl.BlockSpec(me...]
where the time goes in v6:
time: 139 us
  starting transfers between devices  48.9 us (35%)
  Pallas kernels  45.1 us (32%)
  waiting for transfers between devices  40.1 us (29%)
  local copies, waits for them, and re-layouts  3.99 us (3%)
    ppermute x23, starting transfers between devices, send(): return lax.ppermute(x, AXES, perm)  48.9 us
    pallas_call x10, Pallas kernels, local_call(): pl.pallas_call(functools.partial(here_body, body), in_specs=[VMEM] * len(...  40.2 us
    ppermute x23, waiting for transfers between devices, send(): return lax.ppermute(x, AXES, perm)  40.1 us
    unnamed x16, local copies, waits for them, and re-layouts  3.98 us
  transfers between devices with their start and end apart: 23, of which 13 were waited for; matrix products, arithmetic and copies ran while one was open for 0% of the time, Pallas kernels for 31%

profile of v6, /device:TPU:3, one launch (start us, length us, event | category | flops | bytes accessed | tf_op | source)
XLA Modules:
  0.0 138.5 jit_solution(4437532499482918271)
XLA Ops:
  0.0 3.7 %copy-done = bf16[1536,3072]{1,0:T(8,128)(2,1)S(1)} copy-done((bf16[1536,3072]{1,0:T(8,128)(2,1)S(1)}, bf16[1536,3072]{1,0:T(8,128)(2,1)}, u32[]{:S(2)}) %copy-start) | copy-done | bytes 9437208
  3.7 0.3 shard_map.64
  4.0 0.0 copy-start.3
  4.0 0.8 collective-permute-start.22
  4.8 0.0 copy-done.1
  4.8 0.2 copy-done.2
  5.1 0.3 shard_map.55
  5.4 3.8 %collective-permute-start = (bf16[3,2,256,128]{3,2,1,0:T(8,128)(2,1)S(1)}, bf16[3,2,256,128]{3,2,1,0:T(8,128)(2,1)S(1)}, u32[]{:S(2)}, u32[]{:S(2)}) collective-permute-start(bf16[3,2,256,128]{3,2,1,0:T(8,128)(2,1)S(1)} %get-tuple-element.29), channel_id=1, source_target_pairs={{0,0},{1,1},{2,2},{3,3},{4,4},{5,5},{6,6},{7,7},{8,8},{9,9},{10,10... | collective-permute-start | bytes 1179656 | tf_op jit(solution)/shard_map/ppermute | solution.py:69
  9.1 1.4 %collective-permute-start.1 = (bf16[3,2,256,128]{3,2,1,0:T(8,128)(2,1)S(1)}, bf16[3,2,256,128]{3,2,1,0:T(8,128)(2,1)S(1)}, u32[]{:S(2)}, u32[]{:S(2)}) collective-permute-start(bf16[3,2,256,128]{3,2,1,0:T(8,128)(2,1)S(1)} %get-tuple-element.30), channel_id=1, source_target_pairs={{0,8},{1,9},{2,10},{3,11},{4,12},{5,13},{6,14},{7,15},{8,1},{9,0},... | collective-permute-start | bytes 1179656 | tf_op jit(solution)/shard_map/ppermute | solution.py:69
  10.6 4.8 %collective-permute-start.2 = (bf16[3,2,256,128]{3,2,1,0:T(8,128)(2,1)S(1)}, bf16[3,2,256,128]{3,2,1,0:T(8,128)(2,1)S(1)}, u32[]{:S(2)}, u32[]{:S(2)}) collective-permute-start(bf16[3,2,256,128]{3,2,1,0:T(8,128)(2,1)S(1)} %get-tuple-element.31), channel_id=1, source_target_pairs={{0,1},{1,0},{2,3},{3,2},{4,5},{5,4},{6,7},{7,6},{8,9},{9,8},{10,11... | collective-permute-start | bytes 1179656 | tf_op jit(solution)/shard_map/ppermute | solution.py:69
  15.3 0.5 collective-permute-start.3
  15.8 0.0 collective-permute-done.refs_0_
  15.8 6.8 %collective-permute-done.1.refs_1_ = bf16[3,2,256,128]{3,2,1,0:T(8,128)(2,1)S(1)} collective-permute-done((bf16[3,2,256,128]{3,2,1,0:T(8,128)(2,1)S(1)}, bf16[3,2,256,128]{3,2,1,0:T(8,128)(2,1)S(1)}, u32[]{:S(2)}, u32[]{:S(2)}) %collective-permute-start.1) | collective-permute-done | bytes 393248 | tf_op jit(solution)/shard_map/ppermute | solution.py:69
  22.6 3.9 %collective-permute-done.2.refs_2_ = bf16[3,2,256,128]{3,2,1,0:T(8,128)(2,1)S(1)} collective-permute-done((bf16[3,2,256,128]{3,2,1,0:T(8,128)(2,1)S(1)}, bf16[3,2,256,128]{3,2,1,0:T(8,128)(2,1)S(1)}, u32[]{:S(2)}, u32[]{:S(2)}) %collective-permute-start.2) | collective-permute-done | bytes 393248 | tf_op jit(solution)/shard_map/ppermute | solution.py:69
  26.5 2.5 %collective-permute-done.3.refs_3_ = bf16[3,2,256,128]{3,2,1,0:T(8,128)(2,1)S(1)} collective-permute-done((bf16[3,2,256,128]{3,2,1,0:T(8,128)(2,1)S(1)}, bf16[3,2,256,128]{3,2,1,0:T(8,128)(2,1)S(1)}, u32[]{:S(2)}, u32[]{:S(2)}) %collective-permute-start.3) | collective-permute-done | bytes 393248 | tf_op jit(solution)/shard_map/ppermute | solution.py:69
  29.0 0.3 shard_map.56
  29.3 4.5 %collective-permute-start.4 = (bf16[3,2,2,256,128]{4,3,2,1,0:T(8,128)(2,1)S(1)}, bf16[3,2,2,256,128]{4,3,2,1,0:T(8,128)(2,1)S(1)}, u32[]{:S(2)}, u32[]{:S(2)}) collective-permute-start(bf16[3,2,2,256,128]{4,3,2,1,0:T(8,128)(2,1)S(1)} %get-tuple-element.33.refs_0_), channel_id=1, source_target_pairs={{64,112},{65,113},{66,114},{67,115},{68,116},{69,117},{70,118},{71... | collective-permute-start | bytes 2359304 | tf_op jit(solution)/shard_map/ppermute | solution.py:69
  33.8 0.1 collective-permute-start.8
  33.9 0.3 shard_map.57
  34.2 0.1 collective-permute-start.10
  34.3 4.4 %collective-permute-start.11 = (bf16[3,256,128]{2,1,0:T(8,128)(2,1)S(1)}, bf16[3,256,128]{2,1,0:T(8,128)(2,1)S(1)}, u32[]{:S(2)}, u32[]{:S(2)}) collective-permute-start(bf16[3,256,128]{2,1,0:T(8,128)(2,1)S(1)} %get-tuple-element.38), channel_id=1, source_target_pairs={{0,1},{1,0},{2,3},{3,2},{4,5},{5,4},{6,7},{7,6},{8,9},{9,8},{10,11... | collective-permute-start | bytes 589832 | tf_op jit(solution)/shard_map/ppermute | solution.py:69
  38.7 2.9 %collective-permute-done.10.refs_4_ = bf16[3,256,128]{2,1,0:T(8,128)(2,1)S(1)} collective-permute-done((bf16[3,256,128]{2,1,0:T(8,128)(2,1)S(1)}, bf16[3,256,128]{2,1,0:T(8,128)(2,1)S(1)}, u32[]{:S(2)}, u32[]{:S(2)}) %collective-permute-start.10) | collective-permute-done | bytes 196640 | tf_op jit(solution)/shard_map/ppermute | solution.py:69
  41.6 0.7 collective-permute-start.12
  42.2 2.0 %collective-permute-done.11.refs_5_ = bf16[3,256,128]{2,1,0:T(8,128)(2,1)S(1)} collective-permute-done((bf16[3,256,128]{2,1,0:T(8,128)(2,1)S(1)}, bf16[3,256,128]{2,1,0:T(8,128)(2,1)S(1)}, u32[]{:S(2)}, u32[]{:S(2)}) %collective-permute-start.11) | collective-permute-done | bytes 196640 | tf_op jit(solution)/shard_map/ppermute | solution.py:69
  44.3 3.2 %collective-permute-start.9 = (bf16[3,256,128]{2,1,0:T(8,128)(2,1)S(1)}, bf16[3,256,128]{2,1,0:T(8,128)(2,1)S(1)}, u32[]{:S(2)}, u32[]{:S(2)}) collective-permute-start(bf16[3,256,128]{2,1,0:T(8,128)(2,1)S(1)} %get-tuple-element.36), channel_id=1, source_target_pairs={{0,0},{1,1},{2,2},{3,3},{4,4},{5,5},{6,6},{7,7},{8,8},{9,9},{10,10... | collective-permute-start | bytes 589832 | tf_op jit(solution)/shard_map/ppermute | solution.py:69
  47.5 0.3 collective-permute-done.12.refs_6_
  47.9 0.3 collective-permute-start.13
  48.1 3.1 %collective-permute-done.9.refs_3_ = bf16[3,256,128]{2,1,0:T(8,128)(2,1)S(1)} collective-permute-done((bf16[3,256,128]{2,1,0:T(8,128)(2,1)S(1)}, bf16[3,256,128]{2,1,0:T(8,128)(2,1)S(1)}, u32[]{:S(2)}, u32[]{:S(2)}) %collective-permute-start.9) | collective-permute-done | bytes 196640 | tf_op jit(solution)/shard_map/ppermute | solution.py:69
  51.2 3.1 %collective-permute-start.15 = (bf16[3,2,2,256,128]{4,3,2,1,0:T(8,128)(2,1)S(1)}, bf16[3,2,2,256,128]{4,3,2,1,0:T(8,128)(2,1)S(1)}, u32[]{:S(2)}, u32[]{:S(2)}) collective-permute-start(bf16[3,2,2,256,128]{4,3,2,1,0:T(8,128)(2,1)S(1)} %get-tuple-element.34.refs_1_), channel_id=1, source_target_pairs={{2,4},{3,5},{4,2},{5,3},{10,12},{11,13},{12,10},{13,11},{18,20},{1... | collective-permute-start | bytes 2359304 | tf_op jit(solution)/shard_map/ppermute | solution.py:69
  54.4 0.0 collective-permute-done.4.refs_0_
  54.4 2.3 %collective-permute-start.6 = (bf16[3,2,2,256,128]{4,3,2,1,0:T(8,128)(2,1)S(1)}, bf16[3,2,2,256,128]{4,3,2,1,0:T(8,128)(2,1)S(1)}, u32[]{:S(2)}, u32[]{:S(2)}) collective-permute-start(bf16[3,2,2,256,128]{4,3,2,1,0:T(8,128)(2,1)S(1)} %get-tuple-element.34.refs_1_), channel_id=1, source_target_pairs={{64,112},{65,113},{66,114},{67,115},{68,116},{69,117},{70,118},{71... | collective-permute-start | bytes 2359304 | tf_op jit(solution)/shard_map/ppermute | solution.py:69
  56.7 6.7 %collective-permute-done.13.refs_0_ = bf16[3,2,2,256,128]{4,3,2,1,0:T(8,128)(2,1)S(1)} collective-permute-done((bf16[3,2,2,256,128]{4,3,2,1,0:T(8,128)(2,1)S(1)}, bf16[3,2,2,256,128]{4,3,2,1,0:T(8,128)(2,1)S(1)}, u32[]{:S(2)}, u32[]{:S(2)}) %collective-permute-start.13) | collective-permute-done | bytes 786464 | tf_op jit(solution)/shard_map/ppermute | solution.py:69
  63.3 4.5 %collective-permute-start.14 = (bf16[3,2,2,256,128]{4,3,2,1,0:T(8,128)(2,1)S(1)}, bf16[3,2,2,256,128]{4,3,2,1,0:T(8,128)(2,1)S(1)}, u32[]{:S(2)}, u32[]{:S(2)}) collective-permute-start(bf16[3,2,2,256,128]{4,3,2,1,0:T(8,128)(2,1)S(1)} %collective-permute-done.13.refs_0_), channel_id=1, source_target_pairs={{0,64},{1,65},{2,66},{3,67},{4,68},{5,69},{6,70},{7,71},{8,72},{9,... | collective-permute-start | bytes 2359304 | tf_op jit(solution)/shard_map/ppermute | solution.py:69
  67.8 3.5 %collective-permute-done.15.refs_1_ = bf16[3,2,2,256,128]{4,3,2,1,0:T(8,128)(2,1)S(1)} collective-permute-done((bf16[3,2,2,256,128]{4,3,2,1,0:T(8,128)(2,1)S(1)}, bf16[3,2,2,256,128]{4,3,2,1,0:T(8,128)(2,1)S(1)}, u32[]{:S(2)}, u32[]{:S(2)}) %collective-permute-start.15) | collective-permute-done | bytes 786464 | tf_op jit(solution)/shard_map/ppermute | solution.py:69
  71.3 1.8 %collective-permute-start.16 = (bf16[3,2,2,256,128]{4,3,2,1,0:T(8,128)(2,1)S(1)}, bf16[3,2,2,256,128]{4,3,2,1,0:T(8,128)(2,1)S(1)}, u32[]{:S(2)}, u32[]{:S(2)}) collective-permute-start(bf16[3,2,2,256,128]{4,3,2,1,0:T(8,128)(2,1)S(1)} %collective-permute-done.15.refs_1_), channel_id=1, source_target_pairs={{0,64},{1,65},{2,66},{3,67},{4,68},{5,69},{6,70},{7,71},{8,72},{9,... | collective-permute-start | bytes 2359304 | tf_op jit(solution)/shard_map/ppermute | solution.py:69
  73.1 0.0 collective-permute-done.6.refs_1_
  73.1 1.9 %collective-permute-start.5 = (bf16[3,2,2,256,128]{4,3,2,1,0:T(8,128)(2,1)S(1)}, bf16[3,2,2,256,128]{4,3,2,1,0:T(8,128)(2,1)S(1)}, u32[]{:S(2)}, u32[]{:S(2)}) collective-permute-start(bf16[3,2,2,256,128]{4,3,2,1,0:T(8,128)(2,1)S(1)} %collective-permute-done.4.refs_0_), channel_id=1, source_target_pairs={{64,66},{65,67},{66,64},{67,65},{68,70},{69,71},{70,68},{71,69},{7... | collective-permute-start | bytes 2359304 | tf_op jit(solution)/shard_map/ppermute | solution.py:69
  75.0 0.0 collective-permute-done.8.refs_2_
  75.0 3.1 %collective-permute-start.7 = (bf16[3,2,2,256,128]{4,3,2,1,0:T(8,128)(2,1)S(1)}, bf16[3,2,2,256,128]{4,3,2,1,0:T(8,128)(2,1)S(1)}, u32[]{:S(2)}, u32[]{:S(2)}) collective-permute-start(bf16[3,2,2,256,128]{4,3,2,1,0:T(8,128)(2,1)S(1)} %collective-permute-done.6.refs_1_), channel_id=1, source_target_pairs={{66,68},{67,69},{68,66},{69,67},{74,76},{75,77},{76,74},{77,75},{8... | collective-permute-start | bytes 2359304 | tf_op jit(solution)/shard_map/ppermute | solution.py:69
  78.1 29.9 %shard_map.58 = (bf16[3,4,256,256]{3,2,1,0:T(8,128)(2,1)S(1)}, f32[3,2,144,512]{3,2,1,0:T(8,128)S(1)}, f32[3,2,1,512]{3,2,1,0:T(1,128)S(1)}) custom-call(bf16[3,2,2,256,128]{4,3,2,1,0:T(8,128)(2,1)S(1)} %get-tuple-element.33.refs_0_, bf16[3,2,2,256,128]{4,3,2,1,0:T(8,128)(2,1)S(1)} %get-tuple-element.34.refs_1_, ...), custom_call_target="tpu_custom_call" | custom-call | flops 4831838208 | bytes 7286784 | tf_op jit(solution)/shard_map/pallas_call | solution.py:114
  108.0 0.0 slice-start
  108.0 0.0 slice-start.1
  108.0 3.0 %shard_map.59 = (f32[3,2,144,512]{3,2,1,0:T(8,128)S(1)}, f32[3,2,1,512]{3,2,1,0:T(1,128)S(1)}) custom-call(bf16[3,2,2,256,128]{4,3,2,1,0:T(8,128)(2,1)S(1)} %collective-permute-done.4.refs_0_, bf16[3,2,2,256,128]{4,3,2,1,0:T(8,128)(2,1)S(1)} %collective-permute-done.6.refs_1_, ...), custom_call_target="tpu_custom_call", output_to_operand_aliasing={{1}: (4, {})} | custom-call | flops 2415919104 | bytes 6709248 | tf_op jit(solution)/shard_map/pallas_call | solution.py:114
  111.0 2.3 %shard_map.60 = (f32[3,2,144,512]{3,2,1,0:T(8,128)S(1)}, f32[3,2,1,512]{3,2,1,0:T(1,128)S(1)}) custom-call(bf16[3,2,2,256,128]{4,3,2,1,0:T(8,128)(2,1)S(1)} %collective-permute-done.13.refs_0_, bf16[3,2,2,256,128]{4,3,2,1,0:T(8,128)(2,1)S(1)} %collective-permute-done.15.refs_1_, ...), custom_call_target="tpu_custom_call", output_to_operand_aliasing={{1}: (4, {})} | custom-call | flops 1207959552 | bytes 6709248 | tf_op jit(solution)/shard_map/pallas_call | solution.py:114
  113.4 0.0 collective-permute-done.14.refs_0_
  113.4 0.0 collective-permute-done.16.refs_1_
  113.4 0.0 slice-start.2
  113.4 2.3 %shard_map.61 = (f32[3,2,144,512]{3,2,1,0:T(8,128)S(1)}, f32[3,2,1,512]{3,2,1,0:T(1,128)S(1)}) custom-call(bf16[3,2,2,256,128]{4,3,2,1,0:T(8,128)(2,1)S(1)} %collective-permute-done.14.refs_0_, bf16[3,2,2,256,128]{4,3,2,1,0:T(8,128)(2,1)S(1)} %collective-permute-done.16.refs_1_, ...), custom_call_target="tpu_custom_call", output_to_operand_aliasing={{1}: (4, {})} | custom-call | flops 1207959552 | bytes 6709248 | tf_op jit(solution)/shard_map/pallas_call | solution.py:114
  115.7 0.0 collective-permute-done.5.refs_0_
  115.7 0.0 copy-start.4
  115.8 2.7 %last.1 = (bf16[256,384]{1,0:T(8,128)(2,1)S(1)}, bf16[256,384]{1,0:T(8,128)(2,1)S(1)}, bf16[256,384]{1,0:T(8,128)(2,1)S(1)}, bf16[256,384]{1,0:T(8,128)(2,1)S(1)}, f32[3,2,1,512]{3,2,1,0:T(1,128)S(1)}) custom-call(bf16[3,2,2,256,128]{4,3,2,1,0:T(8,128)(2,1)S(1)} %collective-permute-done.5.refs_0_, ...), custom_call_target="tpu_custom_call", output_to_operand_aliasing={{4}: (4, {})} | custom-call | flops 1207959552 | bytes 1048576 | tf_op jit(solution)/shard_map/last/pallas_call | solution.py:339
  118.5 1.9 %collective-permute-start.17 = (bf16[256,384]{1,0:T(8,128)(2,1)S(1)}, bf16[256,384]{1,0:T(8,128)(2,1)S(1)}, u32[]{:S(2)}, u32[]{:S(2)}) collective-permute-start(bf16[256,384]{1,0:T(8,128)(2,1)S(1)} %get-tuple-element.49), channel_id=1, source_target_pairs={{0,0},{1,1},{2,2},{3,3},{4,4},{5,5},{6,6},{7,7},{8,8},{9,9},{10,10... | collective-permute-start | bytes 589832 | tf_op jit(solution)/shard_map/ppermute | solution.py:69
  120.4 3.5 %collective-permute-start.18 = (bf16[256,384]{1,0:T(8,128)(2,1)S(1)}, bf16[256,384]{1,0:T(8,128)(2,1)S(1)}, u32[]{:S(2)}, u32[]{:S(2)}) collective-permute-start(bf16[256,384]{1,0:T(8,128)(2,1)S(1)} %get-tuple-element.50), channel_id=1, source_target_pairs={{0,9},{1,8},{2,11},{3,10},{4,13},{5,12},{6,15},{7,14},{8,0},{9,1},... | collective-permute-start | bytes 589832 | tf_op jit(solution)/shard_map/ppermute | solution.py:69
  123.9 0.3 collective-permute-start.19
  124.2 1.9 %collective-permute-start.20 = (bf16[256,384]{1,0:T(8,128)(2,1)S(1)}, bf16[256,384]{1,0:T(8,128)(2,1)S(1)}, u32[]{:S(2)}, u32[]{:S(2)}) collective-permute-start(bf16[256,384]{1,0:T(8,128)(2,1)S(1)} %get-tuple-element.52), channel_id=1, source_target_pairs={{0,8},{1,9},{2,10},{3,11},{4,12},{5,13},{6,14},{7,15},{8,1},{9,0},... | collective-permute-start | bytes 589832 | tf_op jit(solution)/shard_map/ppermute | solution.py:69
  126.2 0.0 collective-permute-done.17.refs_0_
  126.2 1.7 %collective-permute-done.18.refs_1_ = bf16[256,384]{1,0:T(8,128)(2,1)S(1)} collective-permute-done((bf16[256,384]{1,0:T(8,128)(2,1)S(1)}, bf16[256,384]{1,0:T(8,128)(2,1)S(1)}, u32[]{:S(2)}, u32[]{:S(2)}) %collective-permute-start.18) | collective-permute-done | bytes 196640 | tf_op jit(solution)/shard_map/ppermute | solution.py:69
  127.8 4.0 %collective-permute-done.19.refs_2_ = bf16[256,384]{1,0:T(8,128)(2,1)S(1)} collective-permute-done((bf16[256,384]{1,0:T(8,128)(2,1)S(1)}, bf16[256,384]{1,0:T(8,128)(2,1)S(1)}, u32[]{:S(2)}, u32[]{:S(2)}) %collective-permute-start.19) | collective-permute-done | bytes 196640 | tf_op jit(solution)/shard_map/ppermute | solution.py:69
  131.9 1.9 %collective-permute-done.20.refs_3_ = bf16[256,384]{1,0:T(8,128)(2,1)S(1)} collective-permute-done((bf16[256,384]{1,0:T(8,128)(2,1)S(1)}, bf16[256,384]{1,0:T(8,128)(2,1)S(1)}, u32[]{:S(2)}, u32[]{:S(2)}) %collective-permute-start.20) | collective-permute-done | bytes 196640 | tf_op jit(solution)/shard_map/ppermute | solution.py:69
  133.7 0.1 shard_map.62.refs_0_
  133.9 0.1 collective-permute-start.21
  134.0 1.4 %shard_map.63.here = f32[256,1536]{1,0:T(8,128)S(1)} custom-call(bf16[256,1536]{1,0:T(8,128)(2,1)S(1)} %shard_map.62.refs_0_, bf16[1536,3072]{1,0:T(8,128)(2,1)S(1)} %bitcast.5), custom_call_target="tpu_custom_call" | custom-call | flops 1207959552 | bytes 11796480 | tf_op jit(solution)/shard_map/pallas_call | solution.py:114
  135.4 0.8 collective-permute-done.21.joined
  136.2 2.1 %close.1 = bf16[256,1536]{1,0:T(8,128)(2,1)} custom-call(f32[256,1536]{1,0:T(8,128)S(1)} %shard_map.63.here, bf16[256,1536]{1,0:T(8,128)(2,1)S(1)} %collective-permute-done.21.joined, bf16[1536,1536]{1,0:T(8,128)(2,1)S(1)} %collective-permute-done.22.weight, bf16[1,1536]{1,0:T(2,128)(2,1)S(1)} %reshape.18.gate), custom_call_target="tpu_custom_call" | custom-call | flops 1207959552 | bytes 1048576 | tf_op jit(solution)/shard_map/close/pallas_call | solution.py:391
  (12 shorter events, 0.0 us)
Async XLA Ops:
  0.0 3.7 %copy-start = (bf16[1536,3072]{1,0:T(8,128)(2,1)S(1)}, bf16[1536,3072]{1,0:T(8,128)(2,1)}, u32[]{:S(2)}) copy-start(bf16[1536,3072]{1,0:T(8,128)(2,1)} %refs_0_.1) | copy-start | bytes 28311556
  3.7 1.1 copy-start.1
  3.7 1.4 copy-start.2
  4.0 29.9 %copy-start.3 = (bf16[1,1,1,256,1536]{4,3,2,1,0:T(8,128)(2,1)S(1)}, bf16[1,1,1,256,1536]{4,3,2,1,0:T(8,128)(2,1)}, u32[]{:S(2)}) copy-start(bf16[1,1,1,256,1536]{4,3,2,1,0:T(8,128)(2,1)} %param.5) | copy-start | bytes 2359300
  4.0 132.2 %collective-permute-start.22 = (bf16[1536,1536]{1,0:T(8,128)(2,1)S(1)}, bf16[1536,1536]{1,0:T(8,128)(2,1)S(1)}, u32[]{:S(2)}, u32[]{:S(2)}) collective-permute-start(bf16[1536,1536]{1,0:T(8,128)(2,1)S(1)} %shard_map.64), channel_id=1, source_target_pairs={{0,64},{1,65},{2,66},{3,67},{4,68},{5,69},{6,70},{7,71},{8,72},{9,... | collective-permute-start | bytes 14155784 | tf_op jit(solution)/shard_map/ppermute | solution.py:69
  5.4 10.4 %collective-permute-start = (bf16[3,2,256,128]{3,2,1,0:T(8,128)(2,1)S(1)}, bf16[3,2,256,128]{3,2,1,0:T(8,128)(2,1)S(1)}, u32[]{:S(2)}, u32[]{:S(2)}) collective-permute-start(bf16[3,2,256,128]{3,2,1,0:T(8,128)(2,1)S(1)} %get-tuple-element.29), channel_id=1, source_target_pairs={{0,0},{1,1},{2,2},{3,3},{4,4},{5,5},{6,6},{7,7},{8,8},{9,9},{10,10... | collective-permute-start | bytes 1179656 | tf_op jit(solution)/shard_map/ppermute | solution.py:69
  9.1 13.4 %collective-permute-start.1 = (bf16[3,2,256,128]{3,2,1,0:T(8,128)(2,1)S(1)}, bf16[3,2,256,128]{3,2,1,0:T(8,128)(2,1)S(1)}, u32[]{:S(2)}, u32[]{:S(2)}) collective-permute-start(bf16[3,2,256,128]{3,2,1,0:T(8,128)(2,1)S(1)} %get-tuple-element.30), channel_id=1, source_target_pairs={{0,8},{1,9},{2,10},{3,11},{4,12},{5,13},{6,14},{7,15},{8,1},{9,0},... | collective-permute-start | bytes 1179656 | tf_op jit(solution)/shard_map/ppermute | solution.py:69
  10.6 15.9 %collective-permute-start.2 = (bf16[3,2,256,128]{3,2,1,0:T(8,128)(2,1)S(1)}, bf16[3,2,256,128]{3,2,1,0:T(8,128)(2,1)S(1)}, u32[]{:S(2)}, u32[]{:S(2)}) collective-permute-start(bf16[3,2,256,128]{3,2,1,0:T(8,128)(2,1)S(1)} %get-tuple-element.31), channel_id=1, source_target_pairs={{0,1},{1,0},{2,3},{3,2},{4,5},{5,4},{6,7},{7,6},{8,9},{9,8},{10,11... | collective-permute-start | bytes 1179656 | tf_op jit(solution)/shard_map/ppermute | solution.py:69
  15.3 13.7 %collective-permute-start.3 = (bf16[3,2,256,128]{3,2,1,0:T(8,128)(2,1)S(1)}, bf16[3,2,256,128]{3,2,1,0:T(8,128)(2,1)S(1)}, u32[]{:S(2)}, u32[]{:S(2)}) collective-permute-start(bf16[3,2,256,128]{3,2,1,0:T(8,128)(2,1)S(1)} %get-tuple-element.32), channel_id=1, source_target_pairs={{0,9},{1,8},{2,11},{3,10},{4,13},{5,12},{6,15},{7,14},{8,0},{9,1},... | collective-permute-start | bytes 1179656 | tf_op jit(solution)/shard_map/ppermute | solution.py:69
  29.3 25.1 %collective-permute-start.4 = (bf16[3,2,2,256,128]{4,3,2,1,0:T(8,128)(2,1)S(1)}, bf16[3,2,2,256,128]{4,3,2,1,0:T(8,128)(2,1)S(1)}, u32[]{:S(2)}, u32[]{:S(2)}) collective-permute-start(bf16[3,2,2,256,128]{4,3,2,1,0:T(8,128)(2,1)S(1)} %get-tuple-element.33.refs_0_), channel_id=1, source_target_pairs={{64,112},{65,113},{66,114},{67,115},{68,116},{69,117},{70,118},{71... | collective-permute-start | bytes 2359304 | tf_op jit(solution)/shard_map/ppermute | solution.py:69
  33.8 41.2 %collective-permute-start.8 = (bf16[2,3,2,2,256,128]{5,4,3,2,1,0:T(8,128)(2,1)S(1)}, bf16[2,3,2,2,256,128]{5,4,3,2,1,0:T(8,128)(2,1)S(1)}, u32[]{:S(2)}, u32[]{:S(2)}) collective-permute-start(bf16[2,3,2,2,256,128]{5,4,3,2,1,0:T(8,128)(2,1)S(1)} %get-tuple-element.35), channel_id=1, source_target_pairs={{0,64},{1,65},{2,66},{3,67},{4,68},{5,69},{6,70},{7,71},{8,72},{9,... | collective-permute-start | bytes 4718600 | tf_op jit(solution)/shard_map/ppermute | solution.py:69
  34.2 7.4 %collective-permute-start.10 = (bf16[3,256,128]{2,1,0:T(8,128)(2,1)S(1)}, bf16[3,256,128]{2,1,0:T(8,128)(2,1)S(1)}, u32[]{:S(2)}, u32[]{:S(2)}) collective-permute-start(bf16[3,256,128]{2,1,0:T(8,128)(2,1)S(1)} %get-tuple-element.37), channel_id=1, source_target_pairs={{0,8},{1,9},{2,10},{3,11},{4,12},{5,13},{6,14},{7,15},{8,1},{9,0},... | collective-permute-start | bytes 589832 | tf_op jit(solution)/shard_map/ppermute | solution.py:69
  34.3 10.0 %collective-permute-start.11 = (bf16[3,256,128]{2,1,0:T(8,128)(2,1)S(1)}, bf16[3,256,128]{2,1,0:T(8,128)(2,1)S(1)}, u32[]{:S(2)}, u32[]{:S(2)}) collective-permute-start(bf16[3,256,128]{2,1,0:T(8,128)(2,1)S(1)} %get-tuple-element.38), channel_id=1, source_target_pairs={{0,1},{1,0},{2,3},{3,2},{4,5},{5,4},{6,7},{7,6},{8,9},{9,8},{10,11... | collective-permute-start | bytes 589832 | tf_op jit(solution)/shard_map/ppermute | solution.py:69
  41.6 6.3 %collective-permute-start.12 = (bf16[3,256,128]{2,1,0:T(8,128)(2,1)S(1)}, bf16[3,256,128]{2,1,0:T(8,128)(2,1)S(1)}, u32[]{:S(2)}, u32[]{:S(2)}) collective-permute-start(bf16[3,256,128]{2,1,0:T(8,128)(2,1)S(1)} %get-tuple-element.39), channel_id=1, source_target_pairs={{0,9},{1,8},{2,11},{3,10},{4,13},{5,12},{6,15},{7,14},{8,0},{9,1},... | collective-permute-start | bytes 589832 | tf_op jit(solution)/shard_map/ppermute | solution.py:69
  44.3 7.0 %collective-permute-start.9 = (bf16[3,256,128]{2,1,0:T(8,128)(2,1)S(1)}, bf16[3,256,128]{2,1,0:T(8,128)(2,1)S(1)}, u32[]{:S(2)}, u32[]{:S(2)}) collective-permute-start(bf16[3,256,128]{2,1,0:T(8,128)(2,1)S(1)} %get-tuple-element.36), channel_id=1, source_target_pairs={{0,0},{1,1},{2,2},{3,3},{4,4},{5,5},{6,6},{7,7},{8,8},{9,9},{10,10... | collective-permute-start | bytes 589832 | tf_op jit(solution)/shard_map/ppermute | solution.py:69
  47.9 15.5 %collective-permute-start.13 = (bf16[3,2,2,256,128]{4,3,2,1,0:T(8,128)(2,1)S(1)}, bf16[3,2,2,256,128]{4,3,2,1,0:T(8,128)(2,1)S(1)}, u32[]{:S(2)}, u32[]{:S(2)}) collective-permute-start(bf16[3,2,2,256,128]{4,3,2,1,0:T(8,128)(2,1)S(1)} %get-tuple-element.33.refs_0_), channel_id=1, source_target_pairs={{0,2},{1,3},{2,0},{3,1},{4,6},{5,7},{6,4},{7,5},{8,10},{9,11},{10,... | collective-permute-start | bytes 2359304 | tf_op jit(solution)/shard_map/ppermute | solution.py:69
  51.2 20.1 %collective-permute-start.15 = (bf16[3,2,2,256,128]{4,3,2,1,0:T(8,128)(2,1)S(1)}, bf16[3,2,2,256,128]{4,3,2,1,0:T(8,128)(2,1)S(1)}, u32[]{:S(2)}, u32[]{:S(2)}) collective-permute-start(bf16[3,2,2,256,128]{4,3,2,1,0:T(8,128)(2,1)S(1)} %get-tuple-element.34.refs_1_), channel_id=1, source_target_pairs={{2,4},{3,5},{4,2},{5,3},{10,12},{11,13},{12,10},{13,11},{18,20},{1... | collective-permute-start | bytes 2359304 | tf_op jit(solution)/shard_map/ppermute | solution.py:69
  54.4 18.7 %collective-permute-start.6 = (bf16[3,2,2,256,128]{4,3,2,1,0:T(8,128)(2,1)S(1)}, bf16[3,2,2,256,128]{4,3,2,1,0:T(8,128)(2,1)S(1)}, u32[]{:S(2)}, u32[]{:S(2)}) collective-permute-start(bf16[3,2,2,256,128]{4,3,2,1,0:T(8,128)(2,1)S(1)} %get-tuple-element.34.refs_1_), channel_id=1, source_target_pairs={{64,112},{65,113},{66,114},{67,115},{68,116},{69,117},{70,118},{71... | collective-permute-start | bytes 2359304 | tf_op jit(solution)/shard_map/ppermute | solution.py:69
  63.3 50.0 %collective-permute-start.14 = (bf16[3,2,2,256,128]{4,3,2,1,0:T(8,128)(2,1)S(1)}, bf16[3,2,2,256,128]{4,3,2,1,0:T(8,128)(2,1)S(1)}, u32[]{:S(2)}, u32[]{:S(2)}) collective-permute-start(bf16[3,2,2,256,128]{4,3,2,1,0:T(8,128)(2,1)S(1)} %collective-permute-done.13.refs_0_), channel_id=1, source_target_pairs={{0,64},{1,65},{2,66},{3,67},{4,68},{5,69},{6,70},{7,71},{8,72},{9,... | collective-permute-start | bytes 2359304 | tf_op jit(solution)/shard_map/ppermute | solution.py:69
  71.3 42.1 %collective-permute-start.16 = (bf16[3,2,2,256,128]{4,3,2,1,0:T(8,128)(2,1)S(1)}, bf16[3,2,2,256,128]{4,3,2,1,0:T(8,128)(2,1)S(1)}, u32[]{:S(2)}, u32[]{:S(2)}) collective-permute-start(bf16[3,2,2,256,128]{4,3,2,1,0:T(8,128)(2,1)S(1)} %collective-permute-done.15.refs_1_), channel_id=1, source_target_pairs={{0,64},{1,65},{2,66},{3,67},{4,68},{5,69},{6,70},{7,71},{8,72},{9,... | collective-permute-start | bytes 2359304 | tf_op jit(solution)/shard_map/ppermute | solution.py:69
  73.1 42.6 %collective-permute-start.5 = (bf16[3,2,2,256,128]{4,3,2,1,0:T(8,128)(2,1)S(1)}, bf16[3,2,2,256,128]{4,3,2,1,0:T(8,128)(2,1)S(1)}, u32[]{:S(2)}, u32[]{:S(2)}) collective-permute-start(bf16[3,2,2,256,128]{4,3,2,1,0:T(8,128)(2,1)S(1)} %collective-permute-done.4.refs_0_), channel_id=1, source_target_pairs={{64,66},{65,67},{66,64},{67,65},{68,70},{69,71},{70,68},{71,69},{7... | collective-permute-start | bytes 2359304 | tf_op jit(solution)/shard_map/ppermute | solution.py:69
  75.0 40.7 %collective-permute-start.7 = (bf16[3,2,2,256,128]{4,3,2,1,0:T(8,128)(2,1)S(1)}, bf16[3,2,2,256,128]{4,3,2,1,0:T(8,128)(2,1)S(1)}, u32[]{:S(2)}, u32[]{:S(2)}) collective-permute-start(bf16[3,2,2,256,128]{4,3,2,1,0:T(8,128)(2,1)S(1)} %collective-permute-done.6.refs_1_), channel_id=1, source_target_pairs={{66,68},{67,69},{68,66},{69,67},{74,76},{75,77},{76,74},{77,75},{8... | collective-permute-start | bytes 2359304 | tf_op jit(solution)/shard_map/ppermute | solution.py:69
  108.0 26.0 %slice-start = ((s8[9437184]{0:T(1024)(128)(4,1)}), s8[4194304]{0:T(1024)(128)(4,1)S(1)}, s32[]{:S(2)}) async-start(s8[9437184]{0:T(1024)(128)(4,1)} %bitcast.4), calls=%async_computation | async-start | bytes 8388608
  108.0 26.0 %slice-start.1 = ((s8[9437184]{0:T(1024)(128)(4,1)}), s8[4194304]{0:T(1024)(128)(4,1)S(1)}, s32[]{:S(2)}) async-start(s8[9437184]{0:T(1024)(128)(4,1)} %bitcast.4), calls=%async_computation.1 | async-start | bytes 8388608
  113.4 20.6 %slice-start.2 = ((s8[9437184]{0:T(1024)(128)(4,1)}), s8[1048576]{0:T(1024)(128)(4,1)S(1)}, s32[]{:S(2)}) async-start(s8[9437184]{0:T(1024)(128)(4,1)} %bitcast.4), calls=%async_computation.2 | async-start | bytes 2097152
  115.7 18.2 %copy-start.4 = (bf16[1536]{0:T(1024)(128)(2,1)S(1)}, bf16[1536]{0:T(1024)(128)(2,1)}, u32[]{:S(2)}) copy-start(bf16[1536]{0:T(1024)(128)(2,1)} %param.9) | copy-start | bytes 9220
  118.5 7.7 %collective-permute-start.17 = (bf16[256,384]{1,0:T(8,128)(2,1)S(1)}, bf16[256,384]{1,0:T(8,128)(2,1)S(1)}, u32[]{:S(2)}, u32[]{:S(2)}) collective-permute-start(bf16[256,384]{1,0:T(8,128)(2,1)S(1)} %get-tuple-element.49), channel_id=1, source_target_pairs={{0,0},{1,1},{2,2},{3,3},{4,4},{5,5},{6,6},{7,7},{8,8},{9,9},{10,10... | collective-permute-start | bytes 589832 | tf_op jit(solution)/shard_map/ppermute | solution.py:69
  120.4 7.4 %collective-permute-start.18 = (bf16[256,384]{1,0:T(8,128)(2,1)S(1)}, bf16[256,384]{1,0:T(8,128)(2,1)S(1)}, u32[]{:S(2)}, u32[]{:S(2)}) collective-permute-start(bf16[256,384]{1,0:T(8,128)(2,1)S(1)} %get-tuple-element.50), channel_id=1, source_target_pairs={{0,9},{1,8},{2,11},{3,10},{4,13},{5,12},{6,15},{7,14},{8,0},{9,1},... | collective-permute-start | bytes 589832 | tf_op jit(solution)/shard_map/ppermute | solution.py:69
  123.9 8.0 %collective-permute-start.19 = (bf16[256,384]{1,0:T(8,128)(2,1)S(1)}, bf16[256,384]{1,0:T(8,128)(2,1)S(1)}, u32[]{:S(2)}, u32[]{:S(2)}) collective-permute-start(bf16[256,384]{1,0:T(8,128)(2,1)S(1)} %get-tuple-element.51), channel_id=1, source_target_pairs={{0,1},{1,0},{2,3},{3,2},{4,5},{5,4},{6,7},{7,6},{8,9},{9,8},{10,11... | collective-permute-start | bytes 589832 | tf_op jit(solution)/shard_map/ppermute | solution.py:69
  124.2 9.5 %collective-permute-start.20 = (bf16[256,384]{1,0:T(8,128)(2,1)S(1)}, bf16[256,384]{1,0:T(8,128)(2,1)S(1)}, u32[]{:S(2)}, u32[]{:S(2)}) collective-permute-start(bf16[256,384]{1,0:T(8,128)(2,1)S(1)} %get-tuple-element.52), channel_id=1, source_target_pairs={{0,8},{1,9},{2,10},{3,11},{4,12},{5,13},{6,14},{7,15},{8,1},{9,0},... | collective-permute-start | bytes 589832 | tf_op jit(solution)/shard_map/ppermute | solution.py:69
  133.9 2.4 %collective-permute-start.21 = (bf16[256,1536]{1,0:T(8,128)(2,1)S(1)}, bf16[256,1536]{1,0:T(8,128)(2,1)S(1)}, u32[]{:S(2)}, u32[]{:S(2)}) collective-permute-start(bf16[256,1536]{1,0:T(8,128)(2,1)S(1)} %shard_map.62.refs_0_), channel_id=1, source_target_pairs={{0,64},{1,65},{2,66},{3,67},{4,68},{5,69},{6,70},{7,71},{8,72},{9,... | collective-permute-start | bytes 2359304 | tf_op jit(solution)/shard_map/ppermute | solution.py:69
